TPU v7x, 256 devices: a 8x8x2 block of a 8x8x16 slice. The times are simulated.
256 devices in a mesh: shots: 2 (over z), mx: 128 (over x, y, core).
Axes of the slice: x: 8, y: 8, z: 2, core: 2. Of those that a mesh axis runs over, the one named last changes fastest.
The devices are a block of a 8x8x16 slice.
Arguments:
- initial: float32 [18, 125, 16384], P('shots', None, 'mx'), parts along dimension 0, may hold values from -6 to 6
- derivative: float32 [3, 125, 125], replicated, may hold values from -0.5 to 0.5
- coupling: float32 [3, 9, 9], replicated, may hold values from -2 to 2
- face_lift: float32 [2, 125, 125], replicated, may hold values from -0.5 to 0.5
- metric: float32 [3, 16384], P(None, 'mx'), may hold values from 0.3 to 3
- rec_element: int32 [32768], P('mx'), may hold values from 0 to 127
- rec_weight: float32 [125, 32768], P(None, 'mx'), may hold values from -0.5 to 0.5
- live_counts: int32 [128], replicated, may hold values from 1 to 256, 16384 in all
- shot_order: int32 [32768], replicated, may hold values from 0 to 32767, as said below
- observed: float32 [65536, 48], P(('shots', 'mx')), parts along dimension 0, may hold values from -6 to 6
Outputs:
- residual: float32 [65536, 48], P(('shots', 'mx')), parts along dimension 0
- misfit: float32 [65536], P(('shots', 'mx')), parts along dimension 0
- adjoint: float32 [65536, 48], P(('shots', 'mx')), parts along dimension 0
There are 2 independent parts, one for each index of `shots`. A program takes and returns all parts, laid end to end along the dimension named above; an argument that names none is the same for every part. Nothing has to cross between parts.
Inputs may be any that keep to these rules, and one draw needn't show every extreme that they name: `rec_element`: local element index of the slot within its block of 128 elements. The live receivers of block b are its first live_counts[b] slots. `shot_order`: a permutation of the slots; of the 256 positions of each block of shot-receiver order, exactly 2 come from the slots of each block.
All inputs are finite; a program needn't handle non-finite values.
Results may differ from a plain program's by a relative error of at most 0.00018.
Values sent between devices are 32-bit elements; how exact they have to be, the bound alone decides.
No kernel may reach another device: no remote copies, remote signals or barrier semaphores. Data moves between devices by JAX's collectives and lax.ppermute only.
A program may use at most 64 MiB of HBM per device.

v0:
```python
import jax
import jax.numpy as jnp
from jax import lax
from jax.sharding import Mesh
from jax.sharding import PartitionSpec as P

STEPS = 12
DEPTH = 4
MX = ("mx_0", "mx_1", "mx_2")
SHOTS_MX = ("shots", "mx_0", "mx_1", "mx_2")


HIGH = lax.Precision.HIGHEST


def split_up(shard, dim, count):
    before, after = (shard.shape[:dim], shard.shape[dim + 1 :])
    return jnp.moveaxis(shard.reshape(*before, count, -1, *after), dim, 0)


def joined_along(blocks, dim):
    blocks = jnp.moveaxis(blocks, 0, dim)
    dims = blocks.shape
    return blocks.reshape(*dims[:dim], dims[dim] * dims[dim + 1], *dims[dim + 2 :])


def turned_blocks(blocks, axes, turns):
    inside = blocks.shape[1:]
    out = blocks.reshape(*(lax.axis_size(a) for a in axes), *inside)
    for k in turns:
        out = lax.all_to_all(out, axes[k], k, k, tiled=True)
    return out.reshape(-1, *inside)


def core_and_chips(shard, groups, turns, split_dim, concat_dim):
    count = lax.axis_size(groups[0]) * lax.axis_size(groups[1])
    blocks = split_up(shard, split_dim, count)
    return joined_along(turned_blocks(blocks, groups, turns), concat_dim)


def with_halo(block, sides, width):
    for axis, dim in sides:
        count = lax.axis_size(axis)
        forward = [(i, i + 1) for i in range(count - 1)]
        backward = [(target, source) for source, target in forward]
        low = lax.ppermute(
            lax.slice_in_dim(block, block.shape[dim] - width, None, axis=dim), axis, forward
        )
        high = lax.ppermute(lax.slice_in_dim(block, 0, width, axis=dim), axis, backward)
        block = jnp.concatenate([low, block, high], axis=dim)
    return block


def advance(extended, metric_cols, derivative, coupling, face_lift, time_step):
    middle = extended[:, :, 1:-1]
    summed = jnp.einsum("pq,fqe->fpe", face_lift[0], extended[:, :, :-2] - middle, precision=HIGH)
    summed = summed + jnp.einsum(
        "pq,fqe->fpe", face_lift[1], extended[:, :, 2:] - middle, precision=HIGH
    )
    for k in range(3):
        gradient = jnp.einsum("pq,fqe->fpe", derivative[k], middle, precision=HIGH)
        summed = (
            summed
            + jnp.einsum("gf,fpe->gpe", coupling[k], gradient, precision=HIGH)
            * metric_cols[k][None, None, :]
        )
    return middle + time_step * summed


def sample(wavefield, elements, rec_weight, live_slot):
    components = jnp.stack(
        [
            wavefield[0],
            wavefield[1],
            wavefield[2],
            (wavefield[3] + wavefield[4] + wavefield[5]) / 3.0,
        ]
    )
    columns = jnp.take(components, elements, axis=2)
    return jnp.sum(columns * rec_weight[None], axis=1) * live_slot[None]


def shards(
    initial,
    derivative,
    coupling,
    face_lift,
    metric,
    rec_element,
    rec_weight,
    live_counts,
    shot_order,
    observed,
):
    time_step = 0.5 / STEPS
    elem_count = initial.shape[2]
    slot_count = rec_element.shape[0]
    peer_count = lax.axis_size(MX)
    pair_rows = slot_count // peer_count
    my_index = lax.axis_index(MX)
    row_width = 4 * STEPS
    live_slot = (jnp.arange(slot_count, dtype=jnp.int32) < live_counts[my_index]).astype(
        jnp.float32
    )
    by_block = shot_order.reshape(peer_count, slot_count)
    source_blk = by_block // slot_count
    slot_of = by_block % slot_count
    mine = (source_blk == my_index).astype(jnp.int32)
    rank_in = jnp.cumsum(mine, axis=1) - 1
    rank_in = jnp.where(mine > 0, rank_in, pair_rows)
    dest_rows = jnp.broadcast_to(jnp.arange(peer_count, dtype=jnp.int32)[:, None], rank_in.shape)
    send_index = (
        jnp.zeros((peer_count, pair_rows), jnp.int32)
        .at[dest_rows, rank_in]
        .set(slot_of, mode="drop")
    )
    own_source = lax.dynamic_index_in_dim(source_blk, my_index, 0, keepdims=False)
    own_slot = lax.dynamic_index_in_dim(slot_of, my_index, 0, keepdims=False)
    onehot = (own_source[:, None] == jnp.arange(peer_count, dtype=jnp.int32)[None, :]).astype(
        jnp.int32
    )
    running = jnp.cumsum(onehot, axis=0)
    own_rank = jnp.take_along_axis(running, own_source[:, None], axis=1)[:, 0] - 1
    flat_pos = own_source * pair_rows + own_rank
    live_out = (own_slot < live_counts[own_source]).astype(jnp.float32)
    obs_buffer = (
        jnp.zeros((peer_count * pair_rows, row_width), jnp.float32).at[flat_pos].set(observed)
    )
    obs_back = core_and_chips(
        obs_buffer.reshape(peer_count, pair_rows, row_width),
        (("mx_0", "mx_1"), "mx_2"),
        (1, 0),
        0,
        0,
    )
    obs_slot = (
        jnp.zeros((slot_count, row_width), jnp.float32)
        .at[send_index.reshape(-1)]
        .set(obs_back.reshape(peer_count * pair_rows, row_width))
    )
    trace_buffer = jnp.zeros((4, STEPS, slot_count), jnp.float32)
    metric_wide = with_halo(metric, ((MX, 1),), DEPTH)
    full_width = elem_count + 2 * DEPTH
    first_cell = my_index * elem_count - DEPTH
    cell_ids = first_cell + jnp.arange(full_width, dtype=jnp.int32)
    inside_mask = ((cell_ids >= 0) & (cell_ids < elem_count * peer_count)).astype(jnp.float32)

    def block_step(b, carry):
        wavefield, record_buf = carry
        extended = with_halo(wavefield, ((MX, 2),), DEPTH)
        for s in range(DEPTH):
            rim_left = DEPTH - 1 - s
            stop_col = full_width - s - 1
            extended = advance(
                extended,
                metric_wide[:, s + 1 : stop_col],
                derivative,
                coupling,
                face_lift,
                time_step,
            )
            extended = extended * inside_mask[None, None, s + 1 : stop_col]
            current = extended[:, :, rim_left : rim_left + elem_count]
            sampled = sample(current, rec_element, rec_weight, live_slot)
            record_buf = lax.dynamic_update_slice(
                record_buf, sampled[:, None, :], (0, b * DEPTH + s, 0)
            )
        return (extended, record_buf)

    final_field, trace_buffer = lax.fori_loop(
        0, STEPS // DEPTH, block_step, (initial, trace_buffer)
    )
    synthetic = trace_buffer.transpose(2, 0, 1).reshape(slot_count, row_width)
    send_buffer = synthetic[send_index]
    received = lax.all_to_all(send_buffer, MX, split_axis=0, concat_axis=0, tiled=True)
    ordered = received.reshape(peer_count * pair_rows, row_width)[flat_pos]
    residual = live_out[:, None] * (ordered - observed)
    misfit = 0.5 * jnp.sum(residual * residual, axis=1)
    slot_resid = live_slot[:, None] * (synthetic - obs_slot)
    adjoint = slot_resid.reshape(slot_count, 4, STEPS)[:, :, ::-1].reshape(slot_count, row_width)
    return (residual, misfit, adjoint)


def solution(mesh):
    split = Mesh(
        mesh.devices.reshape(mesh.shape["shots"], 8, 8, 2), ("shots", "mx_0", "mx_1", "mx_2")
    )
    in_specs = (
        P("shots", None, MX),
        P(),
        P(),
        P(),
        P(None, MX),
        P(MX),
        P(None, MX),
        P(),
        P(),
        P(SHOTS_MX, None),
    )
    out_specs = (P(SHOTS_MX, None), P(SHOTS_MX), P(SHOTS_MX, None))
    return jax.shard_map(
        shards, mesh=split, in_specs=in_specs, out_specs=out_specs, check_vma=False
    )
```

profile of v0, /device:TPU:513, one launch (start us, length us, event | category | flops | bytes accessed | tf_op | source)
XLA Modules:
  0.0 445.5 jit_solution(4504976439680232341)
XLA Ops:
  1.5 5.7 %collective-permute-start.2 = (f32[3,4]{1,0:T(4,128)S(1)}, f32[3,4]{1,0:T(4,128)S(1)}, u32[]{:S(2)}, u32[]{:S(2)}) collective-permute-start(f32[3,4]{1,0:T(4,128)S(1)} %get-tuple-element.445), channel_id=1, source_target_pairs={{0,1},{1,2},{2,3},{3,4},{4,5},{5,6},{6,7},{7,8},{8,9},{9,10},{10,1... | collective-permute-start | bytes 152 | tf_op jit(solution)/shard_map/ppermute | solution.py:46
  7.2 17.9 %collective-permute-start.3 = (f32[3,4]{1,0:T(4,128)S(1)}, f32[3,4]{1,0:T(4,128)S(1)}, u32[]{:S(2)}, u32[]{:S(2)}) collective-permute-start(f32[3,4]{1,0:T(4,128)S(1)} %get-tuple-element.446), channel_id=1, source_target_pairs={{1,0},{2,1},{3,2},{4,3},{5,4},{6,5},{7,6},{8,7},{9,8},{10,9},{11,1... | collective-permute-start | bytes 152 | tf_op jit(solution)/shard_map/ppermute | solution.py:49
  27.7 2.4 gather_fusion.7
  31.6 3.5 all_to_all.15
  37.4 7.1 %all-to-all-start.2 = ((f32[64,1,192]{2,1,0:T(1,128)}), f32[64,1,192]{2,1,0:T(1,128)}, u32[]{:S(2)}, u32[]{:S(2)}) async-start(f32[64,1,192]{2,1,0:T(1,128)} %reshape.659), calls=%async_computation.2 | async-start | bytes 131072 | tf_op jit(solution)/shard_map/all_to_all | solution.py:31
  49.1 1.9 gather_fusion.4
  51.0 120.0 %scatter_custom_fusion.2 = s32[256]{0:T(256)S(1)} fusion(s32[32768]{0:T(1024)S(1)} %bitcast.464, s32[32768]{0:T(1024)S(1)} %bitcast.465, s32[]{:T(128)} %constant.205.clone.1), kind=kCustom, calls=%fused_computation.298 | custom fusion | bytes 1028
  175.0 233.3 %while.18 = (s32[]{:T(128)}, f32[9,125,128]{1,2,0:T(8,128)S(1)}, f32[4,12,256]{0,2,1:T(8,128)}, f32[2,125,125]{2,1,0:T(8,128)S(1)}, f32[3,125,125]{2,1,0:T(8,128...) while((s32[]{:T(128)}, f32[9,125,128]{1,2,0:T(8,128)S(1)}, ...), condition=%wide.region_5.7_spmd.clone, body=%wide.region_0.6_spmd.clone.sunk | while | flops 4621616640 | bytes 95887288 | solution.py:170
  175.0 2.3 collective-permute-start
  177.3 3.3 collective-permute-start.1
  194.8 2.0 fusion.343
  206.1 2.0 fusion.349
  217.7 2.1 fusion.355
  234.7 3.1 fusion.360
  244.9 3.1 fusion.365
  251.5 2.0 collective-permute-start
  253.4 3.7 collective-permute-start.1
  271.3 2.0 fusion.343
  282.4 2.0 fusion.349
  294.0 2.1 fusion.355
  311.1 3.1 fusion.360
  321.3 3.1 fusion.365
  327.7 2.0 collective-permute-start
  329.7 3.7 collective-permute-start.1
  347.5 2.0 fusion.343
  358.8 2.0 fusion.349
  370.4 2.1 fusion.355
  387.4 3.1 fusion.360
  397.6 3.1 fusion.365
  408.3 2.0 copy.207
  411.8 19.1 %all-to-all-start = ((f32[128,2,48]{2,1,0:T(2,128)}), f32[128,2,48]{2,1,0:T(2,128)S(1)}, u32[]{:S(2)}, u32[]{:S(2)}) async-start(f32[128,2,48]{2,1,0:T(2,128)} %bitcast.11), calls=%async_computation | async-start | bytes 262144 | tf_op jit(solution)/shard_map/all_to_all | solution.py:175
  434.9 8.1 %all-to-all-done = f32[128,2,48]{2,1,0:T(2,128)S(1)} async-done(((f32[128,2,48]{2,1,0:T(2,128)}), f32[128,2,48]{2,1,0:T(2,128)S(1)}, u32[]{:S(2)}, u32[]{:S(2)}) %all-to-all-start) | async-done | bytes 49184 | tf_op jit(solution)/shard_map/all_to_all | solution.py:175
  (464 shorter events, 195.9 us)
Async XLA Ops:
  1.5 171.5 %collective-permute-start.2 = (f32[3,4]{1,0:T(4,128)S(1)}, f32[3,4]{1,0:T(4,128)S(1)}, u32[]{:S(2)}, u32[]{:S(2)}) collective-permute-start(f32[3,4]{1,0:T(4,128)S(1)} %get-tuple-element.445), channel_id=1, source_target_pairs={{0,1},{1,2},{2,3},{3,4},{4,5},{5,6},{6,7},{7,8},{8,9},{9,10},{10,1... | collective-permute-start | bytes 152 | tf_op jit(solution)/shard_map/ppermute | solution.py:46
  7.2 165.8 %collective-permute-start.3 = (f32[3,4]{1,0:T(4,128)S(1)}, f32[3,4]{1,0:T(4,128)S(1)}, u32[]{:S(2)}, u32[]{:S(2)}) collective-permute-start(f32[3,4]{1,0:T(4,128)S(1)} %get-tuple-element.446), channel_id=1, source_target_pairs={{1,0},{2,1},{3,2},{4,3},{5,4},{6,5},{7,6},{8,7},{9,8},{10,9},{11,1... | collective-permute-start | bytes 152 | tf_op jit(solution)/shard_map/ppermute | solution.py:49
  27.7 16.8 %copy-start.13 = (s32[32768]{0:T(1024)S(1)}, s32[32768]{0:T(1024)}, u32[]{:S(2)}) copy-start(s32[32768]{0:T(1024)} %param.22) | copy-start | bytes 393220
  30.1 15.1 %copy-start = (s32[128]{0:T(128)S(1)}, s32[128]{0:T(128)}, u32[]{:S(2)}) copy-start(s32[128]{0:T(128)} %param.21) | copy-start | bytes 1540
  30.1 17.0 %copy-start.31 = (f32[3,9,9]{2,0,1:T(4,128)S(1)}, f32[3,9,9]{2,0,1:T(4,128)}, u32[]{:S(2)}) copy-start(f32[3,9,9]{2,0,1:T(4,128)} %param.16) | copy-start | bytes 2920
  30.1 16.9 %copy-start.22 = (f32[2,125,125]{2,0,1:T(2,128)S(1)}, f32[2,125,125]{2,0,1:T(2,128)}, u32[]{:S(2)}) copy-start(f32[2,125,125]{2,0,1:T(2,128)} %param.17) | copy-start | bytes 375004
  31.3 15.7 %copy-start.21 = (f32[125,256]{1,0:T(8,128)S(1)}, f32[125,256]{1,0:T(8,128)}, u32[]{:S(2)}) copy-start(f32[125,256]{1,0:T(8,128)} %param.20) | copy-start | bytes 384004
  37.4 374.4 %all-to-all-start.2 = ((f32[64,1,192]{2,1,0:T(1,128)}), f32[64,1,192]{2,1,0:T(1,128)}, u32[]{:S(2)}, u32[]{:S(2)}) async-start(f32[64,1,192]{2,1,0:T(1,128)} %reshape.659), calls=%async_computation.2 | async-start | bytes 131072 | tf_op jit(solution)/shard_map/all_to_all | solution.py:31
  48.9 123.3 %copy-start.15 = (f32[9,125,128]{2,1,0:T(8,128)S(1)}, f32[9,125,128]{2,1,0:T(8,128)}, u32[]{:S(2)}) copy-start(f32[9,125,128]{2,1,0:T(8,128)} %param.14) | copy-start | bytes 1728004
  50.9 122.1 %copy-start.25 = (f32[3,128]{1,0:T(4,128)S(1)}, f32[3,128]{1,0:T(4,128)}, u32[]{:S(2)}) copy-start(f32[3,128]{1,0:T(4,128)} %param.18) | copy-start | bytes 4612
  175.0 12.8 %copy-start.19 = (f32[136]{0:T(256)}, f32[136]{0:T(256)S(1)}, u32[]{:S(2)}) copy-start(f32[136]{0:T(256)S(1)} %get-tuple-element.609) | copy-start | bytes 1636 | tf_op jit(solution)/shard_map/while
  175.0 48.8 %copy-start.4 = (f32[2,125,125]{2,1,0:T(8,128)}, f32[2,125,125]{2,1,0:T(8,128)S(1)}, u32[]{:S(2)}) copy-start(f32[2,125,125]{2,1,0:T(8,128)S(1)} %get-tuple-element.605) | copy-start | bytes 375004 | tf_op jit(solution)/shard_map/while
  175.0 11.5 %collective-permute-start = (f32[9,125,4]{1,2,0:T(4,128)S(1)}, f32[9,125,4]{1,2,0:T(4,128)S(1)}, u32[]{:S(2)}, u32[]{:S(2)}) collective-permute-start(f32[9,125,4]{1,2,0:T(4,128)S(1)} %get-tuple-element.540), channel_id=1, source_target_pairs={{1,0},{2,1},{3,2},{4,3},{5,4},{6,5},{7,6},{8,7},{9,8},{10,9},{11,1... | collective-permute-start | bytes 54008 | tf_op jit(solution)/shard_map/while/body/eval_jaxpr/ppermute | solution.py:49
  177.3 9.2 %collective-permute-start.1 = (f32[9,125,4]{1,2,0:T(4,128)S(1)}, f32[9,125,4]{1,2,0:T(4,128)S(1)}, u32[]{:S(2)}, u32[]{:S(2)}) collective-permute-start(f32[9,125,4]{1,2,0:T(4,128)S(1)} %get-tuple-element.541), channel_id=1, source_target_pairs={{0,1},{1,2},{2,3},{3,4},{4,5},{5,6},{6,7},{7,8},{8,9},{9,10},{10,1... | collective-permute-start | bytes 54008 | tf_op jit(solution)/shard_map/while/body/eval_jaxpr/ppermute | solution.py:46
  244.8 6.2 %copy-start.5 = (f32[2,125,125]{2,1,0:T(8,128)S(1)}, f32[2,125,125]{2,1,0:T(8,128)}, u32[]{:S(2)}) copy-start(f32[2,125,125]{2,1,0:T(8,128)} %copy-done.4) | copy-start | bytes 375004 | tf_op jit(solution)/shard_map/while
  244.8 6.2 %copy-start.6 = (f32[9,125,128]{1,2,0:T(8,128)S(1)}, f32[9,125,128]{1,2,0:T(8,128)}, u32[]{:S(2)}) copy-start(f32[9,125,128]{1,2,0:T(8,128)} %fusion.360) | copy-start | bytes 1728004 | tf_op jit(solution)/shard_map/while
  244.9 6.2 %copy-start.20 = (f32[136]{0:T(256)S(1)}, f32[136]{0:T(256)}, u32[]{:S(2)}) copy-start(f32[136]{0:T(256)} %copy-done.19) | copy-start | bytes 1636 | tf_op jit(solution)/shard_map/while
  251.4 12.8 %copy-start.19 = (f32[136]{0:T(256)}, f32[136]{0:T(256)S(1)}, u32[]{:S(2)}) copy-start(f32[136]{0:T(256)S(1)} %get-tuple-element.609) | copy-start | bytes 1636 | tf_op jit(solution)/shard_map/while
  251.5 48.7 %copy-start.4 = (f32[2,125,125]{2,1,0:T(8,128)}, f32[2,125,125]{2,1,0:T(8,128)S(1)}, u32[]{:S(2)}) copy-start(f32[2,125,125]{2,1,0:T(8,128)S(1)} %get-tuple-element.605) | copy-start | bytes 375004 | tf_op jit(solution)/shard_map/while
  251.5 11.5 %collective-permute-start = (f32[9,125,4]{1,2,0:T(4,128)S(1)}, f32[9,125,4]{1,2,0:T(4,128)S(1)}, u32[]{:S(2)}, u32[]{:S(2)}) collective-permute-start(f32[9,125,4]{1,2,0:T(4,128)S(1)} %get-tuple-element.540), channel_id=1, source_target_pairs={{1,0},{2,1},{3,2},{4,3},{5,4},{6,5},{7,6},{8,7},{9,8},{10,9},{11,1... | collective-permute-start | bytes 54008 | tf_op jit(solution)/shard_map/while/body/eval_jaxpr/ppermute | solution.py:49
  253.4 9.6 %collective-permute-start.1 = (f32[9,125,4]{1,2,0:T(4,128)S(1)}, f32[9,125,4]{1,2,0:T(4,128)S(1)}, u32[]{:S(2)}, u32[]{:S(2)}) collective-permute-start(f32[9,125,4]{1,2,0:T(4,128)S(1)} %get-tuple-element.541), channel_id=1, source_target_pairs={{0,1},{1,2},{2,3},{3,4},{4,5},{5,6},{6,7},{7,8},{8,9},{9,10},{10,1... | collective-permute-start | bytes 54008 | tf_op jit(solution)/shard_map/while/body/eval_jaxpr/ppermute | solution.py:46
  321.3 6.2 %copy-start.5 = (f32[2,125,125]{2,1,0:T(8,128)S(1)}, f32[2,125,125]{2,1,0:T(8,128)}, u32[]{:S(2)}) copy-start(f32[2,125,125]{2,1,0:T(8,128)} %copy-done.4) | copy-start | bytes 375004 | tf_op jit(solution)/shard_map/while
  321.3 6.2 %copy-start.6 = (f32[9,125,128]{1,2,0:T(8,128)S(1)}, f32[9,125,128]{1,2,0:T(8,128)}, u32[]{:S(2)}) copy-start(f32[9,125,128]{1,2,0:T(8,128)} %fusion.360) | copy-start | bytes 1728004 | tf_op jit(solution)/shard_map/while
  327.7 12.8 %copy-start.19 = (f32[136]{0:T(256)}, f32[136]{0:T(256)S(1)}, u32[]{:S(2)}) copy-start(f32[136]{0:T(256)S(1)} %get-tuple-element.609) | copy-start | bytes 1636 | tf_op jit(solution)/shard_map/while
  327.7 48.8 %copy-start.4 = (f32[2,125,125]{2,1,0:T(8,128)}, f32[2,125,125]{2,1,0:T(8,128)S(1)}, u32[]{:S(2)}) copy-start(f32[2,125,125]{2,1,0:T(8,128)S(1)} %get-tuple-element.605) | copy-start | bytes 375004 | tf_op jit(solution)/shard_map/while
  327.7 11.5 %collective-permute-start = (f32[9,125,4]{1,2,0:T(4,128)S(1)}, f32[9,125,4]{1,2,0:T(4,128)S(1)}, u32[]{:S(2)}, u32[]{:S(2)}) collective-permute-start(f32[9,125,4]{1,2,0:T(4,128)S(1)} %get-tuple-element.540), channel_id=1, source_target_pairs={{1,0},{2,1},{3,2},{4,3},{5,4},{6,5},{7,6},{8,7},{9,8},{10,9},{11,1... | collective-permute-start | bytes 54008 | tf_op jit(solution)/shard_map/while/body/eval_jaxpr/ppermute | solution.py:49
  329.7 9.6 %collective-permute-start.1 = (f32[9,125,4]{1,2,0:T(4,128)S(1)}, f32[9,125,4]{1,2,0:T(4,128)S(1)}, u32[]{:S(2)}, u32[]{:S(2)}) collective-permute-start(f32[9,125,4]{1,2,0:T(4,128)S(1)} %get-tuple-element.541), channel_id=1, source_target_pairs={{0,1},{1,2},{2,3},{3,4},{4,5},{5,6},{6,7},{7,8},{8,9},{9,10},{10,1... | collective-permute-start | bytes 54008 | tf_op jit(solution)/shard_map/while/body/eval_jaxpr/ppermute | solution.py:46
  397.5 6.2 %copy-start.5 = (f32[2,125,125]{2,1,0:T(8,128)S(1)}, f32[2,125,125]{2,1,0:T(8,128)}, u32[]{:S(2)}) copy-start(f32[2,125,125]{2,1,0:T(8,128)} %copy-done.4) | copy-start | bytes 375004 | tf_op jit(solution)/shard_map/while
  410.4 23.7 %copy-start.34 = (f32[256]{0:T(256)S(1)}, f32[256]{0:T(256)}, u32[]{:S(2)}) copy-start(f32[256]{0:T(256)} %compare_convert_fusion.5) | copy-start | bytes 3076
  411.8 31.2 %all-to-all-start = ((f32[128,2,48]{2,1,0:T(2,128)}), f32[128,2,48]{2,1,0:T(2,128)S(1)}, u32[]{:S(2)}, u32[]{:S(2)}) async-start(f32[128,2,48]{2,1,0:T(2,128)} %bitcast.11), calls=%async_computation | async-start | bytes 262144 | tf_op jit(solution)/shard_map/all_to_all | solution.py:175
  432.6 11.3 %copy-start.17 = (f32[256,48]{1,0:T(8,128)S(1)}, f32[256,48]{1,0:T(8,128)}, u32[]{:S(2)}) copy-start(f32[256,48]{1,0:T(8,128)} %copy-done.16) | copy-start | bytes 147460
  432.6 11.3 %copy-start.33 = (f32[256]{0:T(256)S(1)}, f32[256]{0:T(256)}, u32[]{:S(2)}) copy-start(f32[256]{0:T(256)} %compare_convert_fusion.6) | copy-start | bytes 3076
  (59 other events, 147.4 us)
where the time goes:
time: 453 us; the launch traced here: 446 us
  local copies, waits for them, and re-layouts  196 us (43%)
  matrix products  124 us (27%)
  starting transfers between devices  66.7 us (15%)
  other arithmetic  39.1 us (9%)
  waiting for transfers between devices  8.11 us (2%)
  loops' own time  7.01 us (2%)
    unnamed x45, local copies, waits for them, and re-layouts  124 us
    dot_general x36, matrix products, advance(): jnp.einsum('gf,fpe->gpe', coupling[k], gradient, precision=HIGH)  41 us
    dot_general x36, matrix products, advance(): gradient = jnp.einsum('pq,fqe->fpe', derivative[k], middle, precision=HIGH)  40.8 us
    dot_general x12, matrix products, advance(): jnp.einsum('pq,fqe->fpe', face_lift[1], extended[:, :, 2:] - middle, prec...  24.7 us
    ppermute x4, starting transfers between devices, with_halo(): lax.ppermute(lax.slice_in_dim(block, 0, width, axis=dim), axis, backward)  24.1 us
    all_to_all x1, starting transfers between devices, shards(): lax.all_to_all(send_buffer, MX, split_axis=0, concat_axis=0, tiled=True)  19.1 us
    dot_general x12, matrix products, advance(): jnp.einsum('pq,fqe->fpe', face_lift[0], extended[:, :, :-2] - middle, pre...  17.5 us
    ppermute x4, starting transfers between devices, with_halo(): lax.ppermute(lax.slice_in_dim(block, block.shape[dim] - width, None, axis...  16.4 us
  transfers between devices with their start and end apart: 10, of which 1 were waited for; matrix products, arithmetic and copies ran while one was open for 80% of the time, Pallas kernels for 0%

commit v1 on v0

v1 whole, which is shorter than its diff:
```python
import jax
import jax.numpy as jnp
from jax import lax
from jax.experimental import pallas as pl
from jax.experimental.pallas import tpu as pltpu
from jax.sharding import Mesh
from jax.sharding import PartitionSpec as P

STEPS = 12
COMPS = 4
MX = ("mx_0", "mx_1", "mx_2")
SHOTS_MX = ("shots", "mx_0", "mx_1", "mx_2")
F32 = jnp.float32
BF16 = jnp.bfloat16
I32 = jnp.int32
LANES = 128
GROUP = 8
PAIR_ROWS = 2 * GROUP
HALO = 16
OBS_LANE = 64
VMEM = pltpu.VMEM


def iota(shape, dim):
    return lax.broadcasted_iota(I32, shape, dim)


def split2(x):
    hi = x.astype(BF16)
    return hi, (x - hi.astype(F32)).astype(BF16)


def split3(x):
    hi = x.astype(BF16)
    rest = x - hi.astype(F32)
    mid = rest.astype(BF16)
    return hi, mid, (rest - mid.astype(F32)).astype(BF16)


def dot(a, b):
    return jnp.dot(a, b, preferred_element_type=F32)


def pick(onehot, x):
    parts = split3(x)
    return dot(onehot, parts[0]) + (dot(onehot, parts[1]) + dot(onehot, parts[2]))


def padded(x, rows, cols):
    if x.shape[1] < cols:
        x = jnp.concatenate([x, jnp.zeros((x.shape[0], cols - x.shape[1]), x.dtype)], axis=1)
    if x.shape[0] < rows:
        x = jnp.concatenate([x, jnp.zeros((rows - x.shape[0], cols), x.dtype)], axis=0)
    return x


def turn_kernel(initial_ref, metric_ref, own_ref, low_ref, high_ref):
    fields, _, elems = initial_ref.shape
    for f in range(fields):
        own_ref[f] = padded(initial_ref[f], LANES, elems).T
    for k in range(metric_ref.shape[0]):
        own_ref[fields + k] = jnp.broadcast_to(metric_ref[k : k + 1, :], (LANES, elems)).T
    low_ref[...] = own_ref[:, :HALO, :]
    high_ref[...] = own_ref[:, elems - HALO :, :]


def turn(initial, metric):
    fields, _, elems = initial.shape
    planes = fields + metric.shape[0]
    return pl.pallas_call(
        turn_kernel,
        out_shape=(
            jax.ShapeDtypeStruct((planes, elems, LANES), F32),
            jax.ShapeDtypeStruct((planes, HALO, LANES), F32),
            jax.ShapeDtypeStruct((planes, HALO, LANES), F32),
        ),
        compiler_params=pltpu.CompilerParams(vmem_limit_bytes=8 << 20),
        name="turn",
    )(initial, metric)


def plan_kernel(
    me_ref,
    live_ref,
    lives_ref,
    derivative_ref,
    coupling_ref,
    lift_ref,
    element_ref,
    weight_ref,
    order_ref,
    observed_ref,
    wt_ref,
    wl_ref,
    ck_ref,
    eh_ref,
    wp_ref,
    acc_ref,
    back_slot_ref,
    back_pos_ref,
    seen_ref,
):
    slots, width = observed_ref.shape
    blocks = slots // 2
    me = me_ref[0]
    axes = derivative_ref.shape[0]
    fields = coupling_ref.shape[1]
    dh, dl = [], []
    for k in range(axes):
        hi, lo = split2(padded(derivative_ref[k], LANES, LANES).T)
        dh.append(hi)
        dl.append(lo)
    zero = jnp.zeros((LANES, LANES), BF16)
    for row, (left, right) in enumerate(
        [(dh[0], dl[0]), (dh[1], dl[1]), (dh[2], dl[2]), (dh[2], zero), (dh[0], zero), (dh[1], zero)]
    ):
        wt_ref[row * LANES : (row + 1) * LANES, :] = jnp.concatenate([left, right], axis=1)
    l0h, l0l = split2(padded(lift_ref[0], LANES, LANES).T)
    l1h, l1l = split2(padded(lift_ref[1], LANES, LANES).T)
    for row, (left, right) in enumerate([(l0h, l1h), (l0h, l1h), (l0l, l1l)]):
        wl_ref[row * LANES : (row + 1) * LANES, :] = jnp.concatenate([left, right], axis=1)
    rows, cols = axes * fields * GROUP, fields * GROUP
    spread_rows = (iota((rows, axes * fields), 0) // GROUP == iota((rows, axes * fields), 1)).astype(BF16)
    spread_cols = (iota((fields, cols), 0) == iota((fields, cols), 1) // GROUP).astype(BF16)
    stacked = jnp.concatenate([coupling_ref[k] for k in range(axes)], axis=0)
    by_row = pick(spread_rows, stacked)
    by_hi, by_mid, by_lo = split3(by_row)
    full = dot(by_hi, spread_cols) + (dot(by_mid, spread_cols) + dot(by_lo, spread_cols))
    diagonal = iota((rows, cols), 0) % GROUP == iota((rows, cols), 1) % GROUP
    full = jnp.where(diagonal, full, 0.0)
    full_hi = full.astype(BF16).astype(F32)
    ck_ref[...] = jnp.concatenate([full_hi, full_hi, full - full_hi], axis=1).astype(BF16)
    order = order_ref[...]
    half = iota((slots, LANES), 0) % 2
    position = half * LANES + iota((slots, LANES), 1)
    slot_of = order % slots
    key = (position * slots + slot_of).astype(F32)
    mine = (order // slots) == me
    big = float(slots * slots)
    first = jnp.min(jnp.where(mine, key, big), axis=1, keepdims=True)
    last = jnp.max(jnp.where(mine, key, -1.0), axis=1, keepdims=True)
    first = jnp.broadcast_to(first, (slots, LANES))
    last = jnp.broadcast_to(last, (slots, LANES))
    up = lambda x: pltpu.roll(x, slots - 1, 0)
    down = lambda x: pltpu.roll(x, 1, 0)
    chosen = jnp.where(half == 0, jnp.minimum(first, up(first)), jnp.maximum(last, down(last)))
    chosen = chosen.astype(I32) % slots
    chosen = jnp.concatenate([chosen, chosen], axis=1)
    send_slot = chosen == iota((slots, slots), 1)
    send_slot_f = send_slot.astype(F32)
    send_slot_b = send_slot_f.astype(BF16)
    my_rows = order_ref[pl.ds(2 * me, 2), :]
    my_row = jnp.concatenate([my_rows[0:1], my_rows[1:2]], axis=1)
    my_block = my_row // slots
    my_slot = (my_row % slots).astype(F32)
    row_id = iota((slots, slots), 0)
    col_id = iota((slots, slots), 1).astype(F32)
    from_block = my_block == row_id // 2
    jmin = jnp.min(jnp.where(from_block, col_id, big), axis=1, keepdims=True)
    jmax = jnp.max(jnp.where(from_block, col_id, -1.0), axis=1, keepdims=True)
    picked = jnp.where(row_id % 2 == 0, jmin, jmax)
    at_pos = (picked == col_id).astype(F32)
    lives = jnp.broadcast_to(lives_ref[...].astype(F32), (slots, blocks))
    live_of = jnp.sum(
        jnp.where(iota((slots, blocks), 0) // 2 == iota((slots, blocks), 1), lives, 0.0), axis=1, keepdims=True
    )
    slot_there = jnp.sum(at_pos * my_slot, axis=1, keepdims=True)
    alive = (slot_there < live_of).astype(F32)
    at_pos_live = (at_pos * alive).T
    back_pos_ref[...] = at_pos_live.astype(BF16)
    live_pos = jnp.sum(at_pos_live, axis=1, keepdims=True)
    observed = observed_ref[...]
    seen_ref[...] = observed * live_pos
    back_slot_ref[...] = send_slot_f.T.astype(BF16)
    my_live = live_ref[me]
    element = element_ref[...].astype(F32)
    element_sent = jnp.sum(send_slot_f * element, axis=1, keepdims=True)
    hit = (element_sent.astype(I32) == iota((slots, LANES), 1)).astype(BF16)
    eh_ref[...] = jnp.concatenate([hit, hit], axis=1)
    weight = jnp.where(iota(weight_ref.shape, 1) < my_live, weight_ref[...], 0.0)
    weight = padded(weight, LANES, slots).T
    wp_ref[...] = pick(send_slot_b, weight)
    lane, time = iota((width, LANES), 1) - OBS_LANE, iota((width, LANES), 0)
    comp = time // STEPS
    flipped = comp * STEPS + (STEPS - 1 - (time - comp * STEPS))
    turn_time = (lane == flipped).astype(BF16)
    hi, mid, lo = split3(observed)
    reversed_rows = dot(hi, turn_time) + (dot(mid, turn_time) + dot(lo, turn_time))
    acc_ref[...] = pick(at_pos.astype(BF16), reversed_rows)


def plan(me, live_counts, derivative, coupling, face_lift, rec_element, rec_weight, order, observed):
    slots, width = observed.shape
    axes, fields = coupling.shape[0], coupling.shape[1]
    block = axes * fields * GROUP
    smem = pl.BlockSpec(memory_space=pltpu.SMEM)
    vmem = pl.BlockSpec(memory_space=VMEM)
    return pl.pallas_call(
        plan_kernel,
        in_specs=[smem, smem] + [vmem] * 8,
        out_shape=(
            jax.ShapeDtypeStruct((6 * LANES, 2 * LANES), BF16),
            jax.ShapeDtypeStruct((3 * LANES, 2 * LANES), BF16),
            jax.ShapeDtypeStruct((block, 3 * fields * GROUP), BF16),
            jax.ShapeDtypeStruct((slots, 2 * LANES), BF16),
            jax.ShapeDtypeStruct((slots, LANES), F32),
            jax.ShapeDtypeStruct((slots, LANES), F32),
            jax.ShapeDtypeStruct((slots, slots), BF16),
            jax.ShapeDtypeStruct((slots, slots), BF16),
            jax.ShapeDtypeStruct((slots, width), F32),
        ),
        compiler_params=pltpu.CompilerParams(vmem_limit_bytes=16 << 20),
        cost_estimate=pl.CostEstimate(flops=4_000_000_000, bytes_accessed=2_000_000, transcendentals=0),
        name="plan",
    )(
        me,
        live_counts,
        live_counts.reshape(1, -1),
        derivative,
        coupling,
        face_lift,
        rec_element.reshape(1, -1),
        rec_weight,
        order,
        observed,
    )


def march_kernel(
    me_ref,
    own_ref,
    low_ref,
    high_ref,
    wt_ref,
    wl_ref,
    ck_ref,
    eh_ref,
    wp_ref,
    acc0_ref,
    send_ref,
    rev_ref,
    u_ref,
    m_ref,
    h_ref,
    t_ref,
    lt_ref,
    lu_ref,
    *,
    last_block,
):
    planes, elems, _ = own_ref.shape
    axes = 3
    fields = planes - axes
    rows = elems + 2 * HALO
    pairs = rows // PAIR_ROWS
    slots = eh_ref.shape[0]
    dt = 0.5 / STEPS
    me = me_ref[0]
    dt_low = jnp.where(me == 0, 0.0, dt).astype(F32)
    dt_high = jnp.where(me == last_block, 0.0, dt).astype(F32)
    u_ref[:, :HALO, :] = low_ref[:fields]
    u_ref[:, HALO : HALO + elems, :] = own_ref[:fields]
    u_ref[:, HALO + elems :, :] = high_ref[:fields]
    m_ref[:, :HALO, :] = low_ref[fields:]
    m_ref[:, HALO : HALO + elems, :] = own_ref[fields:]
    m_ref[:, HALO + elems :, :] = high_ref[fields:]
    send_ref[...] = acc0_ref[...]
    rev_ref[...] = jnp.zeros(rev_ref.shape, F32)
    tile = fields * PAIR_ROWS

    def load_pair(j):
        r = j * PAIR_ROWS
        halves = ([], [])
        for f in range(fields):
            x = u_ref[f, r : r + PAIR_ROWS, :]
            hi, lo = split2(x)
            lu_ref[j, f * PAIR_ROWS : (f + 1) * PAIR_ROWS, :LANES] = hi
            lu_ref[j, f * PAIR_ROWS : (f + 1) * PAIR_ROWS, LANES:] = lo
            hi32 = hi.astype(F32)
            lo32 = x - hi32
            for side in range(2):
                halves[side].append((hi32[side * GROUP : (side + 1) * GROUP], lo32[side * GROUP : (side + 1) * GROUP]))
        columns = []
        for side in range(2):
            his = [p[0] for p in halves[side]]
            los = [p[1] for p in halves[side]]
            columns.append(jnp.concatenate(his + los + his, axis=0).astype(BF16))
        return jnp.concatenate(columns, axis=1)

    def couple(j):
        v = dot(ck_ref[...], load_pair(j))
        r = j * PAIR_ROWS
        for k in range(axes):
            ma = m_ref[k, r : r + GROUP, :]
            mb = m_ref[k, r + GROUP : r + PAIR_ROWS, :]
            parts = []
            for g in range(fields):
                base = (k * fields + g) * GROUP
                parts.append(v[base : base + GROUP, :LANES] * ma)
                parts.append(v[base : base + GROUP, LANES:] * mb)
            hi, lo = split2(jnp.concatenate(parts, axis=0))
            lanes = ((0, 4), (1, 5), (2, 3))[k]
            lt_ref[j, :, lanes[0] * LANES : (lanes[0] + 1) * LANES] = hi
            lt_ref[j, :, lanes[1] * LANES : (lanes[1] + 1) * LANES] = lo

    def apply(j):
        r = j * PAIR_ROWS
        both = dot(lt_ref[j], wt_ref[...])
        both = both[:, :LANES] + both[:, LANES:]
        lifted = dot(lu_ref[j], wl_ref[: 2 * LANES, :]) + dot(lu_ref[j, :, :LANES], wl_ref[2 * LANES :, :])
        for g in range(fields):
            t_ref[g, r : r + PAIR_ROWS, :] = both[g * PAIR_ROWS : (g + 1) * PAIR_ROWS]
            for side in range(2):
                h_ref[side, g, GROUP + r : GROUP + r + PAIR_ROWS, :] = lifted[
                    g * PAIR_ROWS : (g + 1) * PAIR_ROWS, side * LANES : (side + 1) * LANES
                ]

    def update(j):
        r = j * PAIR_ROWS
        a = GROUP + r
        factor = dt_low if r < HALO else (dt_high if r >= HALO + elems else dt)
        for g in range(fields):
            lift = (h_ref[0, g, a - 1 : a - 1 + PAIR_ROWS, :] - h_ref[0, g, a : a + PAIR_ROWS, :]) + (
                h_ref[1, g, a + 1 : a + 1 + PAIR_ROWS, :] - h_ref[1, g, a : a + PAIR_ROWS, :]
            )
            u_ref[g, r : r + PAIR_ROWS, :] = u_ref[g, r : r + PAIR_ROWS, :] + factor * (
                t_ref[g, r : r + PAIR_ROWS, :] + lift
            )

    def sample(t, have_parts):
        lo_pair, hi_pair = HALO // PAIR_ROWS, (HALO + elems) // PAIR_ROWS
        columns = []
        own = slice(HALO, HALO + elems)
        for c in range(COMPS):
            if c < 3 and have_parts:
                part = lambda lanes: jnp.concatenate(
                    [lu_ref[j, c * PAIR_ROWS : (c + 1) * PAIR_ROWS, lanes] for j in range(lo_pair, hi_pair)], axis=0
                )
                hi, lo = part(slice(0, LANES)), part(slice(LANES, 2 * LANES))
            else:
                if c < 3:
                    x = u_ref[c, own, :]
                else:
                    x = (u_ref[3, own, :] + u_ref[4, own, :] + u_ref[5, own, :]) / 3.0
                hi, lo = split2(x)
            columns.append(jnp.concatenate([hi, lo], axis=0))
        lane = iota((slots, LANES), 1)
        send = send_ref[...]
        rev = rev_ref[...]
        for c in range(0, COMPS, 2):
            found = dot(eh_ref[...], jnp.concatenate(columns[c : c + 2], axis=1))
            for i in range(2):
                value = jnp.sum(found[:, i * LANES : (i + 1) * LANES] * wp_ref[...], axis=1, keepdims=True)
                send = jnp.where(lane == (c + i) * STEPS + t, value, send)
                rev = jnp.where(lane == OBS_LANE + (c + i) * STEPS + (STEPS - 1) - t, value, rev)
        send_ref[...] = send
        rev_ref[...] = rev

    def step(t, first, stop):
        for j in range(first, stop):
            couple(j)
        for j in range(first, stop):
            apply(j)
        for j in range(first, stop):
            update(j)

    def body(first, stop):
        def run(t, carry):
            step(t, first, stop)
            sample(t, False)
            return carry

        return run

    lax.fori_loop(0, 3, body(0, pairs), 0)
    lax.fori_loop(3, STEPS, body(0, pairs), 0)


def march(me, own, low, high, operators, last_block):
    wt, wl, ck, eh, wp, acc0 = operators
    planes, elems, _ = own.shape
    fields = planes - 3
    rows = elems + 2 * HALO
    pairs = rows // PAIR_ROWS
    slots = eh.shape[0]
    smem = pl.BlockSpec(memory_space=pltpu.SMEM)
    vmem = pl.BlockSpec(memory_space=VMEM)
    import functools

    return pl.pallas_call(
        functools.partial(march_kernel, last_block=last_block),
        in_specs=[smem] + [vmem] * 9,
        out_shape=(
            jax.ShapeDtypeStruct((slots, LANES), F32),
            jax.ShapeDtypeStruct((slots, LANES), F32),
        ),
        scratch_shapes=[
            VMEM((fields, rows, LANES), F32),
            VMEM((3, rows, LANES), F32),
            VMEM((2, fields, rows + 2 * GROUP, LANES), F32),
            VMEM((fields, rows, LANES), F32),
            VMEM((pairs, fields * PAIR_ROWS, 6 * LANES), BF16),
            VMEM((pairs, fields * PAIR_ROWS, 2 * LANES), BF16),
        ],
        compiler_params=pltpu.CompilerParams(vmem_limit_bytes=40 << 20),
        cost_estimate=pl.CostEstimate(flops=20_000_000_000, bytes_accessed=4_000_000, transcendentals=0),
        name="march",
    )(me, own, low, high, wt, wl, ck, eh, wp, acc0)


def finish_kernel(me_ref, live_ref, got_ref, rev_ref, back_slot_ref, back_pos_ref, seen_ref, res_ref, mis_ref, adj_ref):
    slots, width = res_ref.shape
    got = got_ref[...]
    ordered = pick(back_pos_ref[...], got)
    residual = ordered[:, :width] - seen_ref[...]
    res_ref[...] = residual
    squares = padded(residual * residual, slots, LANES)
    mis_ref[...] = 0.5 * jnp.sum(squares.T, axis=0, keepdims=True)
    adjoint = pick(back_slot_ref[...], pltpu.roll(rev_ref[...] - got, LANES - OBS_LANE, 1))
    live = iota((slots, LANES), 0) < live_ref[me_ref[0]]
    adj_ref[...] = jnp.where(live, adjoint, 0.0)[:, :width]


def finish(me, live_counts, got, rev, back_slot, back_pos, seen):
    slots, width = seen.shape
    smem = pl.BlockSpec(memory_space=pltpu.SMEM)
    vmem = pl.BlockSpec(memory_space=VMEM)
    return pl.pallas_call(
        finish_kernel,
        in_specs=[smem, smem] + [vmem] * 5,
        out_shape=(
            jax.ShapeDtypeStruct((slots, width), F32),
            jax.ShapeDtypeStruct((1, slots), F32),
            jax.ShapeDtypeStruct((slots, width), F32),
        ),
        compiler_params=pltpu.CompilerParams(vmem_limit_bytes=8 << 20),
        name="finish",
    )(me, live_counts, got, rev, back_slot, back_pos, seen)


def shards(
    initial,
    derivative,
    coupling,
    face_lift,
    metric,
    rec_element,
    rec_weight,
    live_counts,
    shot_order,
    observed,
):
    blocks = lax.axis_size(MX)
    slots = rec_element.shape[0]
    me = lax.axis_index(MX).astype(I32).reshape(1)
    own, low, high = turn(initial, metric)
    forward = [(i, i + 1) for i in range(blocks - 1)]
    backward = [(target, source) for source, target in forward]
    from_low = lax.ppermute(high, MX, forward)
    from_high = lax.ppermute(low, MX, backward)
    order = shot_order.reshape(-1, LANES)
    wt, wl, ck, eh, wp, acc0, back_slot, back_pos, seen = plan(
        me, live_counts, derivative, coupling, face_lift, rec_element, rec_weight, order, observed
    )
    send, rev = march(me, own, from_low, from_high, (wt, wl, ck, eh, wp, acc0), blocks - 1)
    got = lax.all_to_all(send.reshape(blocks, 2, LANES), MX, split_axis=0, concat_axis=0, tiled=True)
    residual, misfit, adjoint = finish(me, live_counts, got.reshape(slots, LANES), rev, back_slot, back_pos, seen)
    return (residual, misfit.reshape(slots), adjoint)


def solution(mesh):
    split = Mesh(
        mesh.devices.reshape(mesh.shape["shots"], 8, 8, 2), ("shots", "mx_0", "mx_1", "mx_2")
    )
    in_specs = (
        P("shots", None, MX),
        P(),
        P(),
        P(),
        P(None, MX),
        P(MX),
        P(None, MX),
        P(),
        P(),
        P(SHOTS_MX, None),
    )
    out_specs = (P(SHOTS_MX, None), P(SHOTS_MX), P(SHOTS_MX, None))
    return jax.shard_map(
        shards, mesh=split, in_specs=in_specs, out_specs=out_specs, check_vma=False
    )
```

time: 453 us -> 76.7 us (0.17); the launches traced: 446 us -> 76.4 us
  local copies, waits for them, and re-layouts: 196 us -> 4.14 us
  matrix products: 124 us -> 0 us
  starting transfers between devices: 66.7 us -> 23.8 us
  other arithmetic: 39.1 us -> 0 us
  Pallas kernels: 0 us -> 29.4 us
  blocking collectives: 3.46 us -> 18.3 us
  waiting for transfers between devices: 8.11 us -> 0.01 us
  loops' own time: 7.01 us -> 0 us
    dot_general x96 -> x0, matrix products: 124 us -> none  [the longest x36 41 us: advance(): jnp.einsum('gf,fpe->gpe', coupling[k], gradient, precision=HIGH)]
    unnamed x45 -> x25, local copies, waits for them, and re-layouts: 124 us -> 4.14 us
    pallas_call x0 -> x4, Pallas kernels: none -> 29.4 us  [the longest x1 26 us: march(): pl.pallas_call(functools.partial(march_kernel, last_block=last_block), in...]
    all_to_all x2 -> x0, starting transfers between devices: 26.2 us -> none  [the longest x1 19.1 us: shards(): lax.all_to_all(send_buffer, MX, split_axis=0, concat_axis=0, tiled=True)]
    slice x37 -> x0, local copies, waits for them, and re-layouts: 20.4 us -> none  [the longest x12 9.03 us: sample(): wavefield[0]]
    gather x16 -> x0, local copies, waits for them, and re-layouts: 18.4 us -> none  [the longest x12 11.9 us: sample(): columns = jnp.take(components, elements, axis=2)]
    ppermute x8 -> x2, starting transfers between devices: 40.5 us -> 23.8 us  [the longest x1 18 us: shards(): from_high = lax.ppermute(low, MX, backward)]
    all_to_all x1, blocking collectives: 3.46 us -> 18.3 us  [shards(): lax.all_to_all(send.reshape(blocks, 2, LANES), MX, split_axis=0, concat_a...]
  transfers between devices with their start and end apart: 10 -> 2, of which waited for: 1 -> 0; matrix products, arithmetic and copies ran while one was open for 80% -> 0% of each run, Pallas kernels for 0% -> 2%
where the time goes in v1:
time: 76.7 us; the launch traced here: 76.4 us
  Pallas kernels  29.4 us (38%)
  starting transfers between devices  23.8 us (31%)
  blocking collectives  18.3 us (24%)
  local copies, waits for them, and re-layouts  4.14 us (5%)
  between operations  0.81 us (1%)
    pallas_call x1, Pallas kernels, march(): pl.pallas_call(functools.partial(march_kernel, last_block=last_block), in...  26 us
    all_to_all x1, blocking collectives, shards(): lax.all_to_all(send.reshape(blocks, 2, LANES), MX, split_axis=0, concat_a...  18.3 us
    ppermute x1, starting transfers between devices, shards(): from_high = lax.ppermute(low, MX, backward)  18 us
    ppermute x1, starting transfers between devices, shards(): from_low = lax.ppermute(high, MX, forward)  5.75 us
    unnamed x25, local copies, waits for them, and re-layouts  4.14 us
    pallas_call x1, Pallas kernels, plan(): pl.pallas_call(plan_kernel, in_specs=[smem, smem] + [vmem] * 8, out_shape...  1.59 us
  transfers between devices with their start and end apart: 2, of which 0 were waited for; matrix products, arithmetic and copies ran while one was open for 0% of the time, Pallas kernels for 2%

profile of v1, /device:TPU:513, one launch (start us, length us, event | category | flops | bytes accessed | tf_op | source)
XLA Modules:
  0.0 76.4 jit_solution(13998096014032449768)
XLA Ops:
  0.6 0.0 copy-start
  0.6 1.1 %copy-done = f32[9,125,128]{2,1,0:T(8,128)S(1)} copy-done((f32[9,125,128]{2,1,0:T(8,128)S(1)}, f32[9,125,128]{2,1,0:T(8,128)}, u32[]{:S(2)}) %copy-start) | copy-done | bytes 576024
  1.7 0.0 copy-start.1
  1.7 0.7 copy-done.1
  2.4 0.0 copy-start.7
  2.4 0.0 copy-start.9
  2.4 0.3 turn.1
  2.7 5.7 %collective-permute-start = (f32[12,16,128]{2,1,0:T(8,128)S(1)}, f32[12,16,128]{2,1,0:T(8,128)S(1)}, u32[]{:S(2)}, u32[]{:S(2)}) collective-permute-start(f32[12,16,128]{2,1,0:T(8,128)S(1)} %get-tuple-element.21), channel_id=1, source_target_pairs={{0,1},{1,2},{2,3},{3,4},{4,5},{5,6},{6,7},{7,8},{8,9},{9,10},{10,1... | collective-permute-start | bytes 294920 | tf_op jit(solution)/shard_map/ppermute | solution.py:459
  8.4 0.0 copy-start.8
  8.4 18.0 %collective-permute-start.1 = (f32[12,16,128]{2,1,0:T(8,128)S(1)}, f32[12,16,128]{2,1,0:T(8,128)S(1)}, u32[]{:S(2)}, u32[]{:S(2)}) collective-permute-start(f32[12,16,128]{2,1,0:T(8,128)S(1)} %get-tuple-element.22), channel_id=1, source_target_pairs={{1,0},{2,1},{3,2},{4,3},{5,4},{6,5},{7,6},{8,7},{9,8},{10,9},{11,1... | collective-permute-start | bytes 294920 | tf_op jit(solution)/shard_map/ppermute | solution.py:460
  26.5 0.0 copy-done.7
  26.5 0.0 copy-start.3
  26.5 0.0 copy-start.5
  26.5 0.0 copy-done.8
  26.5 0.0 copy-start.4
  26.6 0.1 copy.15.observed_ref
  26.7 0.0 copy-done.9
  26.7 0.0 copy-start.2
  26.7 0.0 copy-start.6
  26.7 0.7 copy-done.3
  27.4 0.1 copy-done.5
  27.5 0.1 copy-done.4
  27.6 0.0 copy-done.2
  27.6 0.0 copy-done.6
  27.6 1.6 %plan.1 = (bf16[768,256]{1,0:T(8,128)(2,1)S(1)}, bf16[384,256]{1,0:T(8,128)(2,1)S(1)}, bf16[216,216]{1,0:T(8,128)(2,1)S(1)}, bf16[256,256]{1,0:T(8,128)(2,1)S(1)...) custom-call(s32[1]{0:T(128)} %bitcast.me_ref, ...), custom_call_target="tpu_custom_call" | custom-call | flops 4000000000 | bytes 2000000 | tf_op jit(solution)/shard_map/plan/pallas_call | solution.py:198
  29.2 0.0 collective-permute-done.low_ref
  29.2 0.0 collective-permute-done.1.high_ref
  29.2 26.0 %march.1 = (f32[256,128]{1,0:T(8,128)S(1)}, f32[256,128]{1,0:T(8,128)S(1)}) custom-call(s32[1]{0:T(128)} %bitcast.me_ref, f32[12,128,128]{2,1,0:T(8,128)S(1)} %get-tuple-element.20.own_ref, f32[12,16,128]{2,1,0:T(8,128)S(1)} %collective-permute-done.low_ref, f32[12,16,128]{2,1,0:T(8,128)S(1)} %collective-permute-done.1.high_ref, ...), custom_call_target="tpu_custom_call" | custom-call | flops 20000000000 | bytes 4000000 | tf_op jit(solution)/shard_map/march/pallas_call | solution.py:390
  55.2 18.3 %all_to_all.5 = f32[128,2,128]{2,1,0:T(2,128)S(1)} all-to-all(f32[128,2,128]{2,1,0:T(2,128)S(1)} %bitcast.8), channel_id=1, replica_groups=mesh['shots'=2,'mx_0'=8,'mx_1'=8,'mx_2'=2] {'mx_0','mx_1','mx_2'}, dimensions={0} | all-to-all | bytes 262144 | tf_op jit(solution)/shard_map/all_to_all | solution.py:466
  73.5 1.5 %finish.1 = (f32[256,48]{1,0:T(8,128)S(1)}, f32[1,256]{1,0:T(1,128)}, f32[256,48]{1,0:T(8,128)S(1)}) custom-call(s32[1]{0:T(128)} %bitcast.me_ref, s32[128]{0:T(128)S(1)} %copy-done.2, f32[256,128]{1,0:T(8,128)S(1)} %bitcast.7, f32[256,128]{1,0:T(8,128)S(1)} %get-tuple-element.30.rev_ref, bf16[256,256]{1,0:T(8,128)(2,1)S(1)} %get-tuple-element.31.back_slot_ref, ...), custom_call_target="tpu_custom_call" | custom-call | tf_op jit(solution)/shard_map/finish/pallas_call | solution.py:428
  75.0 0.7 copy.16
  75.7 0.7 copy.17
  (2 shorter events, 0.0 us)
Async XLA Ops:
  0.6 1.1 %copy-start = (f32[9,125,128]{2,1,0:T(8,128)S(1)}, f32[9,125,128]{2,1,0:T(8,128)}, u32[]{:S(2)}) copy-start(f32[9,125,128]{2,1,0:T(8,128)} %initial_ref.1) | copy-start | bytes 1728004
  1.7 0.7 copy-start.1
  2.4 24.1 %copy-start.7 = (f32[2,125,125]{2,0,1:T(2,128)S(1)}, f32[2,125,125]{2,0,1:T(2,128)}, u32[]{:S(2)}) copy-start(f32[2,125,125]{2,0,1:T(2,128)} %param.13) | copy-start | bytes 375004
  2.4 24.3 %copy-start.9 = (f32[3,9,9]{2,0,1:T(4,128)S(1)}, f32[3,9,9]{2,0,1:T(4,128)}, u32[]{:S(2)}) copy-start(f32[3,9,9]{2,0,1:T(4,128)} %param.12) | copy-start | bytes 2920
  2.7 26.5 %collective-permute-start = (f32[12,16,128]{2,1,0:T(8,128)S(1)}, f32[12,16,128]{2,1,0:T(8,128)S(1)}, u32[]{:S(2)}, u32[]{:S(2)}) collective-permute-start(f32[12,16,128]{2,1,0:T(8,128)S(1)} %get-tuple-element.21), channel_id=1, source_target_pairs={{0,1},{1,2},{2,3},{3,4},{4,5},{5,6},{6,7},{7,8},{8,9},{9,10},{10,1... | collective-permute-start | bytes 294920 | tf_op jit(solution)/shard_map/ppermute | solution.py:459
  8.4 18.1 %copy-start.8 = (f32[256,48]{0,1:T(8,128)S(1)}, f32[256,48]{0,1:T(8,128)}, u32[]{:S(2)}) copy-start(f32[256,48]{0,1:T(8,128)} %param.19) | copy-start | bytes 147460
  8.4 20.8 %collective-permute-start.1 = (f32[12,16,128]{2,1,0:T(8,128)S(1)}, f32[12,16,128]{2,1,0:T(8,128)S(1)}, u32[]{:S(2)}, u32[]{:S(2)}) collective-permute-start(f32[12,16,128]{2,1,0:T(8,128)S(1)} %get-tuple-element.22), channel_id=1, source_target_pairs={{1,0},{2,1},{3,2},{4,3},{5,4},{6,5},{7,6},{8,7},{9,8},{10,9},{11,1... | collective-permute-start | bytes 294920 | tf_op jit(solution)/shard_map/ppermute | solution.py:460
  26.5 0.9 %copy-start.3 = (f32[3,125,125]{2,1,0:T(8,128)S(1)}, f32[3,125,125]{2,1,0:T(8,128)}, u32[]{:S(2)}) copy-start(f32[3,125,125]{2,1,0:T(8,128)} %derivative_ref.1) | copy-start | bytes 562504
  26.5 1.0 %copy-start.5 = (s32[32768]{0:T(1024)S(1)}, s32[32768]{0:T(1024)}, u32[]{:S(2)}) copy-start(s32[32768]{0:T(1024)} %param.18) | copy-start | bytes 393220
  26.5 1.0 %copy-start.4 = (f32[125,256]{1,0:T(8,128)S(1)}, f32[125,256]{1,0:T(8,128)}, u32[]{:S(2)}) copy-start(f32[125,256]{1,0:T(8,128)} %weight_ref.1) | copy-start | bytes 384004
  26.7 0.9 %copy-start.2 = (s32[128]{0:T(128)S(1)}, s32[128]{0:T(128)}, u32[]{:S(2)}) copy-start(s32[128]{0:T(128)} %live_ref.3) | copy-start | bytes 1540
  26.7 0.9 %copy-start.6 = (s32[256]{0:T(256)S(1)}, s32[256]{0:T(256)}, u32[]{:S(2)}) copy-start(s32[256]{0:T(256)} %param.15) | copy-start | bytes 3076

commit v2 on v1

--- a/solution.py
+++ b/solution.py
@@ -268,8 +268,7 @@
     rev_ref[...] = jnp.zeros(rev_ref.shape, F32)
     tile = fields * PAIR_ROWS
 
-    def load_pair(j):
-        r = j * PAIR_ROWS
+    def load_pair(j, r):
         halves = ([], [])
         for f in range(fields):
             x = u_ref[f, r : r + PAIR_ROWS, :]
@@ -287,9 +286,8 @@
             columns.append(jnp.concatenate(his + los + his, axis=0).astype(BF16))
         return jnp.concatenate(columns, axis=1)
 
-    def couple(j):
-        v = dot(ck_ref[...], load_pair(j))
-        r = j * PAIR_ROWS
+    def couple(j, r):
+        v = dot(ck_ref[...], load_pair(j, r))
         for k in range(axes):
             ma = m_ref[k, r : r + GROUP, :]
             mb = m_ref[k, r + GROUP : r + PAIR_ROWS, :]
@@ -303,8 +301,7 @@
             lt_ref[j, :, lanes[0] * LANES : (lanes[0] + 1) * LANES] = hi
             lt_ref[j, :, lanes[1] * LANES : (lanes[1] + 1) * LANES] = lo
 
-    def apply(j):
-        r = j * PAIR_ROWS
+    def apply(j, r):
         both = dot(lt_ref[j], wt_ref[...])
         both = both[:, :LANES] + both[:, LANES:]
         lifted = dot(lu_ref[j], wl_ref[: 2 * LANES, :]) + dot(lu_ref[j, :, :LANES], wl_ref[2 * LANES :, :])
@@ -315,35 +312,24 @@
                     g * PAIR_ROWS : (g + 1) * PAIR_ROWS, side * LANES : (side + 1) * LANES
                 ]
 
-    def update(j):
-        r = j * PAIR_ROWS
+    def update(r):
         a = GROUP + r
         factor = dt_low if r < HALO else (dt_high if r >= HALO + elems else dt)
         for g in range(fields):
-            lift = (h_ref[0, g, a - 1 : a - 1 + PAIR_ROWS, :] - h_ref[0, g, a : a + PAIR_ROWS, :]) + (
-                h_ref[1, g, a + 1 : a + 1 + PAIR_ROWS, :] - h_ref[1, g, a : a + PAIR_ROWS, :]
+            lift = (h_ref[0, g, a - 1 : a - 1 + GROUP, :] - h_ref[0, g, a : a + GROUP, :]) + (
+                h_ref[1, g, a + 1 : a + 1 + GROUP, :] - h_ref[1, g, a : a + GROUP, :]
             )
-            u_ref[g, r : r + PAIR_ROWS, :] = u_ref[g, r : r + PAIR_ROWS, :] + factor * (
-                t_ref[g, r : r + PAIR_ROWS, :] + lift
-            )
-
-    def sample(t, have_parts):
-        lo_pair, hi_pair = HALO // PAIR_ROWS, (HALO + elems) // PAIR_ROWS
+            u_ref[g, r : r + GROUP, :] = u_ref[g, r : r + GROUP, :] + factor * (t_ref[g, r : r + GROUP, :] + lift)
+
+    def sample(t):
         columns = []
         own = slice(HALO, HALO + elems)
         for c in range(COMPS):
-            if c < 3 and have_parts:
-                part = lambda lanes: jnp.concatenate(
-                    [lu_ref[j, c * PAIR_ROWS : (c + 1) * PAIR_ROWS, lanes] for j in range(lo_pair, hi_pair)], axis=0
-                )
-                hi, lo = part(slice(0, LANES)), part(slice(LANES, 2 * LANES))
+            if c < 3:
+                x = u_ref[c, own, :]
             else:
-                if c < 3:
-                    x = u_ref[c, own, :]
-                else:
-                    x = (u_ref[3, own, :] + u_ref[4, own, :] + u_ref[5, own, :]) / 3.0
-                hi, lo = split2(x)
-            columns.append(jnp.concatenate([hi, lo], axis=0))
+                x = (u_ref[3, own, :] + u_ref[4, own, :] + u_ref[5, own, :]) / 3.0
+            columns.append(jnp.concatenate(split2(x), axis=0))
         lane = iota((slots, LANES), 1)
         send = send_ref[...]
         rev = rev_ref[...]
@@ -356,24 +342,38 @@
         send_ref[...] = send
         rev_ref[...] = rev
 
-    def step(t, first, stop):
-        for j in range(first, stop):
-            couple(j)
-        for j in range(first, stop):
-            apply(j)
-        for j in range(first, stop):
-            update(j)
-
-    def body(first, stop):
-        def run(t, carry):
-            step(t, first, stop)
-            sample(t, False)
+    def step(t, drop):
+        sample(t - 1)
+        base = drop * GROUP
+        count = (rows - 2 * base) // PAIR_ROWS
+        at = lambda j: base + j * PAIR_ROWS
+        couple(0, at(0))
+        for j in range(count):
+            if j + 1 < count:
+                couple(j + 1, at(j + 1))
+            apply(j, at(j))
+            if j >= 1:
+                update(at(j - 1))
+                update(at(j - 1) + GROUP)
+        update(at(count - 1))
+        update(at(count - 1) + GROUP)
+
+    def run(drop):
+        def body(t, carry):
+            step(t, drop)
             return carry
 
-        return run
-
-    lax.fori_loop(0, 3, body(0, pairs), 0)
-    lax.fori_loop(3, STEPS, body(0, pairs), 0)
+        return body
+
+    groups = [-(-(STEPS - t) // GROUP) for t in range(STEPS)]
+    t = 0
+    while t < STEPS:
+        stop = t
+        while stop < STEPS and groups[stop] == groups[t]:
+            stop += 1
+        lax.fori_loop(t, stop, run(HALO // GROUP - groups[t]), 0)
+        t = stop
+    sample(STEPS - 1)
 
 
 def march(me, own, low, high, operators, last_block):

time: 76.7 us -> 72.5 us (0.945)
  Pallas kernels: 29.4 us -> 25.1 us
    pallas_call x1, Pallas kernels: 26 us -> 21.8 us  [march(): pl.pallas_call(functools.partial(march_kernel, last_block=last_block), in...]
where the time goes in v2:
time: 72.5 us; the launch traced here: 72.2 us
  Pallas kernels  25.1 us (35%)
  starting transfers between devices  23.8 us (33%)
  blocking collectives  18.3 us (25%)
  local copies, waits for them, and re-layouts  4.14 us (6%)
  between operations  0.81 us (1%)
    pallas_call x1, Pallas kernels, march(): pl.pallas_call(functools.partial(march_kernel, last_block=last_block), in...  21.8 us
    all_to_all x1, blocking collectives, shards(): lax.all_to_all(send.reshape(blocks, 2, LANES), MX, split_axis=0, concat_a...  18.3 us
    ppermute x1, starting transfers between devices, shards(): from_high = lax.ppermute(low, MX, backward)  18 us
    ppermute x1, starting transfers between devices, shards(): from_low = lax.ppermute(high, MX, forward)  5.75 us
    unnamed x25, local copies, waits for them, and re-layouts  4.14 us
    pallas_call x1, Pallas kernels, plan(): pl.pallas_call(plan_kernel, in_specs=[smem, smem] + [vmem] * 8, out_shape...  1.59 us
    pallas_call x1, Pallas kernels, finish(): pl.pallas_call(finish_kernel, in_specs=[smem, smem] + [vmem] * 5, out_sha...  1.49 us
  transfers between devices with their start and end apart: 2, of which 0 were waited for; matrix products, arithmetic and copies ran while one was open for 0% of the time, Pallas kernels for 2%

profile of v2, /device:TPU:513, one launch (start us, length us, event | category | flops | bytes accessed | tf_op | source)
XLA Modules:
  0.0 72.2 jit_solution(10936299961102805008)
XLA Ops:
  0.6 0.0 copy-start
  0.6 1.1 %copy-done = f32[9,125,128]{2,1,0:T(8,128)S(1)} copy-done((f32[9,125,128]{2,1,0:T(8,128)S(1)}, f32[9,125,128]{2,1,0:T(8,128)}, u32[]{:S(2)}) %copy-start) | copy-done | bytes 576024
  1.7 0.0 copy-start.1
  1.7 0.7 copy-done.1
  2.4 0.0 copy-start.7
  2.4 0.0 copy-start.9
  2.4 0.3 turn.1
  2.7 5.7 %collective-permute-start = (f32[12,16,128]{2,1,0:T(8,128)S(1)}, f32[12,16,128]{2,1,0:T(8,128)S(1)}, u32[]{:S(2)}, u32[]{:S(2)}) collective-permute-start(f32[12,16,128]{2,1,0:T(8,128)S(1)} %get-tuple-element.21), channel_id=1, source_target_pairs={{0,1},{1,2},{2,3},{3,4},{4,5},{5,6},{6,7},{7,8},{8,9},{9,10},{10,1... | collective-permute-start | bytes 294920 | tf_op jit(solution)/shard_map/ppermute | solution.py:459
  8.4 0.0 copy-start.8
  8.4 18.0 %collective-permute-start.1 = (f32[12,16,128]{2,1,0:T(8,128)S(1)}, f32[12,16,128]{2,1,0:T(8,128)S(1)}, u32[]{:S(2)}, u32[]{:S(2)}) collective-permute-start(f32[12,16,128]{2,1,0:T(8,128)S(1)} %get-tuple-element.22), channel_id=1, source_target_pairs={{1,0},{2,1},{3,2},{4,3},{5,4},{6,5},{7,6},{8,7},{9,8},{10,9},{11,1... | collective-permute-start | bytes 294920 | tf_op jit(solution)/shard_map/ppermute | solution.py:460
  26.5 0.0 copy-done.7
  26.5 0.0 copy-start.3
  26.5 0.0 copy-start.5
  26.5 0.0 copy-done.8
  26.5 0.0 copy-start.4
  26.6 0.1 copy.15.observed_ref
  26.7 0.0 copy-done.9
  26.7 0.0 copy-start.2
  26.7 0.0 copy-start.6
  26.7 0.7 copy-done.3
  27.4 0.1 copy-done.5
  27.5 0.1 copy-done.4
  27.6 0.0 copy-done.2
  27.6 0.0 copy-done.6
  27.6 1.6 %plan.1 = (bf16[768,256]{1,0:T(8,128)(2,1)S(1)}, bf16[384,256]{1,0:T(8,128)(2,1)S(1)}, bf16[216,216]{1,0:T(8,128)(2,1)S(1)}, bf16[256,256]{1,0:T(8,128)(2,1)S(1)...) custom-call(s32[1]{0:T(128)} %bitcast.me_ref, ...), custom_call_target="tpu_custom_call" | custom-call | flops 4000000000 | bytes 2000000 | tf_op jit(solution)/shard_map/plan/pallas_call | solution.py:198
  29.2 0.0 collective-permute-done.low_ref
  29.2 0.0 collective-permute-done.1.high_ref
  29.2 21.8 %march.1 = (f32[256,128]{1,0:T(8,128)S(1)}, f32[256,128]{1,0:T(8,128)S(1)}) custom-call(s32[1]{0:T(128)} %bitcast.me_ref, f32[12,128,128]{2,1,0:T(8,128)S(1)} %get-tuple-element.20.own_ref, f32[12,16,128]{2,1,0:T(8,128)S(1)} %collective-permute-done.low_ref, f32[12,16,128]{2,1,0:T(8,128)S(1)} %collective-permute-done.1.high_ref, ...), custom_call_target="tpu_custom_call" | custom-call | flops 20000000000 | bytes 4000000 | tf_op jit(solution)/shard_map/march/pallas_call | solution.py:390
  50.9 18.3 %all_to_all.5 = f32[128,2,128]{2,1,0:T(2,128)S(1)} all-to-all(f32[128,2,128]{2,1,0:T(2,128)S(1)} %bitcast.8), channel_id=1, replica_groups=mesh['shots'=2,'mx_0'=8,'mx_1'=8,'mx_2'=2] {'mx_0','mx_1','mx_2'}, dimensions={0} | all-to-all | bytes 262144 | tf_op jit(solution)/shard_map/all_to_all | solution.py:466
  69.3 1.5 %finish.1 = (f32[256,48]{1,0:T(8,128)S(1)}, f32[1,256]{1,0:T(1,128)}, f32[256,48]{1,0:T(8,128)S(1)}) custom-call(s32[1]{0:T(128)} %bitcast.me_ref, s32[128]{0:T(128)S(1)} %copy-done.2, f32[256,128]{1,0:T(8,128)S(1)} %bitcast.7, f32[256,128]{1,0:T(8,128)S(1)} %get-tuple-element.30.rev_ref, bf16[256,256]{1,0:T(8,128)(2,1)S(1)} %get-tuple-element.31.back_slot_ref, ...), custom_call_target="tpu_custom_call" | custom-call | tf_op jit(solution)/shard_map/finish/pallas_call | solution.py:428
  70.8 0.7 copy.16
  71.5 0.7 copy.17
  (2 shorter events, 0.0 us)
Async XLA Ops:
  0.6 1.1 %copy-start = (f32[9,125,128]{2,1,0:T(8,128)S(1)}, f32[9,125,128]{2,1,0:T(8,128)}, u32[]{:S(2)}) copy-start(f32[9,125,128]{2,1,0:T(8,128)} %initial_ref.1) | copy-start | bytes 1728004
  1.7 0.7 copy-start.1
  2.4 24.1 %copy-start.7 = (f32[2,125,125]{2,0,1:T(2,128)S(1)}, f32[2,125,125]{2,0,1:T(2,128)}, u32[]{:S(2)}) copy-start(f32[2,125,125]{2,0,1:T(2,128)} %param.13) | copy-start | bytes 375004
  2.4 24.3 %copy-start.9 = (f32[3,9,9]{2,0,1:T(4,128)S(1)}, f32[3,9,9]{2,0,1:T(4,128)}, u32[]{:S(2)}) copy-start(f32[3,9,9]{2,0,1:T(4,128)} %param.12) | copy-start | bytes 2920
  2.7 26.5 %collective-permute-start = (f32[12,16,128]{2,1,0:T(8,128)S(1)}, f32[12,16,128]{2,1,0:T(8,128)S(1)}, u32[]{:S(2)}, u32[]{:S(2)}) collective-permute-start(f32[12,16,128]{2,1,0:T(8,128)S(1)} %get-tuple-element.21), channel_id=1, source_target_pairs={{0,1},{1,2},{2,3},{3,4},{4,5},{5,6},{6,7},{7,8},{8,9},{9,10},{10,1... | collective-permute-start | bytes 294920 | tf_op jit(solution)/shard_map/ppermute | solution.py:459
  8.4 18.1 %copy-start.8 = (f32[256,48]{0,1:T(8,128)S(1)}, f32[256,48]{0,1:T(8,128)}, u32[]{:S(2)}) copy-start(f32[256,48]{0,1:T(8,128)} %param.19) | copy-start | bytes 147460
  8.4 20.8 %collective-permute-start.1 = (f32[12,16,128]{2,1,0:T(8,128)S(1)}, f32[12,16,128]{2,1,0:T(8,128)S(1)}, u32[]{:S(2)}, u32[]{:S(2)}) collective-permute-start(f32[12,16,128]{2,1,0:T(8,128)S(1)} %get-tuple-element.22), channel_id=1, source_target_pairs={{1,0},{2,1},{3,2},{4,3},{5,4},{6,5},{7,6},{8,7},{9,8},{10,9},{11,1... | collective-permute-start | bytes 294920 | tf_op jit(solution)/shard_map/ppermute | solution.py:460
  26.5 0.9 %copy-start.3 = (f32[3,125,125]{2,1,0:T(8,128)S(1)}, f32[3,125,125]{2,1,0:T(8,128)}, u32[]{:S(2)}) copy-start(f32[3,125,125]{2,1,0:T(8,128)} %derivative_ref.1) | copy-start | bytes 562504
  26.5 1.0 %copy-start.5 = (s32[32768]{0:T(1024)S(1)}, s32[32768]{0:T(1024)}, u32[]{:S(2)}) copy-start(s32[32768]{0:T(1024)} %param.18) | copy-start | bytes 393220
  26.5 1.0 %copy-start.4 = (f32[125,256]{1,0:T(8,128)S(1)}, f32[125,256]{1,0:T(8,128)}, u32[]{:S(2)}) copy-start(f32[125,256]{1,0:T(8,128)} %weight_ref.1) | copy-start | bytes 384004
  26.7 0.9 %copy-start.2 = (s32[128]{0:T(128)S(1)}, s32[128]{0:T(128)}, u32[]{:S(2)}) copy-start(s32[128]{0:T(128)} %live_ref.3) | copy-start | bytes 1540
  26.7 0.9 %copy-start.6 = (s32[256]{0:T(256)S(1)}, s32[256]{0:T(256)}, u32[]{:S(2)}) copy-start(s32[256]{0:T(256)} %param.15) | copy-start | bytes 3076

commit v3 on v2

v3 whole, which is shorter than its diff:
```python
import functools

import jax
import jax.numpy as jnp
from jax import lax
from jax.experimental import pallas as pl
from jax.experimental.pallas import tpu as pltpu
from jax.sharding import Mesh
from jax.sharding import PartitionSpec as P


STEPS = 12
EARLY = 3
DT = 0.5 / STEPS
AXES = 3
COMPS = 4
MX = ("mx_0", "mx_1", "mx_2")
SHOTS_MX = ("shots", "mx_0", "mx_1", "mx_2")
F32 = jnp.float32
BF16 = jnp.bfloat16
I32 = jnp.int32
LANES = 128
GROUP = 8
PAIR_ROWS = 2 * GROUP
HALO = 16
OBS_LANE = 64
VMEM = pltpu.VMEM


def iota(shape, dim):
    return lax.broadcasted_iota(I32, shape, dim)


def split2(x):
    hi = x.astype(BF16)
    return hi, (x - hi.astype(F32)).astype(BF16)


def split3(x):
    hi = x.astype(BF16)
    rest = x - hi.astype(F32)
    mid = rest.astype(BF16)
    return hi, mid, (rest - mid.astype(F32)).astype(BF16)


def dot(a, b):
    return jnp.dot(a, b, preferred_element_type=F32)


def pick(onehot, x):
    parts = split3(x)
    return dot(onehot, parts[0]) + (dot(onehot, parts[1]) + dot(onehot, parts[2]))


def padded(x, rows, cols):
    if x.shape[1] < cols:
        x = jnp.concatenate([x, jnp.zeros((x.shape[0], cols - x.shape[1]), x.dtype)], axis=1)
    if x.shape[0] < rows:
        x = jnp.concatenate([x, jnp.zeros((rows - x.shape[0], cols), x.dtype)], axis=0)
    return x


def turn_kernel(me_ref, *refs):
    staged = (len(refs) - 10) // 2
    initial_hbm, metric_hbm = refs[:2]
    from_refs = refs[2 : 2 + staged]
    own_ref, near_ref, far_ref = refs[2 + staged : 5 + staged]
    to_refs = refs[5 + staged : 5 + 2 * staged]
    initial_ref, metric_ref, low_ref, high_ref, sems = refs[-5:]
    copies = [
        pltpu.make_async_copy(initial_hbm, initial_ref, sems.at[0]),
        pltpu.make_async_copy(metric_hbm, metric_ref, sems.at[1]),
    ]
    copies += [pltpu.make_async_copy(x, y, sems.at[2 + i]) for i, (x, y) in enumerate(zip(from_refs, to_refs))]
    for copy in copies:
        copy.start()
    copies[0].wait()
    copies[1].wait()
    fields, _, elems = initial_ref.shape
    for f in range(fields):
        own_ref[f] = padded(initial_ref[f], LANES, elems).T
    for k in range(metric_ref.shape[0]):
        own_ref[fields + k] = jnp.broadcast_to(metric_ref[k : k + 1, :], (LANES, elems)).T
    third = iota((elems, LANES), 1) // (LANES // 3)
    factors = jnp.where(third == 0, own_ref[fields], jnp.where(third == 1, own_ref[fields + 1], own_ref[fields + 2]))
    for edge_ref, rows in ((low_ref, slice(0, STEPS)), (high_ref, slice(elems - STEPS, elems))):
        for f in range(fields):
            edge_ref[f * STEPS : (f + 1) * STEPS, :] = own_ref[f, rows, :]
        edge_ref[fields * STEPS :, :] = factors[rows]
    odd = me_ref[0] % 2 == 1
    near_ref[...] = jnp.where(odd, low_ref[...], high_ref[...])
    far_ref[...] = jnp.where(odd, high_ref[...], low_ref[...])
    for copy in copies[2:]:
        copy.wait()


def turn(me, initial, metric, staged):
    fields, _, elems = initial.shape
    planes = fields + metric.shape[0]
    edge = jax.ShapeDtypeStruct(((fields + 1) * STEPS, LANES), F32)
    hbm = pl.BlockSpec(memory_space=pltpu.HBM)
    return pl.pallas_call(
        turn_kernel,
        in_specs=[pl.BlockSpec(memory_space=pltpu.SMEM)] + [hbm] * (2 + len(staged)),
        out_shape=(jax.ShapeDtypeStruct((planes, elems, LANES), F32), edge, edge)
        + tuple(jax.ShapeDtypeStruct(x.shape, x.dtype) for x in staged),
        scratch_shapes=[
            VMEM(initial.shape, F32),
            VMEM(metric.shape, F32),
            VMEM(edge.shape, F32),
            VMEM(edge.shape, F32),
            pltpu.SemaphoreType.DMA((2 + len(staged),)),
        ],
        compiler_params=pltpu.CompilerParams(vmem_limit_bytes=8 << 20),
        name="turn",
    )(me, *(pltpu.with_memory_space_constraint(x, pltpu.HBM) for x in (initial, metric, *staged)))


def plan_kernel(
    me_ref,
    lives_ref,
    derivative_ref,
    coupling_ref,
    lift_ref,
    element_ref,
    weight_ref,
    order_ref,
    observed_ref,
    wt_ref,
    wl_ref,
    ck_ref,
    eh_ref,
    wp_ref,
    acc_ref,
    to_slot_ref,
    to_pos_ref,
    seen_ref,
):
    width, slots = observed_ref.shape
    blocks = slots // 2
    me = me_ref[0]
    axes = derivative_ref.shape[0]
    fields = coupling_ref.shape[1]
    dh, dl = [], []
    for k in range(axes):
        hi, lo = split2(padded(derivative_ref[k], LANES, LANES).T)
        dh.append(hi)
        dl.append(lo)
    zero = jnp.zeros((LANES, LANES), BF16)
    for row, (left, right) in enumerate(
        [(dh[0], dl[0]), (dh[1], dl[1]), (dh[2], dl[2]), (dh[2], zero), (dh[0], zero), (dh[1], zero)]
    ):
        wt_ref[row * LANES : (row + 1) * LANES, :] = jnp.concatenate([left, right], axis=1)
    l0h, l0l = split2(padded(lift_ref[0], LANES, LANES).T)
    l1h, l1l = split2(padded(lift_ref[1], LANES, LANES).T)
    for row, (left, right) in enumerate([(l0h, l1h), (l0h, l1h), (l0l, l1l)]):
        wl_ref[row * LANES : (row + 1) * LANES, :] = jnp.concatenate([left, right], axis=1)
    rows, cols = axes * fields * GROUP, fields * GROUP
    spread_rows = (iota((rows, axes * fields), 0) // GROUP == iota((rows, axes * fields), 1)).astype(BF16)
    spread_cols = (iota((fields, cols), 0) == iota((fields, cols), 1) // GROUP).astype(BF16)
    stacked = jnp.concatenate([coupling_ref[k] for k in range(axes)], axis=0)
    by_row = pick(spread_rows, stacked)
    by_hi, by_mid, by_lo = split3(by_row)
    full = dot(by_hi, spread_cols) + (dot(by_mid, spread_cols) + dot(by_lo, spread_cols))
    diagonal = iota((rows, cols), 0) % GROUP == iota((rows, cols), 1) % GROUP
    full = jnp.where(diagonal, full, 0.0)
    full_hi = full.astype(BF16).astype(F32)
    ck_ref[...] = jnp.concatenate([full_hi, full_hi, full - full_hi], axis=1).astype(BF16)
    order = order_ref[...]
    half = iota((slots, LANES), 0) % 2
    position = half * LANES + iota((slots, LANES), 1)
    slot_of = order % slots
    key = (position * slots + slot_of).astype(F32)
    mine = (order // slots) == me
    big = float(slots * slots)
    first = jnp.min(jnp.where(mine, key, big), axis=1, keepdims=True)
    last = jnp.max(jnp.where(mine, key, -1.0), axis=1, keepdims=True)
    first = jnp.broadcast_to(first, (slots, LANES))
    last = jnp.broadcast_to(last, (slots, LANES))
    up = lambda x: pltpu.roll(x, slots - 1, 0)
    down = lambda x: pltpu.roll(x, 1, 0)
    chosen = jnp.where(half == 0, jnp.minimum(first, up(first)), jnp.maximum(last, down(last)))
    chosen = chosen.astype(I32) % slots
    chosen = jnp.concatenate([chosen, chosen], axis=1)
    send_slot = chosen == iota((slots, slots), 1)
    send_slot_f = send_slot.astype(F32)
    send_slot_b = send_slot_f.astype(BF16)
    my_rows = order_ref[pl.ds(2 * me, 2), :]
    my_row = jnp.concatenate([my_rows[0:1], my_rows[1:2]], axis=1)
    my_block = my_row // slots
    my_slot = (my_row % slots).astype(F32)
    row_id = iota((slots, slots), 0)
    col_id = iota((slots, slots), 1).astype(F32)
    from_block = my_block == row_id // 2
    jmin = jnp.min(jnp.where(from_block, col_id, big), axis=1, keepdims=True)
    jmax = jnp.max(jnp.where(from_block, col_id, -1.0), axis=1, keepdims=True)
    picked = jnp.where(row_id % 2 == 0, jmin, jmax)
    at_pos = (picked == col_id).astype(F32)
    lives = jnp.broadcast_to(lives_ref[...].astype(F32), (slots, blocks))
    live_of = jnp.sum(
        jnp.where(iota((slots, blocks), 0) // 2 == iota((slots, blocks), 1), lives, 0.0), axis=1, keepdims=True
    )
    slot_there = jnp.sum(at_pos * my_slot, axis=1, keepdims=True)
    alive = (slot_there < live_of).astype(F32)
    at_pos_live = at_pos * alive
    to_pos_ref[...] = at_pos_live.astype(BF16)
    observed = observed_ref[...]
    seen_ref[...] = observed * jnp.sum(at_pos_live, axis=0, keepdims=True)
    lives_row = lives_ref[...].astype(F32)
    my_live = jnp.sum(jnp.where(iota((1, blocks), 1) == me, lives_row, 0.0), axis=1, keepdims=True)
    element = jnp.concatenate([element_ref[0:1], element_ref[1:2]], axis=1).astype(F32)
    element_sent = jnp.sum(send_slot_f * element, axis=1, keepdims=True)
    hit = (element_sent.astype(I32) == iota((slots, LANES), 1)).astype(BF16)
    eh_ref[...] = jnp.concatenate([hit, hit], axis=1)
    live_slot = iota((1, slots), 1).astype(F32) < my_live
    to_slot_ref[...] = jnp.where(live_slot, send_slot_f, 0.0).astype(BF16)
    weight = jnp.where(live_slot, weight_ref[...], 0.0)
    weight = padded(weight, LANES, slots).T
    wp_ref[...] = pick(send_slot_b, weight)
    lane, time = iota((LANES, width), 0) - OBS_LANE, iota((LANES, width), 1)
    comp = time // STEPS
    flipped = comp * STEPS + (STEPS - 1 - (time - comp * STEPS))
    turn_time = (lane == flipped).astype(BF16)
    sent = at_pos.astype(BF16)
    rows_out = [dot(turn_time, part).astype(BF16) for part in split3(observed)]
    across = lambda part: lax.dot_general(sent, part, (((1,), (1,)), ((), ())), preferred_element_type=F32)
    acc_ref[...] = across(rows_out[0]) + (across(rows_out[1]) + across(rows_out[2]))


def plan(me, lives, derivative, coupling, face_lift, rec_element, rec_weight, order, observed):
    width, slots = observed.shape
    axes, fields = coupling.shape[0], coupling.shape[1]
    block = axes * fields * GROUP
    smem = pl.BlockSpec(memory_space=pltpu.SMEM)
    vmem = pl.BlockSpec(memory_space=VMEM)
    return pl.pallas_call(
        plan_kernel,
        in_specs=[smem] + [vmem] * 8,
        out_shape=(
            jax.ShapeDtypeStruct((6 * LANES, 2 * LANES), BF16),
            jax.ShapeDtypeStruct((3 * LANES, 2 * LANES), BF16),
            jax.ShapeDtypeStruct((block, 3 * fields * GROUP), BF16),
            jax.ShapeDtypeStruct((slots, 2 * LANES), BF16),
            jax.ShapeDtypeStruct((slots, LANES), F32),
            jax.ShapeDtypeStruct((slots, LANES), F32),
            jax.ShapeDtypeStruct((slots, slots), BF16),
            jax.ShapeDtypeStruct((slots, slots), BF16),
            jax.ShapeDtypeStruct((width, slots), F32),
        ),
        compiler_params=pltpu.CompilerParams(vmem_limit_bytes=16 << 20),
        cost_estimate=pl.CostEstimate(flops=4_000_000_000, bytes_accessed=2_000_000, transcendentals=0),
        name="plan",
    )(
        me,
        lives,
        derivative,
        coupling,
        face_lift,
        rec_element,
        rec_weight,
        order,
        observed,
    )


class Stepper:
    def __init__(self, fields, load, store, factor, metric, wt_ref, wl_ref, ck_ref, t_ref, h_ref, lt_ref, lu_ref):
        self.fields, self.load, self.store, self.factor, self.metric = fields, load, store, factor, metric
        self.wt_ref, self.wl_ref, self.ck_ref = wt_ref, wl_ref, ck_ref
        self.t_ref, self.h_ref, self.lt_ref, self.lu_ref = t_ref, h_ref, lt_ref, lu_ref

    def split(self, item):
        halves = ([], [])
        for f in range(self.fields):
            x = jnp.concatenate([self.load(item.t, f, g) for g in item.groups], axis=0)
            hi, lo = split2(x)
            rows = slice(f * PAIR_ROWS, (f + 1) * PAIR_ROWS)
            self.lu_ref[item.slot, rows, :LANES] = hi
            self.lu_ref[item.slot, rows, LANES:] = lo
            hi32 = hi.astype(F32)
            lo32 = x - hi32
            for side in range(2):
                part = slice(side * GROUP, (side + 1) * GROUP)
                halves[side].append((hi32[part], lo32[part]))
        return halves

    def couple(self, item):
        columns = []
        for side in self.split(item):
            his, los = [p[0] for p in side], [p[1] for p in side]
            columns.append(jnp.concatenate(his + los + his, axis=0).astype(BF16))
        if item.lift_only:
            return
        v = dot(self.ck_ref[...], jnp.concatenate(columns, axis=1))
        for k in range(AXES):
            scale = [self.metric(k, g) for g in item.groups]
            parts = []
            for f in range(self.fields):
                base = (k * self.fields + f) * GROUP
                for side in range(2):
                    parts.append(v[base : base + GROUP, side * LANES : (side + 1) * LANES] * scale[side])
            for lane, part in zip(((0, 4), (1, 5), (2, 3))[k], split2(jnp.concatenate(parts, axis=0))):
                self.lt_ref[item.slot, :, lane * LANES : (lane + 1) * LANES] = part

    def apply(self, item):
        lu = self.lu_ref.at[item.slot]
        if not item.lift_only:
            both = dot(self.lt_ref[item.slot], self.wt_ref[...])
            both = both[:, :LANES] + both[:, LANES:]
        lifted = dot(lu[...], self.wl_ref[: 2 * LANES, :]) + dot(lu[:, :LANES], self.wl_ref[2 * LANES :, :])
        for f in range(self.fields):
            for side, g in enumerate(item.groups):
                rows = slice(f * PAIR_ROWS + side * GROUP, f * PAIR_ROWS + (side + 1) * GROUP)
                if not item.lift_only:
                    self.t_ref[f, g * GROUP : (g + 1) * GROUP, :] = both[rows]
                for face in range(2):
                    at = (g + 1) * GROUP
                    self.h_ref[face, f, at : at + GROUP, :] = lifted[rows, face * LANES : (face + 1) * LANES]

    def update(self, t, g):
        at = (g + 1) * GROUP
        here, before, after = slice(at, at + GROUP), slice(at - 1, at - 1 + GROUP), slice(at + 1, at + 1 + GROUP)
        for f in range(self.fields):
            low, high = self.h_ref.at[0, f], self.h_ref.at[1, f]
            lift = (low[before, :] - low[here, :]) + (high[after, :] - high[here, :])
            rate = self.t_ref[f, g * GROUP : (g + 1) * GROUP, :] + lift
            self.store(t, f, g, self.load(t, f, g) + self.factor(g) * rate)

    def run(self, items, ready, after=lambda index: None):
        ready = set(ready)
        product, lifted, done = set(), set(), set()
        wanted = {}
        for item in items:
            for g in item.groups:
                wanted.setdefault(item.t, {})[g] = item
        coupled = 0

        def couple_next(limit):
            nonlocal coupled
            while coupled < limit and all((items[coupled].t, g) in ready for g in items[coupled].groups):
                self.couple(items[coupled])
                coupled += 1

        for index, item in enumerate(items):
            couple_next(min(index + 2, len(items)))
            assert coupled > index
            self.apply(item)
            for g in item.groups:
                lifted.add((item.t, g))
                if not item.lift_only:
                    product.add((item.t, g))
            for t, groups in wanted.items():
                for g in groups:
                    if (t, g) in done or (t, g) not in product:
                        continue
                    if all(n not in groups or (t, n) in lifted for n in (g - 1, g + 1)):
                        self.update(t, g)
                        done.add((t, g))
                        ready.add((t + 1, g))
            after(index)


class Item:
    def __init__(self, t, slot, groups, lift_only=False):
        self.t, self.slot, self.groups, self.lift_only = t, slot, groups, lift_only


def own_pair(t, j):
    first = HALO // GROUP + 2 * j
    return Item(t, j, (first, first + 1))


def early_kernel(own_ref, wt_ref, wl_ref, ck_ref, *refs):
    past = refs[:EARLY]
    t_ref, h_ref, lt_ref, lu_ref = refs[EARLY:]
    planes, elems, _ = own_ref.shape
    fields = planes - AXES
    shift = HALO // GROUP
    rows = lambda g: slice((g - shift) * GROUP, (g - shift + 1) * GROUP)

    def load(t, f, g):
        return own_ref[f, rows(g), :] if t == 0 else past[t - 1][f, rows(g), :]

    def store(t, f, g, value):
        past[t][f, rows(g), :] = value

    pad = slice(HALO, HALO + GROUP), slice(elems + HALO + GROUP, elems + HALO + 2 * GROUP)
    for rim in pad:
        h_ref[:, :, rim, :] = jnp.zeros((2, fields, GROUP, LANES), F32)
    stepper = Stepper(
        fields, load, store, lambda g: DT, lambda k, g: own_ref[fields + k, rows(g), :],
        wt_ref, wl_ref, ck_ref, t_ref, h_ref, lt_ref, lu_ref,
    )
    pairs = elems // PAIR_ROWS
    order = sorted(range(pairs), key=lambda j: abs(2 * j + 1 - pairs))
    items = [own_pair(t, j) for t in range(EARLY) for j in order]
    stepper.run(items, {(0, g) for item in items for g in item.groups})


def scratch(fields, elems):
    rows = elems + 2 * HALO
    tile = fields * PAIR_ROWS
    slots = rows // PAIR_ROWS + 1
    return [
        VMEM((fields, rows, LANES), F32),
        VMEM((2, fields, rows + 2 * GROUP, LANES), F32),
        VMEM((slots, tile, 6 * LANES), BF16),
        VMEM((slots, tile, 2 * LANES), BF16),
    ]


def early(own, wt, wl, ck):
    planes, elems, _ = own.shape
    fields = planes - AXES
    return pl.pallas_call(
        early_kernel,
        out_shape=tuple(jax.ShapeDtypeStruct((fields, elems, LANES), F32) for _ in range(EARLY)),
        scratch_shapes=scratch(fields, elems),
        compiler_params=pltpu.CompilerParams(vmem_limit_bytes=32 << 20),
        cost_estimate=pl.CostEstimate(flops=5_000_000_000, bytes_accessed=4_000_000, transcendentals=0),
        name="early",
    )(own, wt, wl, ck)


def march_kernel(me_ref, own_ref, near_ref, far_ref, *refs, last_block):
    past = (own_ref,) + refs[:EARLY]
    wt_ref, wl_ref, ck_ref, eh_ref, wp_ref, acc0_ref, send_ref, rev_ref, edge_ref, u_ref, m_ref = refs[EARLY : EARLY + 11]
    t_ref, h_ref, lt_ref, lu_ref = refs[EARLY + 11 :]
    planes, elems, _ = own_ref.shape
    fields = planes - AXES
    slots = eh_ref.shape[0]
    shift = HALO // GROUP
    groups = elems // GROUP + 2 * shift
    me = me_ref[0]
    dt_low = jnp.where(me == 0, 0.0, DT).astype(F32)
    dt_high = jnp.where(me == last_block, 0.0, DT).astype(F32)
    rim = list(range(shift + 1)) + list(range(groups - shift - 1, groups))
    own_rows = lambda g: slice((g - shift) * GROUP, (g - shift + 1) * GROUP)
    rim_rows = lambda g: slice(rim.index(g) * GROUP, (rim.index(g) + 1) * GROUP)
    all_rows = lambda g: slice(g * GROUP, (g + 1) * GROUP)

    odd = me % 2 == 1
    low_edge = lambda edge: jnp.where(odd, near_ref[edge], far_ref[edge])
    high_edge = lambda edge: jnp.where(odd, far_ref[edge], near_ref[edge])
    spare = jnp.zeros((HALO - STEPS, LANES), F32)
    low_rim, high_rim = slice(0, HALO), slice((shift + 2) * GROUP, (2 * shift + 2) * GROUP)
    for f in range(fields):
        edge = slice(f * STEPS, (f + 1) * STEPS)
        edge_ref[0, f, low_rim, :] = jnp.concatenate([spare, jnp.where(me > 0, low_edge(edge), 0.0)], axis=0)
        edge_ref[0, f, high_rim, :] = jnp.concatenate([jnp.where(me < last_block, high_edge(edge), 0.0), spare], axis=0)
    edge = slice(fields * STEPS, (fields + 1) * STEPS)
    low_factors, high_factors = low_edge(edge), high_edge(edge)
    for k in range(AXES):
        lane = k * (LANES // AXES)
        spread = lambda x: jnp.broadcast_to(x[:, lane : lane + 1], (STEPS, LANES))
        m_ref[k, :HALO, :] = jnp.concatenate([spare, spread(low_factors)], axis=0)
        m_ref[k, HALO:, :] = jnp.concatenate([spread(high_factors), spare], axis=0)
    h_ref[:, :, :GROUP, :] = jnp.zeros((2, fields, GROUP, LANES), F32)
    h_ref[:, :, (groups + 1) * GROUP :, :] = jnp.zeros((2, fields, GROUP, LANES), F32)
    send_ref[...] = acc0_ref[...]
    rev_ref[...] = jnp.zeros(rev_ref.shape, F32)

    def load(t, f, g):
        if t > EARLY:
            return u_ref[t % 2, f, all_rows(g), :]
        if g in rim and not (t == 0 and shift <= g < groups - shift):
            return edge_ref[t, f, rim_rows(g), :]
        return past[t][f, own_rows(g), :]

    def store(t, f, g, value):
        if t >= EARLY:
            u_ref[(t + 1) % 2, f, all_rows(g), :] = value
            return
        row = iota((GROUP, LANES), 0)
        if g == shift:
            value = jnp.where(row <= t, value, past[t + 1][f, own_rows(g), :])
        if g == groups - shift - 1:
            value = jnp.where(row >= GROUP - 1 - t, value, past[t + 1][f, own_rows(g), :])
        edge_ref[t + 1, f, rim_rows(g), :] = value

    def metric(k, g):
        if g < shift:
            return m_ref[k, g * GROUP : (g + 1) * GROUP, :]
        if g >= groups - shift:
            at = HALO + (g - groups + shift) * GROUP
            return m_ref[k, at : at + GROUP, :]
        return own_ref[fields + k, own_rows(g), :]

    def factor(g):
        return dt_low if g < shift else (dt_high if g >= groups - shift else DT)

    def sample(t):
        field = lambda f: jnp.concatenate([load(t + 1, f, g) for g in range(shift, groups - shift)], axis=0)
        columns = []
        for c in range(COMPS):
            x = field(c) if c < 3 else (field(3) + field(4) + field(5)) / 3.0
            columns.append(jnp.concatenate(split2(x), axis=0))
        lane = iota((slots, LANES), 1)
        send = send_ref[...]
        rev = rev_ref[...]
        for c in range(0, COMPS, 2):
            found = dot(eh_ref[...], jnp.concatenate(columns[c : c + 2], axis=1))
            for i in range(2):
                value = jnp.sum(found[:, i * LANES : (i + 1) * LANES] * wp_ref[...], axis=1, keepdims=True)
                send = jnp.where(lane == (c + i) * STEPS + t, value, send)
                rev = jnp.where(lane == OBS_LANE + (c + i) * STEPS + (STEPS - 1) - t, value, rev)
        send_ref[...] = send
        rev_ref[...] = rev

    pairs = elems // PAIR_ROWS
    order = sorted(range(pairs), key=lambda j: abs(2 * j + 1 - pairs))
    inner, outer = order[:-2], order[-2:]
    halo_pair = lambda t, ring, lift_only=False: Item(t, pairs + ring, (shift - 1 - ring, groups - shift + ring), lift_only)
    first_pair = lambda t: Item(t, pairs + shift, (shift, groups - shift - 1))
    items, samples = [], {}
    fill = -(-len(inner) // EARLY)
    for t in range(EARLY):
        items += [first_pair(t)] + [halo_pair(t, ring) for ring in range(shift)]
        items += [own_pair(EARLY, j) for j in inner[t * fill : (t + 1) * fill]]
        if t >= 1:
            samples[len(items) - 1] = t - 1
    for t in range(EARLY, STEPS):
        items += [own_pair(t, j) for j in (outer if t == EARLY else order)]
        if t > EARLY:
            samples[len(items) - len(order) + 3] = t - 1
        for ring in range(shift):
            if ring * GROUP < STEPS - t:
                items.append(halo_pair(t, ring, lift_only=ring * GROUP >= STEPS - 1 - t))
        if t == EARLY:
            samples[len(items) - 2] = EARLY - 1
    ready = {(0, g) for g in rim} | {(EARLY, g) for g in range(groups) if g not in rim}
    stepper = Stepper(
        fields, load, store, factor, metric, wt_ref, wl_ref, ck_ref, t_ref, h_ref, lt_ref, lu_ref
    )
    stepper.run(items, ready, lambda index: sample(samples[index]) if index in samples else None)
    sample(STEPS - 1)


def march(me, own, near, far, past, operators, last_block):
    eh = operators[3]
    planes, elems, _ = own.shape
    fields = planes - AXES
    slots = eh.shape[0]
    smem = pl.BlockSpec(memory_space=pltpu.SMEM)
    vmem = pl.BlockSpec(memory_space=VMEM)
    return pl.pallas_call(
        functools.partial(march_kernel, last_block=last_block),
        in_specs=[smem] + [vmem] * (3 + EARLY + len(operators)),
        out_shape=(
            jax.ShapeDtypeStruct((slots, LANES), F32),
            jax.ShapeDtypeStruct((slots, LANES), F32),
        ),
        scratch_shapes=[
            VMEM((EARLY + 1, fields, 2 * (HALO + GROUP), LANES), F32),
            VMEM((2, fields, elems + 2 * HALO, LANES), F32),
            VMEM((AXES, 2 * HALO, LANES), F32),
        ]
        + scratch(fields, elems),
        compiler_params=pltpu.CompilerParams(vmem_limit_bytes=40 << 20),
        cost_estimate=pl.CostEstimate(flops=20_000_000_000, bytes_accessed=4_000_000, transcendentals=0),
        name="march",
    )(me, own, near, far, *past, *operators)


def finish_kernel(
    got_ref, rev_ref, to_slot_ref, to_pos_ref, seen_ref, res_hbm, mis_hbm, adj_hbm, res_ref, mis_ref, adj_ref, sems
):
    width, _ = seen_ref.shape
    got = got_ref[...]
    lane = iota(got.shape, 1)
    turned = jnp.where(lane < OBS_LANE, got, rev_ref[...] - got).T

    def place(rows, onehot):
        found = dot(jnp.concatenate(split3(rows), axis=0), onehot)
        return found[:width] + (found[width : 2 * width] + found[2 * width :])

    residual = place(turned[:width], to_pos_ref[...]) - seen_ref[...]
    res_ref[...] = residual
    first = pltpu.make_async_copy(res_ref, res_hbm, sems.at[0])
    first.start()
    mis_ref[...] = 0.5 * jnp.sum(residual * residual, axis=0, keepdims=True)
    second = pltpu.make_async_copy(mis_ref, mis_hbm, sems.at[1])
    second.start()
    adj_ref[...] = place(turned[OBS_LANE : OBS_LANE + width], to_slot_ref[...])
    third = pltpu.make_async_copy(adj_ref, adj_hbm, sems.at[2])
    third.start()
    first.wait()
    second.wait()
    third.wait()


def finish(got, rev, to_slot, to_pos, seen):
    width, slots = seen.shape
    vmem = pl.BlockSpec(memory_space=VMEM)
    hbm = pl.BlockSpec(memory_space=pltpu.HBM)
    shapes = ((width, slots), (1, slots), (width, slots))
    return pl.pallas_call(
        finish_kernel,
        in_specs=[vmem] * 5,
        out_specs=(hbm, hbm, hbm),
        out_shape=tuple(jax.ShapeDtypeStruct(shape, F32) for shape in shapes),
        scratch_shapes=[VMEM(shape, F32) for shape in shapes] + [pltpu.SemaphoreType.DMA((3,))],
        compiler_params=pltpu.CompilerParams(vmem_limit_bytes=8 << 20),
        name="finish",
    )(got, rev, to_slot, to_pos, seen)


def shards(
    initial,
    derivative,
    coupling,
    face_lift,
    metric,
    rec_element,
    rec_weight,
    live_counts,
    shot_order,
    observed,
):
    blocks = lax.axis_size(MX)
    slots = rec_element.shape[0]
    me = lax.axis_index(MX).astype(I32).reshape(1)
    order, element, lives = (x.reshape(-1, LANES) for x in (shot_order, rec_element, live_counts))
    staged = (derivative, rec_weight, order, element, lives, observed.T)
    own, near, far, derivative, rec_weight, order, element, lives, observed = turn(me, initial, metric, staged)
    pairs = [(i, min(i + 1, blocks - 1) if i % 2 else max(i - 1, 0)) for i in range(blocks)]
    far = lax.ppermute(far, MX, pairs)
    near = lax.ppermute(near, MX, [(i, i ^ 1) for i in range(blocks)])
    wt, wl, ck, eh, wp, acc0, to_slot, to_pos, seen = plan(
        me, lives, derivative, coupling, face_lift, element, rec_weight, order, observed
    )
    past = early(own, wt, wl, ck)
    send, rev = march(me, own, near, far, past, (wt, wl, ck, eh, wp, acc0), blocks - 1)
    got = lax.all_to_all(send.reshape(blocks, 2, LANES), MX, split_axis=0, concat_axis=0, tiled=True)
    residual, misfit, adjoint = finish(got.reshape(slots, LANES), rev, to_slot, to_pos, seen)
    return (residual.T, misfit.reshape(slots), adjoint.T)


def solution(mesh):
    split = Mesh(
        mesh.devices.reshape(mesh.shape["shots"], 8, 8, 2), ("shots", "mx_0", "mx_1", "mx_2")
    )
    in_specs = (
        P("shots", None, MX),
        P(),
        P(),
        P(),
        P(None, MX),
        P(MX),
        P(None, MX),
        P(),
        P(),
        P(SHOTS_MX, None),
    )
    out_specs = (P(SHOTS_MX, None), P(SHOTS_MX), P(SHOTS_MX, None))
    return jax.shard_map(
        shards, mesh=split, in_specs=in_specs, out_specs=out_specs, check_vma=False
    )
```

time: 72.5 us -> 63.9 us (0.88)
  local copies, waits for them, and re-layouts: 4.14 us -> 0.02 us
  Pallas kernels: 25.1 us -> 21.8 us
  starting transfers between devices: 23.8 us -> 22.5 us
    pallas_call x1, Pallas kernels: 21.8 us -> 14.5 us  [march(): pl.pallas_call(functools.partial(march_kernel, last_block=last_block), in...]
    unnamed x25 -> x6, local copies, waits for them, and re-layouts: 4.14 us -> 0.02 us
    pallas_call x3 -> x4, Pallas kernels: 3.34 us -> 7.3 us  [the longest x1 3.83 us: early(): pl.pallas_call(early_kernel, out_shape=tuple((jax.ShapeDtypeStruct((field...]
    ppermute x2, starting transfers between devices: 23.8 us -> 22.5 us  [the longest x1 20.5 us: shards(): near = lax.ppermute(near, MX, [(i, i ^ 1) for i in range(blocks)])]
  transfers between devices with their start and end apart: 2 -> 2, of which waited for: 0 -> 0; matrix products, arithmetic and copies ran while one was open for 0% -> 0% of each run, Pallas kernels for 2% -> 8%
where the time goes in v3:
time: 63.9 us; the launch traced here: 63.8 us
  starting transfers between devices  22.5 us (35%)
  Pallas kernels  21.8 us (34%)
  blocking collectives  18.5 us (29%)
  between operations  0.9 us (1%)
    ppermute x1, starting transfers between devices, shards(): near = lax.ppermute(near, MX, [(i, i ^ 1) for i in range(blocks)])  20.5 us
    all_to_all x1, blocking collectives, shards(): lax.all_to_all(send.reshape(blocks, 2, LANES), MX, split_axis=0, concat_a...  18.5 us
    pallas_call x1, Pallas kernels, march(): pl.pallas_call(functools.partial(march_kernel, last_block=last_block), in...  14.5 us
    pallas_call x1, Pallas kernels, early(): pl.pallas_call(early_kernel, out_shape=tuple((jax.ShapeDtypeStruct((field...  3.83 us
    ppermute x1, starting transfers between devices, shards(): far = lax.ppermute(far, MX, pairs)  1.94 us
    pallas_call x1, Pallas kernels, turn(): pl.pallas_call(turn_kernel, in_specs=[pl.BlockSpec(memory_space=pltpu.SME...  1.48 us
  transfers between devices with their start and end apart: 2, of which 0 were waited for; matrix products, arithmetic and copies ran while one was open for 0% of the time, Pallas kernels for 8%

profile of v3, /device:TPU:513, one launch (start us, length us, event | category | flops | bytes accessed | tf_op | source)
XLA Modules:
  0.0 63.8 jit_solution(5690544259068307669)
XLA Ops:
  0.6 0.0 copy-start.1
  0.7 0.0 copy-start
  0.7 1.5 %turn.1 = (f32[12,128,128]{2,1,0:T(8,128)S(1)}, f32[120,128]{1,0:T(8,128)S(1)}, f32[120,128]{1,0:T(8,128)S(1)}, f32[3,125,125]{2,1,0:T(8,128)S(1)}, f32[125,256]...) custom-call(s32[1]{0:T(128)} %bitcast.me_ref, ...), custom_call_target="tpu_custom_call" | custom-call | tf_op jit(solution)/shard_map/turn/pallas_call | solution.py:102
  2.2 20.5 %collective-permute-start = (f32[120,128]{1,0:T(8,128)S(1)}, f32[120,128]{1,0:T(8,128)S(1)}, u32[]{:S(2)}, u32[]{:S(2)}) collective-permute-start(f32[120,128]{1,0:T(8,128)S(1)} %get-tuple-element.30), channel_id=1, source_target_pairs={{0,1},{1,0},{2,3},{3,2},{4,5},{5,4},{6,7},{7,6},{8,9},{9,8},{10,11... | collective-permute-start | bytes 184328 | tf_op jit(solution)/shard_map/ppermute | solution.py:628
  22.7 1.9 %collective-permute-start.1 = (f32[120,128]{1,0:T(8,128)S(1)}, f32[120,128]{1,0:T(8,128)S(1)}, u32[]{:S(2)}, u32[]{:S(2)}) collective-permute-start(f32[120,128]{1,0:T(8,128)S(1)} %get-tuple-element.31), channel_id=1, source_target_pairs={{0,0},{1,2},{2,1},{3,4},{4,3},{5,6},{6,5},{7,8},{8,7},{9,10},{10,9... | collective-permute-start | bytes 184328 | tf_op jit(solution)/shard_map/ppermute | solution.py:627
  24.6 0.0 copy-done.1
  24.7 0.0 copy-done
  24.7 1.1 %plan.1 = (bf16[768,256]{1,0:T(8,128)(2,1)S(1)}, bf16[384,256]{1,0:T(8,128)(2,1)S(1)}, bf16[216,216]{1,0:T(8,128)(2,1)S(1)}, bf16[256,256]{1,0:T(8,128)(2,1)S(1)...) custom-call(s32[1]{0:T(128)} %bitcast.me_ref, ...), custom_call_target="tpu_custom_call" | custom-call | flops 4000000000 | bytes 2000000 | tf_op jit(solution)/shard_map/plan/pallas_call | solution.py:236
  25.8 3.8 %early.1 = (f32[9,128,128]{2,1,0:T(8,128)S(1)}, f32[9,128,128]{2,1,0:T(8,128)S(1)}, f32[9,128,128]{2,1,0:T(8,128)S(1)}) custom-call(f32[12,128,128]{2,1,0:T(8,128)S(1)} %get-tuple-element.29.own_ref, bf16[768,256]{1,0:T(8,128)(2,1)S(1)} %get-tuple-element.38.wt_ref.refs_3_, bf16[384,256]{1,0:T(8,128)(2,1)S(1)} %get-tuple-element.39.wl_ref.refs_4_, ...), custom_call_target="tpu_custom_call" | custom-call | flops 5000000000 | bytes 4000000 | tf_op jit(solution)/shard_map/early/pallas_call | solution.py:415
  29.6 0.0 collective-permute-done.near_ref
  29.6 0.0 collective-permute-done.1.far_ref
  29.6 14.5 %march.1 = (f32[256,128]{1,0:T(8,128)S(1)}, f32[256,128]{1,0:T(8,128)S(1)}) custom-call(s32[1]{0:T(128)} %bitcast.me_ref, f32[12,128,128]{2,1,0:T(8,128)S(1)} %get-tuple-element.29.own_ref, f32[120,128]{1,0:T(8,128)S(1)} %collective-permute-done.near_ref, f32[120,128]{1,0:T(8,128)S(1)} %collective-permute-done.1.far_ref, ...), custom_call_target="tpu_custom_call" | custom-call | flops 20000000000 | bytes 4000000 | tf_op jit(solution)/shard_map/march/pallas_call | solution.py:546
  44.2 18.5 %all_to_all.5 = f32[128,2,128]{2,1,0:T(2,128)S(1)} all-to-all(f32[128,2,128]{2,1,0:T(2,128)S(1)} %bitcast.11), channel_id=1, replica_groups=mesh['shots'=2,'mx_0'=8,'mx_1'=8,'mx_2'=2] {'mx_0','mx_1','mx_2'}, dimensions={0} | all-to-all | bytes 262144 | tf_op jit(solution)/shard_map/all_to_all | solution.py:634
  62.7 0.9 %finish.1 = (f32[48,256]{1,0:T(8,128)}, f32[1,256]{1,0:T(1,128)}, f32[48,256]{1,0:T(8,128)}) custom-call(f32[256,128]{1,0:T(8,128)S(1)} %bitcast.10, f32[256,128]{1,0:T(8,128)S(1)} %get-tuple-element.48.rev_ref, bf16[256,256]{1,0:T(8,128)(2,1)S(1)} %get-tuple-element.49.to_slot_ref, bf16[256,256]{1,0:T(8,128)(2,1)S(1)} %get-tuple-element.50.to_pos_ref, ...), custom_call_target="tpu_custom_call" | custom-call | tf_op jit(solution)/shard_map/finish/pallas_call | solution.py:597
  (2 shorter events, 0.0 us)
Async XLA Ops:
  0.6 24.0 %copy-start.1 = (f32[3,9,9]{2,0,1:T(4,128)S(1)}, f32[3,9,9]{2,0,1:T(4,128)}, u32[]{:S(2)}) copy-start(f32[3,9,9]{2,0,1:T(4,128)} %param.12) | copy-start | bytes 2920
  0.7 24.0 %copy-start = (f32[2,125,125]{2,0,1:T(2,128)S(1)}, f32[2,125,125]{2,0,1:T(2,128)}, u32[]{:S(2)}) copy-start(f32[2,125,125]{2,0,1:T(2,128)} %param.13) | copy-start | bytes 375004
  2.2 27.5 %collective-permute-start = (f32[120,128]{1,0:T(8,128)S(1)}, f32[120,128]{1,0:T(8,128)S(1)}, u32[]{:S(2)}, u32[]{:S(2)}) collective-permute-start(f32[120,128]{1,0:T(8,128)S(1)} %get-tuple-element.30), channel_id=1, source_target_pairs={{0,1},{1,0},{2,3},{3,2},{4,5},{5,4},{6,7},{7,6},{8,9},{9,8},{10,11... | collective-permute-start | bytes 184328 | tf_op jit(solution)/shard_map/ppermute | solution.py:628
  22.7 6.9 %collective-permute-start.1 = (f32[120,128]{1,0:T(8,128)S(1)}, f32[120,128]{1,0:T(8,128)S(1)}, u32[]{:S(2)}, u32[]{:S(2)}) collective-permute-start(f32[120,128]{1,0:T(8,128)S(1)} %get-tuple-element.31), channel_id=1, source_target_pairs={{0,0},{1,2},{2,1},{3,4},{4,3},{5,6},{6,5},{7,8},{8,7},{9,10},{10,9... | collective-permute-start | bytes 184328 | tf_op jit(solution)/shard_map/ppermute | solution.py:627

commit v4 on v3

--- a/solution.py
+++ b/solution.py
@@ -116,36 +116,9 @@
     )(me, *(pltpu.with_memory_space_constraint(x, pltpu.HBM) for x in (initial, metric, *staged)))
 
 
-def plan_kernel(
-    me_ref,
-    lives_ref,
-    derivative_ref,
-    coupling_ref,
-    lift_ref,
-    element_ref,
-    weight_ref,
-    order_ref,
-    observed_ref,
-    wt_ref,
-    wl_ref,
-    ck_ref,
-    eh_ref,
-    wp_ref,
-    acc_ref,
-    to_slot_ref,
-    to_pos_ref,
-    seen_ref,
-):
-    width, slots = observed_ref.shape
-    blocks = slots // 2
-    me = me_ref[0]
-    axes = derivative_ref.shape[0]
+def operators_kernel(derivative_ref, coupling_ref, lift_ref, wt_ref, wl_ref, ck_ref):
     fields = coupling_ref.shape[1]
-    dh, dl = [], []
-    for k in range(axes):
-        hi, lo = split2(padded(derivative_ref[k], LANES, LANES).T)
-        dh.append(hi)
-        dl.append(lo)
+    dh, dl = zip(*(split2(padded(derivative_ref[k], LANES, LANES).T) for k in range(AXES)))
     zero = jnp.zeros((LANES, LANES), BF16)
     for row, (left, right) in enumerate(
         [(dh[0], dl[0]), (dh[1], dl[1]), (dh[2], dl[2]), (dh[2], zero), (dh[0], zero), (dh[1], zero)]
@@ -155,112 +128,123 @@
     l1h, l1l = split2(padded(lift_ref[1], LANES, LANES).T)
     for row, (left, right) in enumerate([(l0h, l1h), (l0h, l1h), (l0l, l1l)]):
         wl_ref[row * LANES : (row + 1) * LANES, :] = jnp.concatenate([left, right], axis=1)
-    rows, cols = axes * fields * GROUP, fields * GROUP
-    spread_rows = (iota((rows, axes * fields), 0) // GROUP == iota((rows, axes * fields), 1)).astype(BF16)
+    rows, cols = AXES * fields * GROUP, fields * GROUP
+    spread_rows = (iota((rows, AXES * fields), 0) // GROUP == iota((rows, AXES * fields), 1)).astype(BF16)
     spread_cols = (iota((fields, cols), 0) == iota((fields, cols), 1) // GROUP).astype(BF16)
-    stacked = jnp.concatenate([coupling_ref[k] for k in range(axes)], axis=0)
-    by_row = pick(spread_rows, stacked)
-    by_hi, by_mid, by_lo = split3(by_row)
-    full = dot(by_hi, spread_cols) + (dot(by_mid, spread_cols) + dot(by_lo, spread_cols))
-    diagonal = iota((rows, cols), 0) % GROUP == iota((rows, cols), 1) % GROUP
-    full = jnp.where(diagonal, full, 0.0)
+    by_row = pick(spread_rows, jnp.concatenate([coupling_ref[k] for k in range(AXES)], axis=0))
+    hi, mid, lo = split3(by_row)
+    full = dot(hi, spread_cols) + (dot(mid, spread_cols) + dot(lo, spread_cols))
+    full = jnp.where(iota((rows, cols), 0) % GROUP == iota((rows, cols), 1) % GROUP, full, 0.0)
     full_hi = full.astype(BF16).astype(F32)
     ck_ref[...] = jnp.concatenate([full_hi, full_hi, full - full_hi], axis=1).astype(BF16)
-    order = order_ref[...]
-    half = iota((slots, LANES), 0) % 2
-    position = half * LANES + iota((slots, LANES), 1)
-    slot_of = order % slots
-    key = (position * slots + slot_of).astype(F32)
-    mine = (order // slots) == me
-    big = float(slots * slots)
-    first = jnp.min(jnp.where(mine, key, big), axis=1, keepdims=True)
-    last = jnp.max(jnp.where(mine, key, -1.0), axis=1, keepdims=True)
-    first = jnp.broadcast_to(first, (slots, LANES))
-    last = jnp.broadcast_to(last, (slots, LANES))
-    up = lambda x: pltpu.roll(x, slots - 1, 0)
-    down = lambda x: pltpu.roll(x, 1, 0)
-    chosen = jnp.where(half == 0, jnp.minimum(first, up(first)), jnp.maximum(last, down(last)))
-    chosen = chosen.astype(I32) % slots
-    chosen = jnp.concatenate([chosen, chosen], axis=1)
-    send_slot = chosen == iota((slots, slots), 1)
-    send_slot_f = send_slot.astype(F32)
-    send_slot_b = send_slot_f.astype(BF16)
-    my_rows = order_ref[pl.ds(2 * me, 2), :]
-    my_row = jnp.concatenate([my_rows[0:1], my_rows[1:2]], axis=1)
-    my_block = my_row // slots
-    my_slot = (my_row % slots).astype(F32)
-    row_id = iota((slots, slots), 0)
-    col_id = iota((slots, slots), 1).astype(F32)
-    from_block = my_block == row_id // 2
-    jmin = jnp.min(jnp.where(from_block, col_id, big), axis=1, keepdims=True)
-    jmax = jnp.max(jnp.where(from_block, col_id, -1.0), axis=1, keepdims=True)
-    picked = jnp.where(row_id % 2 == 0, jmin, jmax)
-    at_pos = (picked == col_id).astype(F32)
-    lives = jnp.broadcast_to(lives_ref[...].astype(F32), (slots, blocks))
-    live_of = jnp.sum(
-        jnp.where(iota((slots, blocks), 0) // 2 == iota((slots, blocks), 1), lives, 0.0), axis=1, keepdims=True
-    )
-    slot_there = jnp.sum(at_pos * my_slot, axis=1, keepdims=True)
-    alive = (slot_there < live_of).astype(F32)
-    at_pos_live = at_pos * alive
-    to_pos_ref[...] = at_pos_live.astype(BF16)
-    observed = observed_ref[...]
-    seen_ref[...] = observed * jnp.sum(at_pos_live, axis=0, keepdims=True)
-    lives_row = lives_ref[...].astype(F32)
-    my_live = jnp.sum(jnp.where(iota((1, blocks), 1) == me, lives_row, 0.0), axis=1, keepdims=True)
-    element = jnp.concatenate([element_ref[0:1], element_ref[1:2]], axis=1).astype(F32)
-    element_sent = jnp.sum(send_slot_f * element, axis=1, keepdims=True)
-    hit = (element_sent.astype(I32) == iota((slots, LANES), 1)).astype(BF16)
-    eh_ref[...] = jnp.concatenate([hit, hit], axis=1)
-    live_slot = iota((1, slots), 1).astype(F32) < my_live
-    to_slot_ref[...] = jnp.where(live_slot, send_slot_f, 0.0).astype(BF16)
-    weight = jnp.where(live_slot, weight_ref[...], 0.0)
-    weight = padded(weight, LANES, slots).T
-    wp_ref[...] = pick(send_slot_b, weight)
-    lane, time = iota((LANES, width), 0) - OBS_LANE, iota((LANES, width), 1)
-    comp = time // STEPS
-    flipped = comp * STEPS + (STEPS - 1 - (time - comp * STEPS))
-    turn_time = (lane == flipped).astype(BF16)
-    sent = at_pos.astype(BF16)
-    rows_out = [dot(turn_time, part).astype(BF16) for part in split3(observed)]
-    across = lambda part: lax.dot_general(sent, part, (((1,), (1,)), ((), ())), preferred_element_type=F32)
-    acc_ref[...] = across(rows_out[0]) + (across(rows_out[1]) + across(rows_out[2]))
-
-
-def plan(me, lives, derivative, coupling, face_lift, rec_element, rec_weight, order, observed):
-    width, slots = observed.shape
-    axes, fields = coupling.shape[0], coupling.shape[1]
-    block = axes * fields * GROUP
-    smem = pl.BlockSpec(memory_space=pltpu.SMEM)
-    vmem = pl.BlockSpec(memory_space=VMEM)
+
+
+def operators(derivative, coupling, face_lift):
+    fields = coupling.shape[1]
+    block = AXES * fields * GROUP
     return pl.pallas_call(
-        plan_kernel,
-        in_specs=[smem] + [vmem] * 8,
+        operators_kernel,
         out_shape=(
             jax.ShapeDtypeStruct((6 * LANES, 2 * LANES), BF16),
             jax.ShapeDtypeStruct((3 * LANES, 2 * LANES), BF16),
             jax.ShapeDtypeStruct((block, 3 * fields * GROUP), BF16),
-            jax.ShapeDtypeStruct((slots, 2 * LANES), BF16),
-            jax.ShapeDtypeStruct((slots, LANES), F32),
-            jax.ShapeDtypeStruct((slots, LANES), F32),
-            jax.ShapeDtypeStruct((slots, slots), BF16),
-            jax.ShapeDtypeStruct((slots, slots), BF16),
-            jax.ShapeDtypeStruct((width, slots), F32),
         ),
-        compiler_params=pltpu.CompilerParams(vmem_limit_bytes=16 << 20),
-        cost_estimate=pl.CostEstimate(flops=4_000_000_000, bytes_accessed=2_000_000, transcendentals=0),
-        name="plan",
-    )(
-        me,
-        lives,
-        derivative,
-        coupling,
-        face_lift,
-        rec_element,
-        rec_weight,
-        order,
-        observed,
-    )
+        compiler_params=pltpu.CompilerParams(vmem_limit_bytes=8 << 20),
+        cost_estimate=pl.CostEstimate(flops=1_000_000_000, bytes_accessed=1_000_000, transcendentals=0),
+        name="operators",
+    )(derivative, coupling, face_lift)
+
+
+class Order:
+    def __init__(self, me, ins, outs, place_ref):
+        self.me = me
+        self.lives_ref, self.element_ref, self.weight_ref, self.order_ref, self.observed_ref = ins
+        self.eh_ref, self.wp_ref, self.acc_ref, self.to_slot_ref, self.to_pos_ref, self.seen_ref = outs
+        self.place_ref = place_ref
+        self.width, self.slots = self.observed_ref.shape
+        self.chips = self.slots // 4
+        self.big = float(self.slots * self.slots)
+        self.bits = self.slots.bit_length() - 1
+        assert self.slots == 1 << self.bits
+        self.odd = me & 1
+
+    def pieces(self):
+        yield from (functools.partial(self.slot_rows, other) for other in range(2))
+        yield from (functools.partial(self.position_rows, other) for other in range(2))
+        yield from (self.weights, self.observations, self.seen)
+
+    def rows(self, other, which):
+        start = (2 * other + which) * self.chips
+        return slice(start, start + self.chips)
+
+    def across(self, ref):
+        return jnp.concatenate([ref[0:1, :], ref[1:2, :]], axis=1)
+
+    def live_of(self, block):
+        lives = self.lives_ref[...]
+        there = block == iota((block.shape[0], lives.shape[1]), 1)
+        return jnp.sum(jnp.where(there, lives.astype(F32), 0.0), axis=1, keepdims=True)
+
+    def slot_rows(self, other):
+        slots, chips = self.slots, self.chips
+        first, last = None, None
+        for half in range(2):
+            core = [self.order_ref[pl.ds(2 * core + half, chips, stride=4), :] for core in range(2)]
+            order = jnp.where(self.odd == 1 - other, core[1], core[0])
+            key = (((half * LANES + iota(order.shape, 1)) << self.bits) + (order & (slots - 1))).astype(F32)
+            mine = (order >> self.bits) == self.me
+            low, high = jnp.where(mine, key, self.big), jnp.where(mine, key, -1.0)
+            first = low if first is None else jnp.minimum(first, low)
+            last = high if last is None else jnp.maximum(last, high)
+        found = jnp.min(first, axis=1, keepdims=True), jnp.max(last, axis=1, keepdims=True)
+        live_slot = iota((1, slots), 1).astype(F32) < self.live_of(jnp.full((1, 1), self.me, I32))
+        element = self.across(self.element_ref).astype(F32)
+        for which in range(2):
+            rows = self.rows(other, which)
+            hot = (found[which].astype(I32) & (slots - 1)) == iota((chips, slots), 1)
+            self.to_slot_ref[rows, :] = jnp.where(hot & live_slot, 1.0, 0.0).astype(BF16)
+            element_of = jnp.sum(jnp.where(hot, element, 0.0), axis=1, keepdims=True)
+            hit = (element_of.astype(I32) == iota((chips, LANES), 1)).astype(BF16)
+            self.eh_ref[rows, :] = jnp.concatenate([hit, hit], axis=1)
+
+    def position_rows(self, other):
+        slots, shape = self.slots, (self.chips, self.slots)
+        mine = self.order_ref[pl.ds(2 * self.me, 2), :]
+        mine = jnp.concatenate([mine[0:1], mine[1:2]], axis=1)
+        block = 2 * iota((self.chips, 1), 0) + jnp.where(self.odd == 1 - other, 1, 0)
+        col = iota(shape, 1).astype(F32)
+        here = (mine >> self.bits) == block
+        found = (
+            jnp.min(jnp.where(here, col, self.big), axis=1, keepdims=True),
+            jnp.max(jnp.where(here, col, -1.0), axis=1, keepdims=True),
+        )
+        live = self.live_of(block)
+        slot = (mine & (slots - 1)).astype(F32)
+        for which in range(2):
+            rows = self.rows(other, which)
+            hot = found[which] == col
+            self.place_ref[rows, :] = hot.astype(BF16)
+            slot_of = jnp.sum(jnp.where(hot, slot, 0.0), axis=1, keepdims=True)
+            self.to_pos_ref[rows, :] = jnp.where(hot & (slot_of < live), 1.0, 0.0).astype(BF16)
+
+    def weights(self):
+        weight = padded(self.weight_ref[...], LANES, self.slots).T
+        self.wp_ref[...] = pick(self.to_slot_ref[...], weight)
+
+    def observations(self):
+        lane, time = iota((LANES, self.width), 0) - OBS_LANE, iota((LANES, self.width), 1)
+        comp = time // STEPS
+        turned = (lane == comp * STEPS + (STEPS - 1 - (time - comp * STEPS))).astype(BF16)
+        parts = [dot(turned, part).astype(BF16) for part in split3(self.observed_ref[...])]
+        place = self.place_ref[...]
+        out = [
+            lax.dot_general(place, part, (((1,), (1,)), ((), ())), preferred_element_type=F32) for part in parts
+        ]
+        self.acc_ref[...] = out[0] + (out[1] + out[2])
+
+    def seen(self):
+        live = jnp.sum(self.to_pos_ref[...].astype(F32), axis=0, keepdims=True)
+        self.seen_ref[...] = self.observed_ref[...] * live
 
 
 class Stepper:
@@ -370,9 +354,9 @@
     return Item(t, j, (first, first + 1))
 
 
-def early_kernel(own_ref, wt_ref, wl_ref, ck_ref, *refs):
-    past = refs[:EARLY]
-    t_ref, h_ref, lt_ref, lu_ref = refs[EARLY:]
+def early_kernel(me_ref, own_ref, wt_ref, wl_ref, ck_ref, *refs):
+    ins, past, outs = refs[:5], refs[5 : 5 + EARLY], refs[5 + EARLY : 11 + EARLY]
+    t_ref, h_ref, lt_ref, lu_ref, place_ref = refs[11 + EARLY :]
     planes, elems, _ = own_ref.shape
     fields = planes - AXES
     shift = HALO // GROUP
@@ -394,7 +378,11 @@
     pairs = elems // PAIR_ROWS
     order = sorted(range(pairs), key=lambda j: abs(2 * j + 1 - pairs))
     items = [own_pair(t, j) for t in range(EARLY) for j in order]
-    stepper.run(items, {(0, g) for item in items for g in item.groups})
+    pieces = list(Order(me_ref[0], ins, outs, place_ref).pieces())
+    at = {1 + (len(items) - 3) * i // len(pieces): piece for i, piece in enumerate(pieces)}
+    stepper.run(
+        items, {(0, g) for item in items for g in item.groups}, lambda index: at[index]() if index in at else None
+    )
 
 
 def scratch(fields, elems):
@@ -409,23 +397,35 @@
     ]
 
 
-def early(own, wt, wl, ck):
+def early(me, own, operators, ins):
     planes, elems, _ = own.shape
     fields = planes - AXES
+    width, slots = ins[-1].shape
+    smem = pl.BlockSpec(memory_space=pltpu.SMEM)
+    vmem = pl.BlockSpec(memory_space=VMEM)
     return pl.pallas_call(
         early_kernel,
-        out_shape=tuple(jax.ShapeDtypeStruct((fields, elems, LANES), F32) for _ in range(EARLY)),
-        scratch_shapes=scratch(fields, elems),
+        in_specs=[smem] + [vmem] * (1 + len(operators) + len(ins)),
+        out_shape=tuple(jax.ShapeDtypeStruct((fields, elems, LANES), F32) for _ in range(EARLY))
+        + (
+            jax.ShapeDtypeStruct((slots, 2 * LANES), BF16),
+            jax.ShapeDtypeStruct((slots, LANES), F32),
+            jax.ShapeDtypeStruct((slots, LANES), F32),
+            jax.ShapeDtypeStruct((slots, slots), BF16),
+            jax.ShapeDtypeStruct((slots, slots), BF16),
+            jax.ShapeDtypeStruct((width, slots), F32),
+        ),
+        scratch_shapes=scratch(fields, elems) + [VMEM((slots, slots), BF16)],
         compiler_params=pltpu.CompilerParams(vmem_limit_bytes=32 << 20),
         cost_estimate=pl.CostEstimate(flops=5_000_000_000, bytes_accessed=4_000_000, transcendentals=0),
         name="early",
-    )(own, wt, wl, ck)
+    )(me, own, *operators, *ins)
 
 
 def march_kernel(me_ref, own_ref, near_ref, far_ref, *refs, last_block):
     past = (own_ref,) + refs[:EARLY]
-    wt_ref, wl_ref, ck_ref, eh_ref, wp_ref, acc0_ref, send_ref, rev_ref, edge_ref, u_ref, m_ref = refs[EARLY : EARLY + 11]
-    t_ref, h_ref, lt_ref, lu_ref = refs[EARLY + 11 :]
+    wt_ref, wl_ref, ck_ref, eh_ref, wp_ref, acc0_ref, keep_ref, give_ref, rev_ref = refs[EARLY : EARLY + 9]
+    edge_ref, u_ref, m_ref, t_ref, h_ref, lt_ref, lu_ref = refs[EARLY + 9 :]
     planes, elems, _ = own_ref.shape
     fields = planes - AXES
     slots = eh_ref.shape[0]
@@ -457,7 +457,9 @@
         m_ref[k, HALO:, :] = jnp.concatenate([spread(high_factors), spare], axis=0)
     h_ref[:, :, :GROUP, :] = jnp.zeros((2, fields, GROUP, LANES), F32)
     h_ref[:, :, (groups + 1) * GROUP :, :] = jnp.zeros((2, fields, GROUP, LANES), F32)
-    send_ref[...] = acc0_ref[...]
+    half = slots // 2
+    keep_ref[...] = acc0_ref[:half]
+    give_ref[...] = acc0_ref[half:]
     rev_ref[...] = jnp.zeros(rev_ref.shape, F32)
 
     def load(t, f, g):
@@ -496,7 +498,7 @@
             x = field(c) if c < 3 else (field(3) + field(4) + field(5)) / 3.0
             columns.append(jnp.concatenate(split2(x), axis=0))
         lane = iota((slots, LANES), 1)
-        send = send_ref[...]
+        send = jnp.concatenate([keep_ref[...], give_ref[...]], axis=0)
         rev = rev_ref[...]
         for c in range(0, COMPS, 2):
             found = dot(eh_ref[...], jnp.concatenate(columns[c : c + 2], axis=1))
@@ -504,7 +506,8 @@
                 value = jnp.sum(found[:, i * LANES : (i + 1) * LANES] * wp_ref[...], axis=1, keepdims=True)
                 send = jnp.where(lane == (c + i) * STEPS + t, value, send)
                 rev = jnp.where(lane == OBS_LANE + (c + i) * STEPS + (STEPS - 1) - t, value, rev)
-        send_ref[...] = send
+        keep_ref[...] = send[:half]
+        give_ref[...] = send[half:]
         rev_ref[...] = rev
 
     pairs = elems // PAIR_ROWS
@@ -536,8 +539,8 @@
     sample(STEPS - 1)
 
 
-def march(me, own, near, far, past, operators, last_block):
-    eh = operators[3]
+def march(me, own, near, far, past, ops, last_block):
+    eh = ops[3]
     planes, elems, _ = own.shape
     fields = planes - AXES
     slots = eh.shape[0]
@@ -545,9 +548,10 @@
     vmem = pl.BlockSpec(memory_space=VMEM)
     return pl.pallas_call(
         functools.partial(march_kernel, last_block=last_block),
-        in_specs=[smem] + [vmem] * (3 + EARLY + len(operators)),
+        in_specs=[smem] + [vmem] * (3 + EARLY + len(ops)),
         out_shape=(
-            jax.ShapeDtypeStruct((slots, LANES), F32),
+            jax.ShapeDtypeStruct((slots // 2, LANES), F32),
+            jax.ShapeDtypeStruct((slots // 2, LANES), F32),
             jax.ShapeDtypeStruct((slots, LANES), F32),
         ),
         scratch_shapes=[
@@ -559,14 +563,31 @@
         compiler_params=pltpu.CompilerParams(vmem_limit_bytes=40 << 20),
         cost_estimate=pl.CostEstimate(flops=20_000_000_000, bytes_accessed=4_000_000, transcendentals=0),
         name="march",
-    )(me, own, near, far, *past, *operators)
+    )(me, own, near, far, *past, *ops)
+
+
+def pack_kernel(keep_ref, given_ref, out_ref):
+    chips = keep_ref.shape[0] // 2
+    for other, ref in enumerate((keep_ref, given_ref)):
+        for which in range(2):
+            out_ref[pl.ds(2 * other + which, chips, stride=4), :] = ref[which * chips : (which + 1) * chips, :]
+
+
+def pack(keep, given):
+    return pl.pallas_call(
+        pack_kernel,
+        out_shape=jax.ShapeDtypeStruct((2 * keep.shape[0], LANES), F32),
+        compiler_params=pltpu.CompilerParams(vmem_limit_bytes=4 << 20),
+        name="pack",
+    )(keep, given)
 
 
 def finish_kernel(
     got_ref, rev_ref, to_slot_ref, to_pos_ref, seen_ref, res_hbm, mis_hbm, adj_hbm, res_ref, mis_ref, adj_ref, sems
 ):
-    width, _ = seen_ref.shape
-    got = got_ref[...]
+    width, slots = seen_ref.shape
+    chips = slots // 4
+    got = jnp.concatenate([got_ref[pl.ds(i, chips, stride=4), :] for i in range(4)], axis=0)
     lane = iota(got.shape, 1)
     turned = jnp.where(lane < OBS_LANE, got, rev_ref[...] - got).T
 
@@ -626,12 +647,13 @@
     pairs = [(i, min(i + 1, blocks - 1) if i % 2 else max(i - 1, 0)) for i in range(blocks)]
     far = lax.ppermute(far, MX, pairs)
     near = lax.ppermute(near, MX, [(i, i ^ 1) for i in range(blocks)])
-    wt, wl, ck, eh, wp, acc0, to_slot, to_pos, seen = plan(
-        me, lives, derivative, coupling, face_lift, element, rec_weight, order, observed
-    )
-    past = early(own, wt, wl, ck)
-    send, rev = march(me, own, near, far, past, (wt, wl, ck, eh, wp, acc0), blocks - 1)
-    got = lax.all_to_all(send.reshape(blocks, 2, LANES), MX, split_axis=0, concat_axis=0, tiled=True)
+    ops = operators(derivative, coupling, face_lift)
+    outs = early(me, own, ops, (lives, element, rec_weight, order, observed))
+    past, eh, wp, acc0, to_slot, to_pos, seen = (outs[:EARLY],) + tuple(outs[EARLY:])
+    keep, give, rev = march(me, own, near, far, past, (*ops, eh, wp, acc0), blocks - 1)
+    given = lax.ppermute(give, MX, [(i, i ^ 1) for i in range(blocks)])
+    rows = pack(keep, given).reshape(blocks // 2, 4, LANES)
+    got = lax.all_to_all(rows, MX[:2], split_axis=0, concat_axis=0, tiled=True)
     residual, misfit, adjoint = finish(got.reshape(slots, LANES), rev, to_slot, to_pos, seen)
     return (residual.T, misfit.reshape(slots), adjoint.T)
 

time: 63.9 us -> 62.9 us (0.984)
  blocking collectives: 18.5 us -> 15.9 us
  waiting for transfers between devices: 0.01 us -> 1.23 us
    all_to_all x1, blocking collectives: 18.5 us -> 15.9 us  [shards(): got = lax.all_to_all(rows, MX[:2], split_axis=0, concat_axis=0, tiled=True)]
    ppermute x0 -> x1, waiting for transfers between devices: none -> 1.23 us  [shards(): given = lax.ppermute(give, MX, [(i, i ^ 1) for i in range(blocks)])]
    pallas_call x2 -> x3, Pallas kernels: 4.91 us -> 4.82 us  [the longest x1 4.32 us: early(): pl.pallas_call(early_kernel, in_specs=[smem] + [vmem] * (1 + len(operator...]
  transfers between devices with their start and end apart: 2 -> 3, of which waited for: 0 -> 1; matrix products, arithmetic and copies ran while one was open for 0% -> 0% of each run, Pallas kernels for 8% -> 8%
where the time goes in v4:
time: 62.9 us; the launch traced here: 62.7 us
  starting transfers between devices  22.6 us (36%)
  Pallas kernels  22 us (35%)
  blocking collectives  15.9 us (25%)
  waiting for transfers between devices  1.23 us (2%)
  between operations  0.91 us (1%)
    ppermute x1, starting transfers between devices, shards(): near = lax.ppermute(near, MX, [(i, i ^ 1) for i in range(blocks)])  20.5 us
    all_to_all x1, blocking collectives, shards(): got = lax.all_to_all(rows, MX[:2], split_axis=0, concat_axis=0, tiled=True)  15.9 us
    pallas_call x1, Pallas kernels, march(): pl.pallas_call(functools.partial(march_kernel, last_block=last_block), in...  14.8 us
    pallas_call x1, Pallas kernels, early(): pl.pallas_call(early_kernel, in_specs=[smem] + [vmem] * (1 + len(operator...  4.32 us
    ppermute x1, starting transfers between devices, shards(): far = lax.ppermute(far, MX, pairs)  1.94 us
    pallas_call x1, Pallas kernels, turn(): pl.pallas_call(turn_kernel, in_specs=[pl.BlockSpec(memory_space=pltpu.SME...  1.48 us
  transfers between devices with their start and end apart: 3, of which 1 were waited for; matrix products, arithmetic and copies ran while one was open for 0% of the time, Pallas kernels for 8%

profile of v4, /device:TPU:513, one launch (start us, length us, event | category | flops | bytes accessed | tf_op | source)
XLA Modules:
  0.0 62.7 jit_solution(877868917873031536)
XLA Ops:
  0.6 0.0 copy-start.1
  0.7 0.0 copy-start
  0.7 1.5 %turn.1 = (f32[12,128,128]{2,1,0:T(8,128)S(1)}, f32[120,128]{1,0:T(8,128)S(1)}, f32[120,128]{1,0:T(8,128)S(1)}, f32[3,125,125]{2,1,0:T(8,128)S(1)}, f32[125,256]...) custom-call(s32[1]{0:T(128)} %bitcast.me_ref, ...), custom_call_target="tpu_custom_call" | custom-call | tf_op jit(solution)/shard_map/turn/pallas_call | solution.py:102
  2.2 20.5 %collective-permute-start = (f32[120,128]{1,0:T(8,128)S(1)}, f32[120,128]{1,0:T(8,128)S(1)}, u32[]{:S(2)}, u32[]{:S(2)}) collective-permute-start(f32[120,128]{1,0:T(8,128)S(1)} %get-tuple-element.31), channel_id=1, source_target_pairs={{0,1},{1,0},{2,3},{3,2},{4,5},{5,4},{6,7},{7,6},{8,9},{9,8},{10,11... | collective-permute-start | bytes 184328 | tf_op jit(solution)/shard_map/ppermute | solution.py:649
  22.7 1.9 %collective-permute-start.1 = (f32[120,128]{1,0:T(8,128)S(1)}, f32[120,128]{1,0:T(8,128)S(1)}, u32[]{:S(2)}, u32[]{:S(2)}) collective-permute-start(f32[120,128]{1,0:T(8,128)S(1)} %get-tuple-element.32), channel_id=1, source_target_pairs={{0,0},{1,2},{2,1},{3,4},{4,3},{5,6},{6,5},{7,8},{8,7},{9,10},{10,9... | collective-permute-start | bytes 184328 | tf_op jit(solution)/shard_map/ppermute | solution.py:648
  24.6 0.0 copy-done.1
  24.7 0.0 copy-done
  24.7 0.5 operators.1
  25.2 4.3 %early.1 = (f32[9,128,128]{2,1,0:T(8,128)S(1)}, f32[9,128,128]{2,1,0:T(8,128)S(1)}, f32[9,128,128]{2,1,0:T(8,128)S(1)}, bf16[256,256]{1,0:T(8,128)(2,1)S(1)}, f3...) custom-call(s32[1]{0:T(128)} %bitcast.me_ref, ...), custom_call_target="tpu_custom_call" | custom-call | flops 5000000000 | bytes 4000000 | tf_op jit(solution)/shard_map/early/pallas_call | solution.py:406
  29.5 0.0 collective-permute-done.near_ref
  29.5 0.0 collective-permute-done.1.far_ref
  29.5 14.8 %march.1 = (f32[128,128]{1,0:T(8,128)S(1)}, f32[128,128]{1,0:T(8,128)S(1)}, f32[256,128]{1,0:T(8,128)S(1)}) custom-call(s32[1]{0:T(128)} %bitcast.me_ref, f32[12,128,128]{2,1,0:T(8,128)S(1)} %get-tuple-element.30.own_ref, f32[120,128]{1,0:T(8,128)S(1)} %collective-permute-done.near_ref, f32[120,128]{1,0:T(8,128)S(1)} %collective-permute-done.1.far_ref, ...), custom_call_target="tpu_custom_call" | custom-call | flops 20000000000 | bytes 4000000 | tf_op jit(solution)/shard_map/march/pallas_call | solution.py:549
  44.3 0.1 collective-permute-start.2
  44.5 1.2 %collective-permute-done.2.given_ref = f32[128,128]{1,0:T(8,128)S(1)} collective-permute-done((f32[128,128]{1,0:T(8,128)S(1)}, f32[128,128]{1,0:T(8,128)S(1)}, u32[]{:S(2)}, u32[]{:S(2)}) %collective-permute-start.2) | collective-permute-done | bytes 65568 | tf_op jit(solution)/shard_map/ppermute | solution.py:654
  45.7 15.9 %all_to_all.5 = f32[64,4,128]{2,1,0:T(4,128)S(1)} all-to-all(f32[64,4,128]{2,1,0:T(4,128)S(1)} %bitcast.10), channel_id=1, replica_groups=mesh['shots'=2,'mx_0'=8,'mx_1'=8,'mx_2'=2] {'mx_0','mx_1'}, dimensions={0} | all-to-all | bytes 262144 | tf_op jit(solution)/shard_map/all_to_all | solution.py:656
  61.7 0.9 %finish.1 = (f32[48,256]{1,0:T(8,128)}, f32[1,256]{1,0:T(1,128)}, f32[48,256]{1,0:T(8,128)}) custom-call(f32[256,128]{1,0:T(8,128)S(1)} %bitcast.11, f32[256,128]{1,0:T(8,128)S(1)} %get-tuple-element.50.rev_ref, bf16[256,256]{1,0:T(8,128)(2,1)S(1)} %get-tuple-element.51.to_slot_ref, bf16[256,256]{1,0:T(8,128)(2,1)S(1)} %get-tuple-element.52.to_pos_ref, ...), custom_call_target="tpu_custom_call" | custom-call | tf_op jit(solution)/shard_map/finish/pallas_call | solution.py:618
  (3 shorter events, 0.0 us)
Async XLA Ops:
  0.6 24.0 %copy-start.1 = (f32[3,9,9]{2,0,1:T(4,128)S(1)}, f32[3,9,9]{2,0,1:T(4,128)}, u32[]{:S(2)}) copy-start(f32[3,9,9]{2,0,1:T(4,128)} %param.12) | copy-start | bytes 2920
  0.7 24.0 %copy-start = (f32[2,125,125]{2,0,1:T(2,128)S(1)}, f32[2,125,125]{2,0,1:T(2,128)}, u32[]{:S(2)}) copy-start(f32[2,125,125]{2,0,1:T(2,128)} %param.13) | copy-start | bytes 375004
  2.2 27.4 %collective-permute-start = (f32[120,128]{1,0:T(8,128)S(1)}, f32[120,128]{1,0:T(8,128)S(1)}, u32[]{:S(2)}, u32[]{:S(2)}) collective-permute-start(f32[120,128]{1,0:T(8,128)S(1)} %get-tuple-element.31), channel_id=1, source_target_pairs={{0,1},{1,0},{2,3},{3,2},{4,5},{5,4},{6,7},{7,6},{8,9},{9,8},{10,11... | collective-permute-start | bytes 184328 | tf_op jit(solution)/shard_map/ppermute | solution.py:649
  22.7 6.8 %collective-permute-start.1 = (f32[120,128]{1,0:T(8,128)S(1)}, f32[120,128]{1,0:T(8,128)S(1)}, u32[]{:S(2)}, u32[]{:S(2)}) collective-permute-start(f32[120,128]{1,0:T(8,128)S(1)} %get-tuple-element.32), channel_id=1, source_target_pairs={{0,0},{1,2},{2,1},{3,4},{4,3},{5,6},{6,5},{7,8},{8,7},{9,10},{10,9... | collective-permute-start | bytes 184328 | tf_op jit(solution)/shard_map/ppermute | solution.py:648
  44.3 1.4 %collective-permute-start.2 = (f32[128,128]{1,0:T(8,128)S(1)}, f32[128,128]{1,0:T(8,128)S(1)}, u32[]{:S(2)}, u32[]{:S(2)}) collective-permute-start(f32[128,128]{1,0:T(8,128)S(1)} %get-tuple-element.49), channel_id=1, source_target_pairs={{0,1},{1,0},{2,3},{3,2},{4,5},{5,4},{6,7},{7,6},{8,9},{9,8},{10,11... | collective-permute-start | bytes 196616 | tf_op jit(solution)/shard_map/ppermute | solution.py:654

commit v5 on v4

--- a/solution.py
+++ b/solution.py
@@ -36,20 +36,13 @@
     return hi, (x - hi.astype(F32)).astype(BF16)
 
 
-def split3(x):
-    hi = x.astype(BF16)
-    rest = x - hi.astype(F32)
-    mid = rest.astype(BF16)
-    return hi, mid, (rest - mid.astype(F32)).astype(BF16)
-
-
 def dot(a, b):
     return jnp.dot(a, b, preferred_element_type=F32)
 
 
 def pick(onehot, x):
-    parts = split3(x)
-    return dot(onehot, parts[0]) + (dot(onehot, parts[1]) + dot(onehot, parts[2]))
+    both = dot(onehot, jnp.concatenate(split2(x), axis=1))
+    return both[:, : x.shape[1]] + both[:, x.shape[1] :]
 
 
 def padded(x, rows, cols):
@@ -67,16 +60,13 @@
     own_ref, near_ref, far_ref = refs[2 + staged : 5 + staged]
     to_refs = refs[5 + staged : 5 + 2 * staged]
     initial_ref, metric_ref, low_ref, high_ref, sems = refs[-5:]
-    copies = [
-        pltpu.make_async_copy(initial_hbm, initial_ref, sems.at[0]),
-        pltpu.make_async_copy(metric_hbm, metric_ref, sems.at[1]),
-    ]
-    copies += [pltpu.make_async_copy(x, y, sems.at[2 + i]) for i, (x, y) in enumerate(zip(from_refs, to_refs))]
+    fields, _, elems = initial_ref.shape
+    pairs = [(initial_hbm, initial_ref), (metric_hbm, metric_ref)] + list(zip(from_refs, to_refs))
+    copies = [pltpu.make_async_copy(x, y, sems.at[i]) for i, (x, y) in enumerate(pairs)]
     for copy in copies:
         copy.start()
     copies[0].wait()
     copies[1].wait()
-    fields, _, elems = initial_ref.shape
     for f in range(fields):
         own_ref[f] = padded(initial_ref[f], LANES, elems).T
     for k in range(metric_ref.shape[0]):
@@ -118,22 +108,21 @@
 
 def operators_kernel(derivative_ref, coupling_ref, lift_ref, wt_ref, wl_ref, ck_ref):
     fields = coupling_ref.shape[1]
-    dh, dl = zip(*(split2(padded(derivative_ref[k], LANES, LANES).T) for k in range(AXES)))
+    dh, dl = zip(*(split2(padded(DT * derivative_ref[k], LANES, LANES).T) for k in range(AXES)))
     zero = jnp.zeros((LANES, LANES), BF16)
     for row, (left, right) in enumerate(
         [(dh[0], dl[0]), (dh[1], dl[1]), (dh[2], dl[2]), (dh[2], zero), (dh[0], zero), (dh[1], zero)]
     ):
         wt_ref[row * LANES : (row + 1) * LANES, :] = jnp.concatenate([left, right], axis=1)
-    l0h, l0l = split2(padded(lift_ref[0], LANES, LANES).T)
-    l1h, l1l = split2(padded(lift_ref[1], LANES, LANES).T)
+    l0h, l0l = split2(padded(DT * lift_ref[0], LANES, LANES).T)
+    l1h, l1l = split2(padded(DT * lift_ref[1], LANES, LANES).T)
     for row, (left, right) in enumerate([(l0h, l1h), (l0h, l1h), (l0l, l1l)]):
         wl_ref[row * LANES : (row + 1) * LANES, :] = jnp.concatenate([left, right], axis=1)
     rows, cols = AXES * fields * GROUP, fields * GROUP
     spread_rows = (iota((rows, AXES * fields), 0) // GROUP == iota((rows, AXES * fields), 1)).astype(BF16)
     spread_cols = (iota((fields, cols), 0) == iota((fields, cols), 1) // GROUP).astype(BF16)
-    by_row = pick(spread_rows, jnp.concatenate([coupling_ref[k] for k in range(AXES)], axis=0))
-    hi, mid, lo = split3(by_row)
-    full = dot(hi, spread_cols) + (dot(mid, spread_cols) + dot(lo, spread_cols))
+    hi, lo = split2(jnp.concatenate([coupling_ref[k] for k in range(AXES)], axis=0))
+    full = dot(dot(spread_rows, hi).astype(BF16), spread_cols) + dot(dot(spread_rows, lo).astype(BF16), spread_cols)
     full = jnp.where(iota((rows, cols), 0) % GROUP == iota((rows, cols), 1) % GROUP, full, 0.0)
     full_hi = full.astype(BF16).astype(F32)
     ck_ref[...] = jnp.concatenate([full_hi, full_hi, full - full_hi], axis=1).astype(BF16)
@@ -235,12 +224,9 @@
         lane, time = iota((LANES, self.width), 0) - OBS_LANE, iota((LANES, self.width), 1)
         comp = time // STEPS
         turned = (lane == comp * STEPS + (STEPS - 1 - (time - comp * STEPS))).astype(BF16)
-        parts = [dot(turned, part).astype(BF16) for part in split3(self.observed_ref[...])]
-        place = self.place_ref[...]
-        out = [
-            lax.dot_general(place, part, (((1,), (1,)), ((), ())), preferred_element_type=F32) for part in parts
-        ]
-        self.acc_ref[...] = out[0] + (out[1] + out[2])
+        parts = jnp.concatenate([dot(turned, part) for part in split2(self.observed_ref[...])], axis=0).astype(BF16)
+        both = lax.dot_general(self.place_ref[...], parts, (((1,), (1,)), ((), ())), preferred_element_type=F32)
+        self.acc_ref[...] = both[:, :LANES] + both[:, LANES:]
 
     def seen(self):
         live = jnp.sum(self.to_pos_ref[...].astype(F32), axis=0, keepdims=True)
@@ -275,7 +261,8 @@
             columns.append(jnp.concatenate(his + los + his, axis=0).astype(BF16))
         if item.lift_only:
             return
-        v = dot(self.ck_ref[...], jnp.concatenate(columns, axis=1))
+        size = 3 * self.fields * GROUP
+        v = dot(self.ck_ref[:size, :size], jnp.concatenate(columns, axis=1))
         for k in range(AXES):
             scale = [self.metric(k, g) for g in item.groups]
             parts = []
@@ -296,21 +283,23 @@
             for side, g in enumerate(item.groups):
                 rows = slice(f * PAIR_ROWS + side * GROUP, f * PAIR_ROWS + (side + 1) * GROUP)
                 if not item.lift_only:
-                    self.t_ref[f, g * GROUP : (g + 1) * GROUP, :] = both[rows]
+                    self.t_ref[f, g : g + GROUP, :] = both[rows]
                 for face in range(2):
-                    at = (g + 1) * GROUP
+                    at = g + GROUP
                     self.h_ref[face, f, at : at + GROUP, :] = lifted[rows, face * LANES : (face + 1) * LANES]
 
     def update(self, t, g):
-        at = (g + 1) * GROUP
+        at = g + GROUP
         here, before, after = slice(at, at + GROUP), slice(at - 1, at - 1 + GROUP), slice(at + 1, at + 1 + GROUP)
         for f in range(self.fields):
             low, high = self.h_ref.at[0, f], self.h_ref.at[1, f]
             lift = (low[before, :] - low[here, :]) + (high[after, :] - high[here, :])
-            rate = self.t_ref[f, g * GROUP : (g + 1) * GROUP, :] + lift
-            self.store(t, f, g, self.load(t, f, g) + self.factor(g) * rate)
-
-    def run(self, items, ready, after=lambda index: None):
+            change = self.t_ref[f, g : g + GROUP, :] + lift
+            if self.factor(g) is not None:
+                change = self.factor(g) * change
+            self.store(t, f, g, self.load(t, f, g) + change)
+
+    def run(self, items, ready, after=lambda index: None, mended=(set(), set())):
         ready = set(ready)
         product, lifted, done = set(), set(), set()
         wanted = {}
@@ -337,10 +326,12 @@
                 for g in groups:
                     if (t, g) in done or (t, g) not in product:
                         continue
-                    if all(n not in groups or (t, n) in lifted for n in (g - 1, g + 1)):
+                    if all(n not in groups or (t, n) in lifted for n in (g - GROUP, g + GROUP)):
                         self.update(t, g)
                         done.add((t, g))
                         ready.add((t + 1, g))
+            if mended[1] <= ready:
+                ready |= mended[0]
             after(index)
 
 
@@ -350,17 +341,24 @@
 
 
 def own_pair(t, j):
-    first = HALO // GROUP + 2 * j
-    return Item(t, j, (first, first + 1))
+    first = HALO + PAIR_ROWS * j
+    return Item(t, j, (first, first + GROUP))
+
+
+def hold(refs, local):
+    for ref, to in zip(refs, local):
+        rows, cols = ref.shape
+        to[:rows, :cols] = ref[...]
+    return local
 
 
 def early_kernel(me_ref, own_ref, wt_ref, wl_ref, ck_ref, *refs):
     ins, past, outs = refs[:5], refs[5 : 5 + EARLY], refs[5 + EARLY : 11 + EARLY]
-    t_ref, h_ref, lt_ref, lu_ref, place_ref = refs[11 + EARLY :]
+    t_ref, h_ref, lt_ref, lu_ref, *local, place_ref = refs[11 + EARLY :]
+    wt_ref, wl_ref, ck_ref = hold((wt_ref, wl_ref, ck_ref), local)
     planes, elems, _ = own_ref.shape
     fields = planes - AXES
-    shift = HALO // GROUP
-    rows = lambda g: slice((g - shift) * GROUP, (g - shift + 1) * GROUP)
+    rows = lambda g: slice(g - HALO, g - HALO + GROUP)
 
     def load(t, f, g):
         return own_ref[f, rows(g), :] if t == 0 else past[t - 1][f, rows(g), :]
@@ -372,7 +370,7 @@
     for rim in pad:
         h_ref[:, :, rim, :] = jnp.zeros((2, fields, GROUP, LANES), F32)
     stepper = Stepper(
-        fields, load, store, lambda g: DT, lambda k, g: own_ref[fields + k, rows(g), :],
+        fields, load, store, lambda g: None, lambda k, g: own_ref[fields + k, rows(g), :],
         wt_ref, wl_ref, ck_ref, t_ref, h_ref, lt_ref, lu_ref,
     )
     pairs = elems // PAIR_ROWS
@@ -388,12 +386,15 @@
 def scratch(fields, elems):
     rows = elems + 2 * HALO
     tile = fields * PAIR_ROWS
-    slots = rows // PAIR_ROWS + 1
+    slots = rows // PAIR_ROWS + 2
     return [
         VMEM((fields, rows, LANES), F32),
         VMEM((2, fields, rows + 2 * GROUP, LANES), F32),
         VMEM((slots, tile, 6 * LANES), BF16),
         VMEM((slots, tile, 2 * LANES), BF16),
+        VMEM((6 * LANES, 2 * LANES), BF16),
+        VMEM((3 * LANES, 2 * LANES), BF16),
+        VMEM((2 * LANES, 2 * LANES), BF16),
     ]
 
 
@@ -425,38 +426,46 @@
 def march_kernel(me_ref, own_ref, near_ref, far_ref, *refs, last_block):
     past = (own_ref,) + refs[:EARLY]
     wt_ref, wl_ref, ck_ref, eh_ref, wp_ref, acc0_ref, keep_ref, give_ref, rev_ref = refs[EARLY : EARLY + 9]
-    edge_ref, u_ref, m_ref, t_ref, h_ref, lt_ref, lu_ref = refs[EARLY + 9 :]
+    edge_ref, u_ref, m_ref, t_ref, h_ref, lt_ref, lu_ref, *local = refs[EARLY + 9 :]
+    wt_ref, wl_ref, ck_ref = hold((wt_ref, wl_ref, ck_ref), local)
     planes, elems, _ = own_ref.shape
     fields = planes - AXES
     slots = eh_ref.shape[0]
-    shift = HALO // GROUP
-    groups = elems // GROUP + 2 * shift
+    end = HALO + elems
     me = me_ref[0]
-    dt_low = jnp.where(me == 0, 0.0, DT).astype(F32)
-    dt_high = jnp.where(me == last_block, 0.0, DT).astype(F32)
-    rim = list(range(shift + 1)) + list(range(groups - shift - 1, groups))
-    own_rows = lambda g: slice((g - shift) * GROUP, (g - shift + 1) * GROUP)
-    rim_rows = lambda g: slice(rim.index(g) * GROUP, (rim.index(g) + 1) * GROUP)
-    all_rows = lambda g: slice(g * GROUP, (g + 1) * GROUP)
+    in_low = jnp.where(me == 0, 0.0, 1.0).astype(F32)
+    in_high = jnp.where(me == last_block, 0.0, 1.0).astype(F32)
+    skip = HALO - STEPS
+    side_rows = HALO + GROUP
+    low_rim, high_rim = [skip, skip + GROUP], [end - skip, end - skip + GROUP]
+    low_groups, high_groups = list(range(0, side_rows, GROUP)), list(range(end - GROUP, end + HALO, GROUP))
+    own_rows = lambda g: slice(g - HALO, g - HALO + GROUP)
+
+    def rim_rows(g):
+        at = g if g < HALO + GROUP else side_rows + g - (end - GROUP)
+        return slice(at, at + GROUP)
 
     odd = me % 2 == 1
     low_edge = lambda edge: jnp.where(odd, near_ref[edge], far_ref[edge])
     high_edge = lambda edge: jnp.where(odd, far_ref[edge], near_ref[edge])
-    spare = jnp.zeros((HALO - STEPS, LANES), F32)
-    low_rim, high_rim = slice(0, HALO), slice((shift + 2) * GROUP, (2 * shift + 2) * GROUP)
+    spare = jnp.zeros((skip, LANES), F32)
     for f in range(fields):
         edge = slice(f * STEPS, (f + 1) * STEPS)
-        edge_ref[0, f, low_rim, :] = jnp.concatenate([spare, jnp.where(me > 0, low_edge(edge), 0.0)], axis=0)
-        edge_ref[0, f, high_rim, :] = jnp.concatenate([jnp.where(me < last_block, high_edge(edge), 0.0), spare], axis=0)
+        low = jnp.where(me > 0, low_edge(edge), 0.0)
+        high = jnp.where(me < last_block, high_edge(edge), 0.0)
+        edge_ref[0, f, :side_rows, :] = jnp.concatenate([spare, low, own_ref[f, :GROUP, :]], axis=0)
+        edge_ref[0, f, side_rows:, :] = jnp.concatenate([own_ref[f, elems - GROUP :, :], high, spare], axis=0)
+    edge_ref[EARLY] = jnp.zeros(edge_ref.shape[1:], F32)
     edge = slice(fields * STEPS, (fields + 1) * STEPS)
     low_factors, high_factors = low_edge(edge), high_edge(edge)
     for k in range(AXES):
         lane = k * (LANES // AXES)
         spread = lambda x: jnp.broadcast_to(x[:, lane : lane + 1], (STEPS, LANES))
-        m_ref[k, :HALO, :] = jnp.concatenate([spare, spread(low_factors)], axis=0)
-        m_ref[k, HALO:, :] = jnp.concatenate([spread(high_factors), spare], axis=0)
-    h_ref[:, :, :GROUP, :] = jnp.zeros((2, fields, GROUP, LANES), F32)
-    h_ref[:, :, (groups + 1) * GROUP :, :] = jnp.zeros((2, fields, GROUP, LANES), F32)
+        own_low, own_high = own_ref[fields + k, :GROUP, :], own_ref[fields + k, elems - GROUP :, :]
+        m_ref[k, :side_rows, :] = jnp.concatenate([spare, spread(low_factors), own_low], axis=0)
+        m_ref[k, side_rows:, :] = jnp.concatenate([own_high, spread(high_factors), spare], axis=0)
+    h_ref[:, :, :PAIR_ROWS, :] = jnp.zeros((2, fields, PAIR_ROWS, LANES), F32)
+    h_ref[:, :, end + GROUP + HALO - GROUP :, :] = jnp.zeros((2, fields, PAIR_ROWS, LANES), F32)
     half = slots // 2
     keep_ref[...] = acc0_ref[:half]
     give_ref[...] = acc0_ref[half:]
@@ -464,35 +473,54 @@
 
     def load(t, f, g):
         if t > EARLY:
-            return u_ref[t % 2, f, all_rows(g), :]
-        if g in rim and not (t == 0 and shift <= g < groups - shift):
+            return u_ref[t % 2, f, g : g + GROUP, :]
+        if t == EARLY and g in low_groups + high_groups or g in low_rim + high_rim:
             return edge_ref[t, f, rim_rows(g), :]
         return past[t][f, own_rows(g), :]
 
     def store(t, f, g, value):
         if t >= EARLY:
-            u_ref[(t + 1) % 2, f, all_rows(g), :] = value
+            u_ref[(t + 1) % 2, f, g : g + GROUP, :] = value
             return
         row = iota((GROUP, LANES), 0)
-        if g == shift:
-            value = jnp.where(row <= t, value, past[t + 1][f, own_rows(g), :])
-        if g == groups - shift - 1:
-            value = jnp.where(row >= GROUP - 1 - t, value, past[t + 1][f, own_rows(g), :])
+        if g == low_rim[1]:
+            rest = past[t + 1][f, : GROUP - skip, :]
+            value = jnp.where(row <= skip + t, value, jnp.concatenate([rest[:skip], rest], axis=0))
+            if t == EARLY - 1:
+                edge_ref[EARLY, f, side_rows - skip : side_rows, :] = past[t + 1][f, GROUP - skip : GROUP, :]
+        if g == high_rim[0]:
+            rest = past[t + 1][f, elems - (GROUP - skip) :, :]
+            value = jnp.where(row >= GROUP - skip - 1 - t, value, jnp.concatenate([rest, rest[:skip]], axis=0))
+            if t == EARLY - 1:
+                at = elems - GROUP
+                edge_ref[EARLY, f, side_rows : side_rows + skip, :] = past[t + 1][f, at : at + skip, :]
         edge_ref[t + 1, f, rim_rows(g), :] = value
 
     def metric(k, g):
-        if g < shift:
-            return m_ref[k, g * GROUP : (g + 1) * GROUP, :]
-        if g >= groups - shift:
-            at = HALO + (g - groups + shift) * GROUP
-            return m_ref[k, at : at + GROUP, :]
+        if g < HALO or g > end - GROUP:
+            return m_ref[k, rim_rows(g), :]
         return own_ref[fields + k, own_rows(g), :]
 
     def factor(g):
-        return dt_low if g < shift else (dt_high if g >= groups - shift else DT)
+        if g + GROUP <= HALO:
+            return in_low
+        if g >= end:
+            return in_high
+        if g < HALO:
+            return jnp.where(iota((GROUP, LANES), 0) < HALO - g, in_low, 1.0)
+        if g + GROUP > end:
+            return jnp.where(iota((GROUP, LANES), 0) >= end - g, in_high, 1.0)
+        return None
+
+    def own_load(t, f, g):
+        if t < EARLY and g in (HALO, end - GROUP):
+            rest, row = past[t][f, own_rows(g), :], iota((GROUP, LANES), 0)
+            mended = edge_ref[t, f, rim_rows(g), :]
+            return jnp.where(row < t, mended, rest) if g == HALO else jnp.where(row >= GROUP - t, mended, rest)
+        return load(t, f, g)
 
     def sample(t):
-        field = lambda f: jnp.concatenate([load(t + 1, f, g) for g in range(shift, groups - shift)], axis=0)
+        field = lambda f: jnp.concatenate([own_load(t + 1, f, g) for g in range(HALO, end, GROUP)], axis=0)
         columns = []
         for c in range(COMPS):
             x = field(c) if c < 3 else (field(3) + field(4) + field(5)) / 3.0
@@ -513,12 +541,11 @@
     pairs = elems // PAIR_ROWS
     order = sorted(range(pairs), key=lambda j: abs(2 * j + 1 - pairs))
     inner, outer = order[:-2], order[-2:]
-    halo_pair = lambda t, ring, lift_only=False: Item(t, pairs + ring, (shift - 1 - ring, groups - shift + ring), lift_only)
-    first_pair = lambda t: Item(t, pairs + shift, (shift, groups - shift - 1))
+    ring_rows = lambda ring: (HALO - GROUP * (ring + 1), end + GROUP * ring)
     items, samples = [], {}
     fill = -(-len(inner) // EARLY)
     for t in range(EARLY):
-        items += [first_pair(t)] + [halo_pair(t, ring) for ring in range(shift)]
+        items += [Item(t, pairs, (low_rim[1], high_rim[0])), Item(t, pairs + 1, (low_rim[0], high_rim[1]))]
         items += [own_pair(EARLY, j) for j in inner[t * fill : (t + 1) * fill]]
         if t >= 1:
             samples[len(items) - 1] = t - 1
@@ -526,16 +553,18 @@
         items += [own_pair(t, j) for j in (outer if t == EARLY else order)]
         if t > EARLY:
             samples[len(items) - len(order) + 3] = t - 1
-        for ring in range(shift):
+        for ring in range(HALO // GROUP):
             if ring * GROUP < STEPS - t:
-                items.append(halo_pair(t, ring, lift_only=ring * GROUP >= STEPS - 1 - t))
+                items.append(Item(t, pairs + ring, ring_rows(ring), lift_only=ring * GROUP >= STEPS - 1 - t))
         if t == EARLY:
             samples[len(items) - 2] = EARLY - 1
-    ready = {(0, g) for g in rim} | {(EARLY, g) for g in range(groups) if g not in rim}
+    ready = {(0, g) for g in low_rim + high_rim}
+    ready |= {(EARLY, g) for g in range(HALO + GROUP, end - GROUP, GROUP)}
+    mended = {(EARLY, g) for g in low_groups + high_groups}, {(EARLY, g) for g in low_rim + high_rim}
     stepper = Stepper(
         fields, load, store, factor, metric, wt_ref, wl_ref, ck_ref, t_ref, h_ref, lt_ref, lu_ref
     )
-    stepper.run(items, ready, lambda index: sample(samples[index]) if index in samples else None)
+    stepper.run(items, ready, lambda index: sample(samples[index]) if index in samples else None, mended)
     sample(STEPS - 1)
 
 
@@ -557,7 +586,7 @@
         scratch_shapes=[
             VMEM((EARLY + 1, fields, 2 * (HALO + GROUP), LANES), F32),
             VMEM((2, fields, elems + 2 * HALO, LANES), F32),
-            VMEM((AXES, 2 * HALO, LANES), F32),
+            VMEM((AXES, 2 * (HALO + GROUP), LANES), F32),
         ]
         + scratch(fields, elems),
         compiler_params=pltpu.CompilerParams(vmem_limit_bytes=40 << 20),
@@ -592,22 +621,19 @@
     turned = jnp.where(lane < OBS_LANE, got, rev_ref[...] - got).T
 
     def place(rows, onehot):
-        found = dot(jnp.concatenate(split3(rows), axis=0), onehot)
-        return found[:width] + (found[width : 2 * width] + found[2 * width :])
+        found = dot(jnp.concatenate(split2(rows), axis=0), onehot)
+        return found[:width] + found[width:]
 
     residual = place(turned[:width], to_pos_ref[...]) - seen_ref[...]
     res_ref[...] = residual
-    first = pltpu.make_async_copy(res_ref, res_hbm, sems.at[0])
-    first.start()
     mis_ref[...] = 0.5 * jnp.sum(residual * residual, axis=0, keepdims=True)
-    second = pltpu.make_async_copy(mis_ref, mis_hbm, sems.at[1])
-    second.start()
     adj_ref[...] = place(turned[OBS_LANE : OBS_LANE + width], to_slot_ref[...])
-    third = pltpu.make_async_copy(adj_ref, adj_hbm, sems.at[2])
-    third.start()
-    first.wait()
-    second.wait()
-    third.wait()
+    pairs = ((res_ref, res_hbm), (adj_ref, adj_hbm), (mis_ref, mis_hbm))
+    copies = [pltpu.make_async_copy(here, out, sems.at[i]) for i, (here, out) in enumerate(pairs)]
+    for copy in copies:
+        copy.start()
+    for copy in copies:
+        copy.wait()
 
 
 def finish(got, rev, to_slot, to_pos, seen):

time: 62.9 us -> 62.2 us (0.989)
  Pallas kernels: 22 us -> 21.3 us
  transfers between devices with their start and end apart: 3 -> 3, of which waited for: 1 -> 1; matrix products, arithmetic and copies ran while one was open for 0% -> 0% of each run, Pallas kernels for 8% -> 7%
where the time goes in v5:
time: 62.2 us; the launch traced here: 62 us
  starting transfers between devices  22.6 us (36%)
  Pallas kernels  21.3 us (34%)
  blocking collectives  15.9 us (26%)
  waiting for transfers between devices  1.23 us (2%)
  between operations  0.91 us (1%)
    ppermute x1, starting transfers between devices, shards(): near = lax.ppermute(near, MX, [(i, i ^ 1) for i in range(blocks)])  20.5 us
    all_to_all x1, blocking collectives, shards(): got = lax.all_to_all(rows, MX[:2], split_axis=0, concat_axis=0, tiled=True)  15.9 us
    pallas_call x1, Pallas kernels, march(): pl.pallas_call(functools.partial(march_kernel, last_block=last_block), in...  14.2 us
    pallas_call x1, Pallas kernels, early(): pl.pallas_call(early_kernel, in_specs=[smem] + [vmem] * (1 + len(operator...  4.22 us
    ppermute x1, starting transfers between devices, shards(): far = lax.ppermute(far, MX, pairs)  1.94 us
    pallas_call x1, Pallas kernels, turn(): pl.pallas_call(turn_kernel, in_specs=[pl.BlockSpec(memory_space=pltpu.SME...  1.48 us
  transfers between devices with their start and end apart: 3, of which 1 were waited for; matrix products, arithmetic and copies ran while one was open for 0% of the time, Pallas kernels for 7%

profile of v5, /device:TPU:513, one launch (start us, length us, event | category | flops | bytes accessed | tf_op | source)
XLA Modules:
  0.0 62.0 jit_solution(12110244739692723415)
XLA Ops:
  0.6 0.0 copy-start.1
  0.7 0.0 copy-start
  0.7 1.5 %turn.1 = (f32[12,128,128]{2,1,0:T(8,128)S(1)}, f32[120,128]{1,0:T(8,128)S(1)}, f32[120,128]{1,0:T(8,128)S(1)}, f32[3,125,125]{2,1,0:T(8,128)S(1)}, f32[125,256]...) custom-call(s32[1]{0:T(128)} %bitcast.me_ref, ...), custom_call_target="tpu_custom_call" | custom-call | tf_op jit(solution)/shard_map/turn/pallas_call | solution.py:92
  2.2 20.5 %collective-permute-start = (f32[120,128]{1,0:T(8,128)S(1)}, f32[120,128]{1,0:T(8,128)S(1)}, u32[]{:S(2)}, u32[]{:S(2)}) collective-permute-start(f32[120,128]{1,0:T(8,128)S(1)} %get-tuple-element.31), channel_id=1, source_target_pairs={{0,1},{1,0},{2,3},{3,2},{4,5},{5,4},{6,7},{7,6},{8,9},{9,8},{10,11... | collective-permute-start | bytes 184328 | tf_op jit(solution)/shard_map/ppermute | solution.py:675
  22.7 1.9 %collective-permute-start.1 = (f32[120,128]{1,0:T(8,128)S(1)}, f32[120,128]{1,0:T(8,128)S(1)}, u32[]{:S(2)}, u32[]{:S(2)}) collective-permute-start(f32[120,128]{1,0:T(8,128)S(1)} %get-tuple-element.32), channel_id=1, source_target_pairs={{0,0},{1,2},{2,1},{3,4},{4,3},{5,6},{6,5},{7,8},{8,7},{9,10},{10,9... | collective-permute-start | bytes 184328 | tf_op jit(solution)/shard_map/ppermute | solution.py:674
  24.6 0.0 copy-done.1
  24.7 0.0 copy-done
  24.7 0.4 operators.1
  25.1 4.2 %early.1 = (f32[9,128,128]{2,1,0:T(8,128)S(1)}, f32[9,128,128]{2,1,0:T(8,128)S(1)}, f32[9,128,128]{2,1,0:T(8,128)S(1)}, bf16[256,256]{1,0:T(8,128)(2,1)S(1)}, f3...) custom-call(s32[1]{0:T(128)} %bitcast.me_ref, ...), custom_call_target="tpu_custom_call" | custom-call | flops 5000000000 | bytes 4000000 | tf_op jit(solution)/shard_map/early/pallas_call | solution.py:407
  29.3 0.0 collective-permute-done.near_ref
  29.4 0.0 collective-permute-done.1.far_ref
  29.4 14.2 %march.1 = (f32[128,128]{1,0:T(8,128)S(1)}, f32[128,128]{1,0:T(8,128)S(1)}, f32[256,128]{1,0:T(8,128)S(1)}) custom-call(s32[1]{0:T(128)} %bitcast.me_ref, f32[12,128,128]{2,1,0:T(8,128)S(1)} %get-tuple-element.30.own_ref, f32[120,128]{1,0:T(8,128)S(1)} %collective-permute-done.near_ref, f32[120,128]{1,0:T(8,128)S(1)} %collective-permute-done.1.far_ref, ...), custom_call_target="tpu_custom_call" | custom-call | flops 20000000000 | bytes 4000000 | tf_op jit(solution)/shard_map/march/pallas_call | solution.py:578
  43.6 0.1 collective-permute-start.2
  43.8 1.2 %collective-permute-done.2.given_ref = f32[128,128]{1,0:T(8,128)S(1)} collective-permute-done((f32[128,128]{1,0:T(8,128)S(1)}, f32[128,128]{1,0:T(8,128)S(1)}, u32[]{:S(2)}, u32[]{:S(2)}) %collective-permute-start.2) | collective-permute-done | bytes 65568 | tf_op jit(solution)/shard_map/ppermute | solution.py:680
  45.0 15.9 %all_to_all.5 = f32[64,4,128]{2,1,0:T(4,128)S(1)} all-to-all(f32[64,4,128]{2,1,0:T(4,128)S(1)} %bitcast.10), channel_id=1, replica_groups=mesh['shots'=2,'mx_0'=8,'mx_1'=8,'mx_2'=2] {'mx_0','mx_1'}, dimensions={0} | all-to-all | bytes 262144 | tf_op jit(solution)/shard_map/all_to_all | solution.py:682
  60.9 0.9 %finish.1 = (f32[48,256]{1,0:T(8,128)}, f32[1,256]{1,0:T(1,128)}, f32[48,256]{1,0:T(8,128)}) custom-call(f32[256,128]{1,0:T(8,128)S(1)} %bitcast.11, f32[256,128]{1,0:T(8,128)S(1)} %get-tuple-element.50.rev_ref, bf16[256,256]{1,0:T(8,128)(2,1)S(1)} %get-tuple-element.51.to_slot_ref, bf16[256,256]{1,0:T(8,128)(2,1)S(1)} %get-tuple-element.52.to_pos_ref, ...), custom_call_target="tpu_custom_call" | custom-call | tf_op jit(solution)/shard_map/finish/pallas_call | solution.py:644
  (3 shorter events, 0.0 us)
Async XLA Ops:
  0.6 24.0 %copy-start.1 = (f32[3,9,9]{2,0,1:T(4,128)S(1)}, f32[3,9,9]{2,0,1:T(4,128)}, u32[]{:S(2)}) copy-start(f32[3,9,9]{2,0,1:T(4,128)} %param.12) | copy-start | bytes 2920
  0.7 24.0 %copy-start = (f32[2,125,125]{2,0,1:T(2,128)S(1)}, f32[2,125,125]{2,0,1:T(2,128)}, u32[]{:S(2)}) copy-start(f32[2,125,125]{2,0,1:T(2,128)} %param.13) | copy-start | bytes 375004
  2.2 27.2 %collective-permute-start = (f32[120,128]{1,0:T(8,128)S(1)}, f32[120,128]{1,0:T(8,128)S(1)}, u32[]{:S(2)}, u32[]{:S(2)}) collective-permute-start(f32[120,128]{1,0:T(8,128)S(1)} %get-tuple-element.31), channel_id=1, source_target_pairs={{0,1},{1,0},{2,3},{3,2},{4,5},{5,4},{6,7},{7,6},{8,9},{9,8},{10,11... | collective-permute-start | bytes 184328 | tf_op jit(solution)/shard_map/ppermute | solution.py:675
  22.7 6.7 %collective-permute-start.1 = (f32[120,128]{1,0:T(8,128)S(1)}, f32[120,128]{1,0:T(8,128)S(1)}, u32[]{:S(2)}, u32[]{:S(2)}) collective-permute-start(f32[120,128]{1,0:T(8,128)S(1)} %get-tuple-element.32), channel_id=1, source_target_pairs={{0,0},{1,2},{2,1},{3,4},{4,3},{5,6},{6,5},{7,8},{8,7},{9,10},{10,9... | collective-permute-start | bytes 184328 | tf_op jit(solution)/shard_map/ppermute | solution.py:674
  43.6 1.4 %collective-permute-start.2 = (f32[128,128]{1,0:T(8,128)S(1)}, f32[128,128]{1,0:T(8,128)S(1)}, u32[]{:S(2)}, u32[]{:S(2)}) collective-permute-start(f32[128,128]{1,0:T(8,128)S(1)} %get-tuple-element.49), channel_id=1, source_target_pairs={{0,1},{1,0},{2,3},{3,2},{4,5},{5,4},{6,7},{7,6},{8,9},{9,8},{10,11... | collective-permute-start | bytes 196616 | tf_op jit(solution)/shard_map/ppermute | solution.py:680

commit v6 on v5

--- a/solution.py
+++ b/solution.py
@@ -23,6 +23,7 @@
 GROUP = 8
 PAIR_ROWS = 2 * GROUP
 HALO = 16
+WHOLE = 32
 OBS_LANE = 64
 VMEM = pltpu.VMEM
 
@@ -40,9 +41,15 @@
     return jnp.dot(a, b, preferred_element_type=F32)
 
 
-def pick(onehot, x):
-    both = dot(onehot, jnp.concatenate(split2(x), axis=1))
-    return both[:, : x.shape[1]] + both[:, x.shape[1] :]
+def block_index():
+    index = 0
+    for axis in MX:
+        index = index * lax.axis_size(axis) + lax.axis_index(axis)
+    return index
+
+
+def whole(rows):
+    return -(-rows // WHOLE) * WHOLE
 
 
 def padded(x, rows, cols):
@@ -53,7 +60,7 @@
     return x
 
 
-def turn_kernel(me_ref, *refs):
+def turn_kernel(*refs):
     staged = (len(refs) - 10) // 2
     initial_hbm, metric_hbm = refs[:2]
     from_refs = refs[2 : 2 + staged]
@@ -61,7 +68,8 @@
     to_refs = refs[5 + staged : 5 + 2 * staged]
     initial_ref, metric_ref, low_ref, high_ref, sems = refs[-5:]
     fields, _, elems = initial_ref.shape
-    pairs = [(initial_hbm, initial_ref), (metric_hbm, metric_ref)] + list(zip(from_refs, to_refs))
+    pairs = [(initial_hbm, initial_ref), (metric_hbm, metric_ref)]
+    pairs += [(x, y if x.shape == y.shape else y.at[: x.shape[0]]) for x, y in zip(from_refs, to_refs)]
     copies = [pltpu.make_async_copy(x, y, sems.at[i]) for i, (x, y) in enumerate(pairs)]
     for copy in copies:
         copy.start()
@@ -76,24 +84,25 @@
     for edge_ref, rows in ((low_ref, slice(0, STEPS)), (high_ref, slice(elems - STEPS, elems))):
         for f in range(fields):
             edge_ref[f * STEPS : (f + 1) * STEPS, :] = own_ref[f, rows, :]
-        edge_ref[fields * STEPS :, :] = factors[rows]
-    odd = me_ref[0] % 2 == 1
+        edge_ref[fields * STEPS : (fields + 1) * STEPS, :] = factors[rows]
+        edge_ref[(fields + 1) * STEPS :, :] = jnp.zeros((edge_ref.shape[0] - (fields + 1) * STEPS, LANES), F32)
+    odd = block_index() % 2 == 1
     near_ref[...] = jnp.where(odd, low_ref[...], high_ref[...])
     far_ref[...] = jnp.where(odd, high_ref[...], low_ref[...])
     for copy in copies[2:]:
         copy.wait()
 
 
-def turn(me, initial, metric, staged):
+def turn(initial, metric, staged):
     fields, _, elems = initial.shape
     planes = fields + metric.shape[0]
-    edge = jax.ShapeDtypeStruct(((fields + 1) * STEPS, LANES), F32)
+    edge = jax.ShapeDtypeStruct((whole((fields + 1) * STEPS), LANES), F32)
     hbm = pl.BlockSpec(memory_space=pltpu.HBM)
     return pl.pallas_call(
         turn_kernel,
-        in_specs=[pl.BlockSpec(memory_space=pltpu.SMEM)] + [hbm] * (2 + len(staged)),
+        in_specs=[hbm] * (2 + len(staged)),
         out_shape=(jax.ShapeDtypeStruct((planes, elems, LANES), F32), edge, edge)
-        + tuple(jax.ShapeDtypeStruct(x.shape, x.dtype) for x in staged),
+        + tuple(jax.ShapeDtypeStruct((whole(x.shape[0]),) + x.shape[1:] if x.shape[0] < GROUP and x.ndim == 2 else x.shape, x.dtype) for x in staged),
         scratch_shapes=[
             VMEM(initial.shape, F32),
             VMEM(metric.shape, F32),
@@ -103,7 +112,7 @@
         ],
         compiler_params=pltpu.CompilerParams(vmem_limit_bytes=8 << 20),
         name="turn",
-    )(me, *(pltpu.with_memory_space_constraint(x, pltpu.HBM) for x in (initial, metric, *staged)))
+    )(*(pltpu.with_memory_space_constraint(x, pltpu.HBM) for x in (initial, metric, *staged)))
 
 
 def operators_kernel(derivative_ref, coupling_ref, lift_ref, wt_ref, wl_ref, ck_ref):
@@ -125,7 +134,8 @@
     full = dot(dot(spread_rows, hi).astype(BF16), spread_cols) + dot(dot(spread_rows, lo).astype(BF16), spread_cols)
     full = jnp.where(iota((rows, cols), 0) % GROUP == iota((rows, cols), 1) % GROUP, full, 0.0)
     full_hi = full.astype(BF16).astype(F32)
-    ck_ref[...] = jnp.concatenate([full_hi, full_hi, full - full_hi], axis=1).astype(BF16)
+    spread = padded(jnp.concatenate([full_hi, full_hi, full - full_hi], axis=1), *ck_ref.shape)
+    ck_ref[...] = spread.astype(BF16)
 
 
 def operators(derivative, coupling, face_lift):
@@ -136,7 +146,7 @@
         out_shape=(
             jax.ShapeDtypeStruct((6 * LANES, 2 * LANES), BF16),
             jax.ShapeDtypeStruct((3 * LANES, 2 * LANES), BF16),
-            jax.ShapeDtypeStruct((block, 3 * fields * GROUP), BF16),
+            jax.ShapeDtypeStruct((whole(block), 2 * LANES), BF16),
         ),
         compiler_params=pltpu.CompilerParams(vmem_limit_bytes=8 << 20),
         cost_estimate=pl.CostEstimate(flops=1_000_000_000, bytes_accessed=1_000_000, transcendentals=0),
@@ -145,11 +155,11 @@
 
 
 class Order:
-    def __init__(self, me, ins, outs, place_ref):
+    def __init__(self, me, ins, outs, local):
         self.me = me
         self.lives_ref, self.element_ref, self.weight_ref, self.order_ref, self.observed_ref = ins
         self.eh_ref, self.wp_ref, self.acc_ref, self.to_slot_ref, self.to_pos_ref, self.seen_ref = outs
-        self.place_ref = place_ref
+        self.place_ref, self.weight_parts_ref, self.observed_parts_ref = local
         self.width, self.slots = self.observed_ref.shape
         self.chips = self.slots // 4
         self.big = float(self.slots * self.slots)
@@ -158,9 +168,9 @@
         self.odd = me & 1
 
     def pieces(self):
-        yield from (functools.partial(self.slot_rows, other) for other in range(2))
-        yield from (functools.partial(self.position_rows, other) for other in range(2))
-        yield from (self.weights, self.observations, self.seen)
+        yield from (functools.partial(self.slot_rows, 0), self.weights, functools.partial(self.slot_rows, 1))
+        yield from (self.observations, functools.partial(self.position_rows, 0), self.place_weights)
+        yield from (functools.partial(self.position_rows, 1), self.seen, self.place_observations)
 
     def rows(self, other, which):
         start = (2 * other + which) * self.chips
@@ -170,7 +180,7 @@
         return jnp.concatenate([ref[0:1, :], ref[1:2, :]], axis=1)
 
     def live_of(self, block):
-        lives = self.lives_ref[...]
+        lives = self.lives_ref[:1, :]
         there = block == iota((block.shape[0], lives.shape[1]), 1)
         return jnp.sum(jnp.where(there, lives.astype(F32), 0.0), axis=1, keepdims=True)
 
@@ -188,6 +198,7 @@
         found = jnp.min(first, axis=1, keepdims=True), jnp.max(last, axis=1, keepdims=True)
         live_slot = iota((1, slots), 1).astype(F32) < self.live_of(jnp.full((1, 1), self.me, I32))
         element = self.across(self.element_ref).astype(F32)
+        done = 0.0
         for which in range(2):
             rows = self.rows(other, which)
             hot = (found[which].astype(I32) & (slots - 1)) == iota((chips, slots), 1)
@@ -195,6 +206,8 @@
             element_of = jnp.sum(jnp.where(hot, element, 0.0), axis=1, keepdims=True)
             hit = (element_of.astype(I32) == iota((chips, LANES), 1)).astype(BF16)
             self.eh_ref[rows, :] = jnp.concatenate([hit, hit], axis=1)
+            done = done + element_of[:GROUP]
+        return jnp.broadcast_to(done, (GROUP, LANES))
 
     def position_rows(self, other):
         slots, shape = self.slots, (self.chips, self.slots)
@@ -209,22 +222,33 @@
         )
         live = self.live_of(block)
         slot = (mine & (slots - 1)).astype(F32)
+        done = 0.0
         for which in range(2):
             rows = self.rows(other, which)
             hot = found[which] == col
             self.place_ref[rows, :] = hot.astype(BF16)
             slot_of = jnp.sum(jnp.where(hot, slot, 0.0), axis=1, keepdims=True)
             self.to_pos_ref[rows, :] = jnp.where(hot & (slot_of < live), 1.0, 0.0).astype(BF16)
+            done = done + slot_of[:GROUP]
+        return jnp.broadcast_to(done, (GROUP, LANES))
 
     def weights(self):
         weight = padded(self.weight_ref[...], LANES, self.slots).T
-        self.wp_ref[...] = pick(self.to_slot_ref[...], weight)
+        self.weight_parts_ref[...] = jnp.concatenate(split2(weight), axis=1)
+
+    def place_weights(self):
+        both = dot(self.to_slot_ref[...], self.weight_parts_ref[...])
+        self.wp_ref[...] = both[:, :LANES] + both[:, LANES:]
 
     def observations(self):
         lane, time = iota((LANES, self.width), 0) - OBS_LANE, iota((LANES, self.width), 1)
         comp = time // STEPS
         turned = (lane == comp * STEPS + (STEPS - 1 - (time - comp * STEPS))).astype(BF16)
-        parts = jnp.concatenate([dot(turned, part) for part in split2(self.observed_ref[...])], axis=0).astype(BF16)
+        parts = [dot(turned, part).astype(BF16) for part in split2(self.observed_ref[...])]
+        self.observed_parts_ref[...] = jnp.concatenate(parts, axis=0)
+
+    def place_observations(self):
+        parts = self.observed_parts_ref[...]
         both = lax.dot_general(self.place_ref[...], parts, (((1,), (1,)), ((), ())), preferred_element_type=F32)
         self.acc_ref[...] = both[:, :LANES] + both[:, LANES:]
 
@@ -265,6 +289,8 @@
         v = dot(self.ck_ref[:size, :size], jnp.concatenate(columns, axis=1))
         for k in range(AXES):
             scale = [self.metric(k, g) for g in item.groups]
+            if item.after is not None:
+                scale = [x + 0.0 * item.after for x in scale]
             parts = []
             for f in range(self.fields):
                 base = (k * self.fields + f) * GROUP
@@ -299,7 +325,7 @@
                 change = self.factor(g) * change
             self.store(t, f, g, self.load(t, f, g) + change)
 
-    def run(self, items, ready, after=lambda index: None, mended=(set(), set())):
+    def run(self, items, ready, after, mended=(set(), set())):
         ready = set(ready)
         product, lifted, done = set(), set(), set()
         wanted = {}
@@ -336,6 +362,8 @@
 
 
 class Item:
+    after = None
+
     def __init__(self, t, slot, groups, lift_only=False):
         self.t, self.slot, self.groups, self.lift_only = t, slot, groups, lift_only
 
@@ -345,17 +373,9 @@
     return Item(t, j, (first, first + GROUP))
 
 
-def hold(refs, local):
-    for ref, to in zip(refs, local):
-        rows, cols = ref.shape
-        to[:rows, :cols] = ref[...]
-    return local
-
-
-def early_kernel(me_ref, own_ref, wt_ref, wl_ref, ck_ref, *refs):
+def early_kernel(own_ref, wt_ref, wl_ref, ck_ref, *refs):
     ins, past, outs = refs[:5], refs[5 : 5 + EARLY], refs[5 + EARLY : 11 + EARLY]
-    t_ref, h_ref, lt_ref, lu_ref, *local, place_ref = refs[11 + EARLY :]
-    wt_ref, wl_ref, ck_ref = hold((wt_ref, wl_ref, ck_ref), local)
+    t_ref, h_ref, lt_ref, lu_ref, *local = refs[11 + EARLY :]
     planes, elems, _ = own_ref.shape
     fields = planes - AXES
     rows = lambda g: slice(g - HALO, g - HALO + GROUP)
@@ -376,11 +396,14 @@
     pairs = elems // PAIR_ROWS
     order = sorted(range(pairs), key=lambda j: abs(2 * j + 1 - pairs))
     items = [own_pair(t, j) for t in range(EARLY) for j in order]
-    pieces = list(Order(me_ref[0], ins, outs, place_ref).pieces())
-    at = {1 + (len(items) - 3) * i // len(pieces): piece for i, piece in enumerate(pieces)}
-    stepper.run(
-        items, {(0, g) for item in items for g in item.groups}, lambda index: at[index]() if index in at else None
-    )
+    pieces = list(Order(block_index(), ins, outs, local).pieces())
+    at = {(len(items) - 4) * i // len(pieces): piece for i, piece in enumerate(pieces)}
+
+    def beside(index):
+        if index in at:
+            items[index + 4].after = at[index]()
+
+    stepper.run(items, {(0, g) for item in items for g in item.groups}, beside)
 
 
 def scratch(fields, elems):
@@ -392,21 +415,17 @@
         VMEM((2, fields, rows + 2 * GROUP, LANES), F32),
         VMEM((slots, tile, 6 * LANES), BF16),
         VMEM((slots, tile, 2 * LANES), BF16),
-        VMEM((6 * LANES, 2 * LANES), BF16),
-        VMEM((3 * LANES, 2 * LANES), BF16),
-        VMEM((2 * LANES, 2 * LANES), BF16),
     ]
 
 
-def early(me, own, operators, ins):
+def early(own, operators, ins):
     planes, elems, _ = own.shape
     fields = planes - AXES
     width, slots = ins[-1].shape
-    smem = pl.BlockSpec(memory_space=pltpu.SMEM)
     vmem = pl.BlockSpec(memory_space=VMEM)
     return pl.pallas_call(
         early_kernel,
-        in_specs=[smem] + [vmem] * (1 + len(operators) + len(ins)),
+        in_specs=[vmem] * (1 + len(operators) + len(ins)),
         out_shape=tuple(jax.ShapeDtypeStruct((fields, elems, LANES), F32) for _ in range(EARLY))
         + (
             jax.ShapeDtypeStruct((slots, 2 * LANES), BF16),
@@ -416,23 +435,22 @@
             jax.ShapeDtypeStruct((slots, slots), BF16),
             jax.ShapeDtypeStruct((width, slots), F32),
         ),
-        scratch_shapes=scratch(fields, elems) + [VMEM((slots, slots), BF16)],
+        scratch_shapes=scratch(fields, elems) + [VMEM((slots, slots), BF16)] * 3,
         compiler_params=pltpu.CompilerParams(vmem_limit_bytes=32 << 20),
         cost_estimate=pl.CostEstimate(flops=5_000_000_000, bytes_accessed=4_000_000, transcendentals=0),
         name="early",
-    )(me, own, *operators, *ins)
-
-
-def march_kernel(me_ref, own_ref, near_ref, far_ref, *refs, last_block):
+    )(own, *operators, *ins)
+
+
+def march_kernel(own_ref, near_ref, far_ref, *refs, last_block):
     past = (own_ref,) + refs[:EARLY]
     wt_ref, wl_ref, ck_ref, eh_ref, wp_ref, acc0_ref, keep_ref, give_ref, rev_ref = refs[EARLY : EARLY + 9]
-    edge_ref, u_ref, m_ref, t_ref, h_ref, lt_ref, lu_ref, *local = refs[EARLY + 9 :]
-    wt_ref, wl_ref, ck_ref = hold((wt_ref, wl_ref, ck_ref), local)
+    edge_ref, u_ref, m_ref, t_ref, h_ref, lt_ref, lu_ref = refs[EARLY + 9 :]
     planes, elems, _ = own_ref.shape
     fields = planes - AXES
     slots = eh_ref.shape[0]
     end = HALO + elems
-    me = me_ref[0]
+    me = block_index()
     in_low = jnp.where(me == 0, 0.0, 1.0).astype(F32)
     in_high = jnp.where(me == last_block, 0.0, 1.0).astype(F32)
     skip = HALO - STEPS
@@ -568,16 +586,15 @@
     sample(STEPS - 1)
 
 
-def march(me, own, near, far, past, ops, last_block):
+def march(own, near, far, past, ops, last_block):
     eh = ops[3]
     planes, elems, _ = own.shape
     fields = planes - AXES
     slots = eh.shape[0]
-    smem = pl.BlockSpec(memory_space=pltpu.SMEM)
     vmem = pl.BlockSpec(memory_space=VMEM)
     return pl.pallas_call(
         functools.partial(march_kernel, last_block=last_block),
-        in_specs=[smem] + [vmem] * (3 + EARLY + len(ops)),
+        in_specs=[vmem] * (3 + EARLY + len(ops)),
         out_shape=(
             jax.ShapeDtypeStruct((slots // 2, LANES), F32),
             jax.ShapeDtypeStruct((slots // 2, LANES), F32),
@@ -592,7 +609,7 @@
         compiler_params=pltpu.CompilerParams(vmem_limit_bytes=40 << 20),
         cost_estimate=pl.CostEstimate(flops=20_000_000_000, bytes_accessed=4_000_000, transcendentals=0),
         name="march",
-    )(me, own, near, far, *past, *ops)
+    )(own, near, far, *past, *ops)
 
 
 def pack_kernel(keep_ref, given_ref, out_ref):
@@ -666,17 +683,16 @@
 ):
     blocks = lax.axis_size(MX)
     slots = rec_element.shape[0]
-    me = lax.axis_index(MX).astype(I32).reshape(1)
     order, element, lives = (x.reshape(-1, LANES) for x in (shot_order, rec_element, live_counts))
     staged = (derivative, rec_weight, order, element, lives, observed.T)
-    own, near, far, derivative, rec_weight, order, element, lives, observed = turn(me, initial, metric, staged)
+    own, near, far, derivative, rec_weight, order, element, lives, observed = turn(initial, metric, staged)
     pairs = [(i, min(i + 1, blocks - 1) if i % 2 else max(i - 1, 0)) for i in range(blocks)]
     far = lax.ppermute(far, MX, pairs)
     near = lax.ppermute(near, MX, [(i, i ^ 1) for i in range(blocks)])
     ops = operators(derivative, coupling, face_lift)
-    outs = early(me, own, ops, (lives, element, rec_weight, order, observed))
+    outs = early(own, ops, (lives, element, rec_weight, order, observed))
     past, eh, wp, acc0, to_slot, to_pos, seen = (outs[:EARLY],) + tuple(outs[EARLY:])
-    keep, give, rev = march(me, own, near, far, past, (*ops, eh, wp, acc0), blocks - 1)
+    keep, give, rev = march(own, near, far, past, (*ops, eh, wp, acc0), blocks - 1)
     given = lax.ppermute(give, MX, [(i, i ^ 1) for i in range(blocks)])
     rows = pack(keep, given).reshape(blocks // 2, 4, LANES)
     got = lax.all_to_all(rows, MX[:2], split_axis=0, concat_axis=0, tiled=True)

time: 62.2 us -> 61.5 us (0.989)
  Pallas kernels: 21.3 us -> 20.6 us
where the time goes in v6:
time: 61.5 us; the launch traced here: 61.3 us
  starting transfers between devices  22.6 us (37%)
  Pallas kernels  20.6 us (33%)
  blocking collectives  15.9 us (26%)
  waiting for transfers between devices  1.23 us (2%)
  between operations  0.91 us (1%)
    ppermute x1, starting transfers between devices, shards(): near = lax.ppermute(near, MX, [(i, i ^ 1) for i in range(blocks)])  20.5 us
    all_to_all x1, blocking collectives, shards(): got = lax.all_to_all(rows, MX[:2], split_axis=0, concat_axis=0, tiled=True)  15.9 us
    pallas_call x1, Pallas kernels, march(): pl.pallas_call(functools.partial(march_kernel, last_block=last_block), in...  13.9 us
    pallas_call x1, Pallas kernels, early(): pl.pallas_call(early_kernel, in_specs=[vmem] * (1 + len(operators) + len(...  3.89 us
    ppermute x1, starting transfers between devices, shards(): far = lax.ppermute(far, MX, pairs)  1.94 us
    pallas_call x1, Pallas kernels, turn(): pl.pallas_call(turn_kernel, in_specs=[hbm] * (2 + len(staged)), out_shape...  1.48 us
  transfers between devices with their start and end apart: 3, of which 1 were waited for; matrix products, arithmetic and copies ran while one was open for 0% of the time, Pallas kernels for 7%

profile of v6, /device:TPU:513, one launch (start us, length us, event | category | flops | bytes accessed | tf_op | source)
XLA Modules:
  0.0 61.3 jit_solution(12680645647208129839)
XLA Ops:
  0.6 0.0 copy-start.1
  0.6 0.0 copy-start
  0.7 1.5 %turn.1 = (f32[12,128,128]{2,1,0:T(8,128)S(1)}, f32[128,128]{1,0:T(8,128)S(1)}, f32[128,128]{1,0:T(8,128)S(1)}, f32[3,125,125]{2,1,0:T(8,128)S(1)}, f32[125,256]...) custom-call(f32[9,125,128]{2,1,0:T(8,128)} %refs_0_.1, ...), custom_call_target="tpu_custom_call" | custom-call | tf_op jit(solution)/shard_map/turn/pallas_call | solution.py:101
  2.1 20.5 %collective-permute-start = (f32[128,128]{1,0:T(8,128)S(1)}, f32[128,128]{1,0:T(8,128)S(1)}, u32[]{:S(2)}, u32[]{:S(2)}) collective-permute-start(f32[128,128]{1,0:T(8,128)S(1)} %get-tuple-element.31), channel_id=1, source_target_pairs={{0,1},{1,0},{2,3},{3,2},{4,5},{5,4},{6,7},{7,6},{8,9},{9,8},{10,11... | collective-permute-start | bytes 196616 | tf_op jit(solution)/shard_map/ppermute | solution.py:691
  22.7 1.9 %collective-permute-start.1 = (f32[128,128]{1,0:T(8,128)S(1)}, f32[128,128]{1,0:T(8,128)S(1)}, u32[]{:S(2)}, u32[]{:S(2)}) collective-permute-start(f32[128,128]{1,0:T(8,128)S(1)} %get-tuple-element.32), channel_id=1, source_target_pairs={{0,0},{1,2},{2,1},{3,4},{4,3},{5,6},{6,5},{7,8},{8,7},{9,10},{10,9... | collective-permute-start | bytes 196616 | tf_op jit(solution)/shard_map/ppermute | solution.py:690
  24.6 0.0 copy-done.1
  24.6 0.0 copy-done
  24.7 0.4 operators.1
  25.1 3.9 %early.1 = (f32[9,128,128]{2,1,0:T(8,128)S(1)}, f32[9,128,128]{2,1,0:T(8,128)S(1)}, f32[9,128,128]{2,1,0:T(8,128)S(1)}, bf16[256,256]{1,0:T(8,128)(2,1)S(1)}, f3...) custom-call(f32[12,128,128]{2,1,0:T(8,128)S(1)} %get-tuple-element.3, ...), custom_call_target="tpu_custom_call" | custom-call | flops 5000000000 | bytes 4000000 | tf_op jit(solution)/shard_map/early/pallas_call | solution.py:426
  29.0 0.0 collective-permute-done.near_ref
  29.0 0.0 collective-permute-done.1.far_ref
  29.0 13.9 %march.1 = (f32[128,128]{1,0:T(8,128)S(1)}, f32[128,128]{1,0:T(8,128)S(1)}, f32[256,128]{1,0:T(8,128)S(1)}) custom-call(f32[12,128,128]{2,1,0:T(8,128)S(1)} %get-tuple-element.30.own_ref, f32[128,128]{1,0:T(8,128)S(1)} %collective-permute-done.near_ref, f32[128,128]{1,0:T(8,128)S(1)} %collective-permute-done.1.far_ref, ...), custom_call_target="tpu_custom_call" | custom-call | flops 20000000000 | bytes 4000000 | tf_op jit(solution)/shard_map/march/pallas_call | solution.py:595
  42.9 0.1 collective-permute-start.2
  43.1 1.2 %collective-permute-done.2.given_ref = f32[128,128]{1,0:T(8,128)S(1)} collective-permute-done((f32[128,128]{1,0:T(8,128)S(1)}, f32[128,128]{1,0:T(8,128)S(1)}, u32[]{:S(2)}, u32[]{:S(2)}) %collective-permute-start.2) | collective-permute-done | bytes 65568 | tf_op jit(solution)/shard_map/ppermute | solution.py:696
  44.3 15.9 %all_to_all.5 = f32[64,4,128]{2,1,0:T(4,128)S(1)} all-to-all(f32[64,4,128]{2,1,0:T(4,128)S(1)} %bitcast.9), channel_id=1, replica_groups=mesh['shots'=2,'mx_0'=8,'mx_1'=8,'mx_2'=2] {'mx_0','mx_1'}, dimensions={0} | all-to-all | bytes 262144 | tf_op jit(solution)/shard_map/all_to_all | solution.py:698
  60.2 0.9 %finish.1 = (f32[48,256]{1,0:T(8,128)}, f32[1,256]{1,0:T(1,128)}, f32[48,256]{1,0:T(8,128)}) custom-call(f32[256,128]{1,0:T(8,128)S(1)} %bitcast.10, f32[256,128]{1,0:T(8,128)S(1)} %get-tuple-element.50.rev_ref, bf16[256,256]{1,0:T(8,128)(2,1)S(1)} %get-tuple-element.51.to_slot_ref, bf16[256,256]{1,0:T(8,128)(2,1)S(1)} %get-tuple-element.52.to_pos_ref, ...), custom_call_target="tpu_custom_call" | custom-call | tf_op jit(solution)/shard_map/finish/pallas_call | solution.py:661
  (3 shorter events, 0.0 us)
Async XLA Ops:
  0.6 24.0 %copy-start.1 = (f32[3,9,9]{2,0,1:T(4,128)S(1)}, f32[3,9,9]{2,0,1:T(4,128)}, u32[]{:S(2)}) copy-start(f32[3,9,9]{2,0,1:T(4,128)} %param.12) | copy-start | bytes 2920
  0.6 24.0 %copy-start = (f32[2,125,125]{2,0,1:T(2,128)S(1)}, f32[2,125,125]{2,0,1:T(2,128)}, u32[]{:S(2)}) copy-start(f32[2,125,125]{2,0,1:T(2,128)} %param.13) | copy-start | bytes 375004
  2.1 26.9 %collective-permute-start = (f32[128,128]{1,0:T(8,128)S(1)}, f32[128,128]{1,0:T(8,128)S(1)}, u32[]{:S(2)}, u32[]{:S(2)}) collective-permute-start(f32[128,128]{1,0:T(8,128)S(1)} %get-tuple-element.31), channel_id=1, source_target_pairs={{0,1},{1,0},{2,3},{3,2},{4,5},{5,4},{6,7},{7,6},{8,9},{9,8},{10,11... | collective-permute-start | bytes 196616 | tf_op jit(solution)/shard_map/ppermute | solution.py:691
  22.7 6.3 %collective-permute-start.1 = (f32[128,128]{1,0:T(8,128)S(1)}, f32[128,128]{1,0:T(8,128)S(1)}, u32[]{:S(2)}, u32[]{:S(2)}) collective-permute-start(f32[128,128]{1,0:T(8,128)S(1)} %get-tuple-element.32), channel_id=1, source_target_pairs={{0,0},{1,2},{2,1},{3,4},{4,3},{5,6},{6,5},{7,8},{8,7},{9,10},{10,9... | collective-permute-start | bytes 196616 | tf_op jit(solution)/shard_map/ppermute | solution.py:690
  42.9 1.4 %collective-permute-start.2 = (f32[128,128]{1,0:T(8,128)S(1)}, f32[128,128]{1,0:T(8,128)S(1)}, u32[]{:S(2)}, u32[]{:S(2)}) collective-permute-start(f32[128,128]{1,0:T(8,128)S(1)} %get-tuple-element.49), channel_id=1, source_target_pairs={{0,1},{1,0},{2,3},{3,2},{4,5},{5,4},{6,7},{7,6},{8,9},{9,8},{10,11... | collective-permute-start | bytes 196616 | tf_op jit(solution)/shard_map/ppermute | solution.py:696

commit v7 on v6

--- a/solution.py
+++ b/solution.py
@@ -373,6 +373,13 @@
     return Item(t, j, (first, first + GROUP))
 
 
+def hold(refs, local):
+    for ref, to in zip(refs, local):
+        rows, cols = ref.shape
+        to[:rows, :cols] = ref[...]
+    return local
+
+
 def early_kernel(own_ref, wt_ref, wl_ref, ck_ref, *refs):
     ins, past, outs = refs[:5], refs[5 : 5 + EARLY], refs[5 + EARLY : 11 + EARLY]
     t_ref, h_ref, lt_ref, lu_ref, *local = refs[11 + EARLY :]
@@ -445,7 +452,8 @@
 def march_kernel(own_ref, near_ref, far_ref, *refs, last_block):
     past = (own_ref,) + refs[:EARLY]
     wt_ref, wl_ref, ck_ref, eh_ref, wp_ref, acc0_ref, keep_ref, give_ref, rev_ref = refs[EARLY : EARLY + 9]
-    edge_ref, u_ref, m_ref, t_ref, h_ref, lt_ref, lu_ref = refs[EARLY + 9 :]
+    edge_ref, u_ref, m_ref, t_ref, h_ref, lt_ref, lu_ref, *local = refs[EARLY + 9 :]
+    wt_ref, wl_ref, ck_ref = hold((wt_ref, wl_ref, ck_ref), local)
     planes, elems, _ = own_ref.shape
     fields = planes - AXES
     slots = eh_ref.shape[0]
@@ -605,7 +613,8 @@
             VMEM((2, fields, elems + 2 * HALO, LANES), F32),
             VMEM((AXES, 2 * (HALO + GROUP), LANES), F32),
         ]
-        + scratch(fields, elems),
+        + scratch(fields, elems)
+        + [VMEM((6 * LANES, 2 * LANES), BF16), VMEM((3 * LANES, 2 * LANES), BF16), VMEM((2 * LANES, 2 * LANES), BF16)],
         compiler_params=pltpu.CompilerParams(vmem_limit_bytes=40 << 20),
         cost_estimate=pl.CostEstimate(flops=20_000_000_000, bytes_accessed=4_000_000, transcendentals=0),
         name="march",

time: 61.5 us -> 61.3 us (level)
  no operation moved by 1% of the time
where the time goes in v7:
time: 61.3 us; the launch traced here: 61.1 us
  starting transfers between devices  22.6 us (37%)
  Pallas kernels  20.4 us (33%)
  blocking collectives  15.9 us (26%)
  waiting for transfers between devices  1.23 us (2%)
  between operations  0.91 us (1%)
    ppermute x1, starting transfers between devices, shards(): near = lax.ppermute(near, MX, [(i, i ^ 1) for i in range(blocks)])  20.5 us
    all_to_all x1, blocking collectives, shards(): got = lax.all_to_all(rows, MX[:2], split_axis=0, concat_axis=0, tiled=True)  15.9 us
    pallas_call x1, Pallas kernels, march(): pl.pallas_call(functools.partial(march_kernel, last_block=last_block), in...  13.7 us
    pallas_call x1, Pallas kernels, early(): pl.pallas_call(early_kernel, in_specs=[vmem] * (1 + len(operators) + len(...  3.89 us
    ppermute x1, starting transfers between devices, shards(): far = lax.ppermute(far, MX, pairs)  1.94 us
    pallas_call x1, Pallas kernels, turn(): pl.pallas_call(turn_kernel, in_specs=[hbm] * (2 + len(staged)), out_shape...  1.48 us
    ppermute x1, waiting for transfers between devices, shards(): given = lax.ppermute(give, MX, [(i, i ^ 1) for i in range(blocks)])  1.23 us
  transfers between devices with their start and end apart: 3, of which 1 were waited for; matrix products, arithmetic and copies ran while one was open for 0% of the time, Pallas kernels for 7%

profile of v7, /device:TPU:513, one launch (start us, length us, event | category | flops | bytes accessed | tf_op | source)
XLA Modules:
  0.0 61.1 jit_solution(17365083462036390632)
XLA Ops:
  0.6 0.0 copy-start.1
  0.6 0.0 copy-start
  0.7 1.5 %turn.1 = (f32[12,128,128]{2,1,0:T(8,128)S(1)}, f32[128,128]{1,0:T(8,128)S(1)}, f32[128,128]{1,0:T(8,128)S(1)}, f32[3,125,125]{2,1,0:T(8,128)S(1)}, f32[125,256]...) custom-call(f32[9,125,128]{2,1,0:T(8,128)} %refs_0_.1, ...), custom_call_target="tpu_custom_call" | custom-call | tf_op jit(solution)/shard_map/turn/pallas_call | solution.py:101
  2.1 20.5 %collective-permute-start = (f32[128,128]{1,0:T(8,128)S(1)}, f32[128,128]{1,0:T(8,128)S(1)}, u32[]{:S(2)}, u32[]{:S(2)}) collective-permute-start(f32[128,128]{1,0:T(8,128)S(1)} %get-tuple-element.31), channel_id=1, source_target_pairs={{0,1},{1,0},{2,3},{3,2},{4,5},{5,4},{6,7},{7,6},{8,9},{9,8},{10,11... | collective-permute-start | bytes 196616 | tf_op jit(solution)/shard_map/ppermute | solution.py:700
  22.7 1.9 %collective-permute-start.1 = (f32[128,128]{1,0:T(8,128)S(1)}, f32[128,128]{1,0:T(8,128)S(1)}, u32[]{:S(2)}, u32[]{:S(2)}) collective-permute-start(f32[128,128]{1,0:T(8,128)S(1)} %get-tuple-element.32), channel_id=1, source_target_pairs={{0,0},{1,2},{2,1},{3,4},{4,3},{5,6},{6,5},{7,8},{8,7},{9,10},{10,9... | collective-permute-start | bytes 196616 | tf_op jit(solution)/shard_map/ppermute | solution.py:699
  24.6 0.0 copy-done.1
  24.6 0.0 copy-done
  24.7 0.4 operators.1
  25.1 3.9 %early.1 = (f32[9,128,128]{2,1,0:T(8,128)S(1)}, f32[9,128,128]{2,1,0:T(8,128)S(1)}, f32[9,128,128]{2,1,0:T(8,128)S(1)}, bf16[256,256]{1,0:T(8,128)(2,1)S(1)}, f3...) custom-call(f32[12,128,128]{2,1,0:T(8,128)S(1)} %get-tuple-element.3, ...), custom_call_target="tpu_custom_call" | custom-call | flops 5000000000 | bytes 4000000 | tf_op jit(solution)/shard_map/early/pallas_call | solution.py:433
  29.0 0.0 collective-permute-done.near_ref
  29.0 0.0 collective-permute-done.1.far_ref
  29.0 13.7 %march.1 = (f32[128,128]{1,0:T(8,128)S(1)}, f32[128,128]{1,0:T(8,128)S(1)}, f32[256,128]{1,0:T(8,128)S(1)}) custom-call(f32[12,128,128]{2,1,0:T(8,128)S(1)} %get-tuple-element.30.own_ref, f32[128,128]{1,0:T(8,128)S(1)} %collective-permute-done.near_ref, f32[128,128]{1,0:T(8,128)S(1)} %collective-permute-done.1.far_ref, ...), custom_call_target="tpu_custom_call" | custom-call | flops 20000000000 | bytes 4000000 | tf_op jit(solution)/shard_map/march/pallas_call | solution.py:603
  42.8 0.1 collective-permute-start.2
  42.9 1.2 %collective-permute-done.2.given_ref = f32[128,128]{1,0:T(8,128)S(1)} collective-permute-done((f32[128,128]{1,0:T(8,128)S(1)}, f32[128,128]{1,0:T(8,128)S(1)}, u32[]{:S(2)}, u32[]{:S(2)}) %collective-permute-start.2) | collective-permute-done | bytes 65568 | tf_op jit(solution)/shard_map/ppermute | solution.py:705
  44.1 15.9 %all_to_all.5 = f32[64,4,128]{2,1,0:T(4,128)S(1)} all-to-all(f32[64,4,128]{2,1,0:T(4,128)S(1)} %bitcast.9), channel_id=1, replica_groups=mesh['shots'=2,'mx_0'=8,'mx_1'=8,'mx_2'=2] {'mx_0','mx_1'}, dimensions={0} | all-to-all | bytes 262144 | tf_op jit(solution)/shard_map/all_to_all | solution.py:707
  60.1 0.9 %finish.1 = (f32[48,256]{1,0:T(8,128)}, f32[1,256]{1,0:T(1,128)}, f32[48,256]{1,0:T(8,128)}) custom-call(f32[256,128]{1,0:T(8,128)S(1)} %bitcast.10, f32[256,128]{1,0:T(8,128)S(1)} %get-tuple-element.50.rev_ref, bf16[256,256]{1,0:T(8,128)(2,1)S(1)} %get-tuple-element.51.to_slot_ref, bf16[256,256]{1,0:T(8,128)(2,1)S(1)} %get-tuple-element.52.to_pos_ref, ...), custom_call_target="tpu_custom_call" | custom-call | tf_op jit(solution)/shard_map/finish/pallas_call | solution.py:670
  (3 shorter events, 0.0 us)
Async XLA Ops:
  0.6 24.0 %copy-start.1 = (f32[3,9,9]{2,0,1:T(4,128)S(1)}, f32[3,9,9]{2,0,1:T(4,128)}, u32[]{:S(2)}) copy-start(f32[3,9,9]{2,0,1:T(4,128)} %param.12) | copy-start | bytes 2920
  0.6 24.0 %copy-start = (f32[2,125,125]{2,0,1:T(2,128)S(1)}, f32[2,125,125]{2,0,1:T(2,128)}, u32[]{:S(2)}) copy-start(f32[2,125,125]{2,0,1:T(2,128)} %param.13) | copy-start | bytes 375004
  2.1 26.9 %collective-permute-start = (f32[128,128]{1,0:T(8,128)S(1)}, f32[128,128]{1,0:T(8,128)S(1)}, u32[]{:S(2)}, u32[]{:S(2)}) collective-permute-start(f32[128,128]{1,0:T(8,128)S(1)} %get-tuple-element.31), channel_id=1, source_target_pairs={{0,1},{1,0},{2,3},{3,2},{4,5},{5,4},{6,7},{7,6},{8,9},{9,8},{10,11... | collective-permute-start | bytes 196616 | tf_op jit(solution)/shard_map/ppermute | solution.py:700
  22.7 6.3 %collective-permute-start.1 = (f32[128,128]{1,0:T(8,128)S(1)}, f32[128,128]{1,0:T(8,128)S(1)}, u32[]{:S(2)}, u32[]{:S(2)}) collective-permute-start(f32[128,128]{1,0:T(8,128)S(1)} %get-tuple-element.32), channel_id=1, source_target_pairs={{0,0},{1,2},{2,1},{3,4},{4,3},{5,6},{6,5},{7,8},{8,7},{9,10},{10,9... | collective-permute-start | bytes 196616 | tf_op jit(solution)/shard_map/ppermute | solution.py:699
  42.8 1.4 %collective-permute-start.2 = (f32[128,128]{1,0:T(8,128)S(1)}, f32[128,128]{1,0:T(8,128)S(1)}, u32[]{:S(2)}, u32[]{:S(2)}) collective-permute-start(f32[128,128]{1,0:T(8,128)S(1)} %get-tuple-element.49), channel_id=1, source_target_pairs={{0,1},{1,0},{2,3},{3,2},{4,5},{5,4},{6,7},{7,6},{8,9},{9,8},{10,11... | collective-permute-start | bytes 196616 | tf_op jit(solution)/shard_map/ppermute | solution.py:705

commit v8 on v7

--- a/solution.py
+++ b/solution.py
@@ -303,23 +303,22 @@
         lu = self.lu_ref.at[item.slot]
         if not item.lift_only:
             both = dot(self.lt_ref[item.slot], self.wt_ref[...])
-            both = both[:, :LANES] + both[:, LANES:]
         lifted = dot(lu[...], self.wl_ref[: 2 * LANES, :]) + dot(lu[:, :LANES], self.wl_ref[2 * LANES :, :])
         for f in range(self.fields):
             for side, g in enumerate(item.groups):
                 rows = slice(f * PAIR_ROWS + side * GROUP, f * PAIR_ROWS + (side + 1) * GROUP)
+                faces = [lifted[rows, face * LANES : (face + 1) * LANES] for face in range(2)]
                 if not item.lift_only:
-                    self.t_ref[f, g : g + GROUP, :] = both[rows]
+                    total = both[rows, :LANES] + both[rows, LANES:]
+                    self.t_ref[f, g : g + GROUP, :] = total - (faces[0] + faces[1])
                 for face in range(2):
                     at = g + GROUP
-                    self.h_ref[face, f, at : at + GROUP, :] = lifted[rows, face * LANES : (face + 1) * LANES]
+                    self.h_ref[face, f, at : at + GROUP, :] = faces[face]
 
     def update(self, t, g):
-        at = g + GROUP
-        here, before, after = slice(at, at + GROUP), slice(at - 1, at - 1 + GROUP), slice(at + 1, at + 1 + GROUP)
+        before, after = slice(g + GROUP - 1, g + 2 * GROUP - 1), slice(g + GROUP + 1, g + 2 * GROUP + 1)
         for f in range(self.fields):
-            low, high = self.h_ref.at[0, f], self.h_ref.at[1, f]
-            lift = (low[before, :] - low[here, :]) + (high[after, :] - high[here, :])
+            lift = self.h_ref[0, f, before, :] + self.h_ref[1, f, after, :]
             change = self.t_ref[f, g : g + GROUP, :] + lift
             if self.factor(g) is not None:
                 change = self.factor(g) * change
@@ -578,7 +577,7 @@
     for t in range(EARLY, STEPS):
         items += [own_pair(t, j) for j in (outer if t == EARLY else order)]
         if t > EARLY:
-            samples[len(items) - len(order) + 3] = t - 1
+            samples[len(items) - len(order) + 2] = t - 1
         for ring in range(HALO // GROUP):
             if ring * GROUP < STEPS - t:
                 items.append(Item(t, pairs + ring, ring_rows(ring), lift_only=ring * GROUP >= STEPS - 1 - t))

time: 61.3 us -> 61.1 us (level)
  no operation moved by 1% of the time
where the time goes in v8:
time: 61.1 us; the launch traced here: 60.9 us
  starting transfers between devices  22.6 us (37%)
  Pallas kernels  20.2 us (33%)
  blocking collectives  16 us (26%)
  waiting for transfers between devices  1.23 us (2%)
  between operations  0.91 us (1%)
    ppermute x1, starting transfers between devices, shards(): near = lax.ppermute(near, MX, [(i, i ^ 1) for i in range(blocks)])  20.5 us
    all_to_all x1, blocking collectives, shards(): got = lax.all_to_all(rows, MX[:2], split_axis=0, concat_axis=0, tiled=True)  16 us
    pallas_call x1, Pallas kernels, march(): pl.pallas_call(functools.partial(march_kernel, last_block=last_block), in...  13.6 us
    pallas_call x1, Pallas kernels, early(): pl.pallas_call(early_kernel, in_specs=[vmem] * (1 + len(operators) + len(...  3.76 us
    ppermute x1, starting transfers between devices, shards(): far = lax.ppermute(far, MX, pairs)  1.94 us
    pallas_call x1, Pallas kernels, turn(): pl.pallas_call(turn_kernel, in_specs=[hbm] * (2 + len(staged)), out_shape...  1.48 us
    ppermute x1, waiting for transfers between devices, shards(): given = lax.ppermute(give, MX, [(i, i ^ 1) for i in range(blocks)])  1.23 us
  transfers between devices with their start and end apart: 3, of which 1 were waited for; matrix products, arithmetic and copies ran while one was open for 0% of the time, Pallas kernels for 7%

profile of v8, /device:TPU:513, one launch (start us, length us, event | category | flops | bytes accessed | tf_op | source)
XLA Modules:
  0.0 60.9 jit_solution(7286611351497474632)
XLA Ops:
  0.6 0.0 copy-start.1
  0.6 0.0 copy-start
  0.7 1.5 %turn.1 = (f32[12,128,128]{2,1,0:T(8,128)S(1)}, f32[128,128]{1,0:T(8,128)S(1)}, f32[128,128]{1,0:T(8,128)S(1)}, f32[3,125,125]{2,1,0:T(8,128)S(1)}, f32[125,256]...) custom-call(f32[9,125,128]{2,1,0:T(8,128)} %refs_0_.1, ...), custom_call_target="tpu_custom_call" | custom-call | tf_op jit(solution)/shard_map/turn/pallas_call | solution.py:101
  2.1 20.5 %collective-permute-start = (f32[128,128]{1,0:T(8,128)S(1)}, f32[128,128]{1,0:T(8,128)S(1)}, u32[]{:S(2)}, u32[]{:S(2)}) collective-permute-start(f32[128,128]{1,0:T(8,128)S(1)} %get-tuple-element.31), channel_id=1, source_target_pairs={{0,1},{1,0},{2,3},{3,2},{4,5},{5,4},{6,7},{7,6},{8,9},{9,8},{10,11... | collective-permute-start | bytes 196616 | tf_op jit(solution)/shard_map/ppermute | solution.py:699
  22.7 1.9 %collective-permute-start.1 = (f32[128,128]{1,0:T(8,128)S(1)}, f32[128,128]{1,0:T(8,128)S(1)}, u32[]{:S(2)}, u32[]{:S(2)}) collective-permute-start(f32[128,128]{1,0:T(8,128)S(1)} %get-tuple-element.32), channel_id=1, source_target_pairs={{0,0},{1,2},{2,1},{3,4},{4,3},{5,6},{6,5},{7,8},{8,7},{9,10},{10,9... | collective-permute-start | bytes 196616 | tf_op jit(solution)/shard_map/ppermute | solution.py:698
  24.6 0.0 copy-done.1
  24.6 0.0 copy-done
  24.7 0.4 operators.1
  25.1 3.8 %early.1 = (f32[9,128,128]{2,1,0:T(8,128)S(1)}, f32[9,128,128]{2,1,0:T(8,128)S(1)}, f32[9,128,128]{2,1,0:T(8,128)S(1)}, bf16[256,256]{1,0:T(8,128)(2,1)S(1)}, f3...) custom-call(f32[12,128,128]{2,1,0:T(8,128)S(1)} %get-tuple-element.3, ...), custom_call_target="tpu_custom_call" | custom-call | flops 5000000000 | bytes 4000000 | tf_op jit(solution)/shard_map/early/pallas_call | solution.py:432
  28.9 0.0 collective-permute-done.near_ref
  28.9 0.0 collective-permute-done.1.far_ref
  28.9 13.6 %march.1 = (f32[128,128]{1,0:T(8,128)S(1)}, f32[128,128]{1,0:T(8,128)S(1)}, f32[256,128]{1,0:T(8,128)S(1)}) custom-call(f32[12,128,128]{2,1,0:T(8,128)S(1)} %get-tuple-element.30.own_ref, f32[128,128]{1,0:T(8,128)S(1)} %collective-permute-done.near_ref, f32[128,128]{1,0:T(8,128)S(1)} %collective-permute-done.1.far_ref, ...), custom_call_target="tpu_custom_call" | custom-call | flops 20000000000 | bytes 4000000 | tf_op jit(solution)/shard_map/march/pallas_call | solution.py:602
  42.5 0.1 collective-permute-start.2
  42.7 1.2 %collective-permute-done.2.given_ref = f32[128,128]{1,0:T(8,128)S(1)} collective-permute-done((f32[128,128]{1,0:T(8,128)S(1)}, f32[128,128]{1,0:T(8,128)S(1)}, u32[]{:S(2)}, u32[]{:S(2)}) %collective-permute-start.2) | collective-permute-done | bytes 65568 | tf_op jit(solution)/shard_map/ppermute | solution.py:704
  43.9 16.0 %all_to_all.5 = f32[64,4,128]{2,1,0:T(4,128)S(1)} all-to-all(f32[64,4,128]{2,1,0:T(4,128)S(1)} %bitcast.9), channel_id=1, replica_groups=mesh['shots'=2,'mx_0'=8,'mx_1'=8,'mx_2'=2] {'mx_0','mx_1'}, dimensions={0} | all-to-all | bytes 262144 | tf_op jit(solution)/shard_map/all_to_all | solution.py:706
  59.9 0.9 %finish.1 = (f32[48,256]{1,0:T(8,128)}, f32[1,256]{1,0:T(1,128)}, f32[48,256]{1,0:T(8,128)}) custom-call(f32[256,128]{1,0:T(8,128)S(1)} %bitcast.10, f32[256,128]{1,0:T(8,128)S(1)} %get-tuple-element.50.rev_ref, bf16[256,256]{1,0:T(8,128)(2,1)S(1)} %get-tuple-element.51.to_slot_ref, bf16[256,256]{1,0:T(8,128)(2,1)S(1)} %get-tuple-element.52.to_pos_ref, ...), custom_call_target="tpu_custom_call" | custom-call | tf_op jit(solution)/shard_map/finish/pallas_call | solution.py:669
  (3 shorter events, 0.0 us)
Async XLA Ops:
  0.6 24.0 %copy-start.1 = (f32[3,9,9]{2,0,1:T(4,128)S(1)}, f32[3,9,9]{2,0,1:T(4,128)}, u32[]{:S(2)}) copy-start(f32[3,9,9]{2,0,1:T(4,128)} %param.12) | copy-start | bytes 2920
  0.6 24.0 %copy-start = (f32[2,125,125]{2,0,1:T(2,128)S(1)}, f32[2,125,125]{2,0,1:T(2,128)}, u32[]{:S(2)}) copy-start(f32[2,125,125]{2,0,1:T(2,128)} %param.13) | copy-start | bytes 375004
  2.1 26.7 %collective-permute-start = (f32[128,128]{1,0:T(8,128)S(1)}, f32[128,128]{1,0:T(8,128)S(1)}, u32[]{:S(2)}, u32[]{:S(2)}) collective-permute-start(f32[128,128]{1,0:T(8,128)S(1)} %get-tuple-element.31), channel_id=1, source_target_pairs={{0,1},{1,0},{2,3},{3,2},{4,5},{5,4},{6,7},{7,6},{8,9},{9,8},{10,11... | collective-permute-start | bytes 196616 | tf_op jit(solution)/shard_map/ppermute | solution.py:699
  22.7 6.2 %collective-permute-start.1 = (f32[128,128]{1,0:T(8,128)S(1)}, f32[128,128]{1,0:T(8,128)S(1)}, u32[]{:S(2)}, u32[]{:S(2)}) collective-permute-start(f32[128,128]{1,0:T(8,128)S(1)} %get-tuple-element.32), channel_id=1, source_target_pairs={{0,0},{1,2},{2,1},{3,4},{4,3},{5,6},{6,5},{7,8},{8,7},{9,10},{10,9... | collective-permute-start | bytes 196616 | tf_op jit(solution)/shard_map/ppermute | solution.py:698
  42.5 1.4 %collective-permute-start.2 = (f32[128,128]{1,0:T(8,128)S(1)}, f32[128,128]{1,0:T(8,128)S(1)}, u32[]{:S(2)}, u32[]{:S(2)}) collective-permute-start(f32[128,128]{1,0:T(8,128)S(1)} %get-tuple-element.49), channel_id=1, source_target_pairs={{0,1},{1,0},{2,3},{3,2},{4,5},{5,4},{6,7},{7,6},{8,9},{9,8},{10,11... | collective-permute-start | bytes 196616 | tf_op jit(solution)/shard_map/ppermute | solution.py:704

commit v9 on v8

--- a/solution.py
+++ b/solution.py
@@ -68,17 +68,17 @@
     to_refs = refs[5 + staged : 5 + 2 * staged]
     initial_ref, metric_ref, low_ref, high_ref, sems = refs[-5:]
     fields, _, elems = initial_ref.shape
-    pairs = [(initial_hbm, initial_ref), (metric_hbm, metric_ref)]
+    pairs = [(metric_hbm, metric_ref), (initial_hbm, initial_ref)]
     pairs += [(x, y if x.shape == y.shape else y.at[: x.shape[0]]) for x, y in zip(from_refs, to_refs)]
     copies = [pltpu.make_async_copy(x, y, sems.at[i]) for i, (x, y) in enumerate(pairs)]
     for copy in copies:
         copy.start()
     copies[0].wait()
+    for k in range(metric_ref.shape[0]):
+        own_ref[fields + k] = jnp.broadcast_to(metric_ref[k : k + 1, :], (LANES, elems)).T
     copies[1].wait()
     for f in range(fields):
         own_ref[f] = padded(initial_ref[f], LANES, elems).T
-    for k in range(metric_ref.shape[0]):
-        own_ref[fields + k] = jnp.broadcast_to(metric_ref[k : k + 1, :], (LANES, elems)).T
     third = iota((elems, LANES), 1) // (LANES // 3)
     factors = jnp.where(third == 0, own_ref[fields], jnp.where(third == 1, own_ref[fields + 1], own_ref[fields + 2]))
     for edge_ref, rows in ((low_ref, slice(0, STEPS)), (high_ref, slice(elems - STEPS, elems))):
@@ -128,10 +128,11 @@
     for row, (left, right) in enumerate([(l0h, l1h), (l0h, l1h), (l0l, l1l)]):
         wl_ref[row * LANES : (row + 1) * LANES, :] = jnp.concatenate([left, right], axis=1)
     rows, cols = AXES * fields * GROUP, fields * GROUP
-    spread_rows = (iota((rows, AXES * fields), 0) // GROUP == iota((rows, AXES * fields), 1)).astype(BF16)
     spread_cols = (iota((fields, cols), 0) == iota((fields, cols), 1) // GROUP).astype(BF16)
-    hi, lo = split2(jnp.concatenate([coupling_ref[k] for k in range(AXES)], axis=0))
-    full = dot(dot(spread_rows, hi).astype(BF16), spread_cols) + dot(dot(spread_rows, lo).astype(BF16), spread_cols)
+    by_row = [coupling_ref[k, g : g + 1, :] for k in range(AXES) for g in range(fields)]
+    by_row = jnp.concatenate([jnp.broadcast_to(x, (GROUP, fields)) for x in by_row], axis=0)
+    hi, lo = split2(by_row)
+    full = dot(hi, spread_cols) + dot(lo, spread_cols)
     full = jnp.where(iota((rows, cols), 0) % GROUP == iota((rows, cols), 1) % GROUP, full, 0.0)
     full_hi = full.astype(BF16).astype(F32)
     spread = padded(jnp.concatenate([full_hi, full_hi, full - full_hi], axis=1), *ck_ref.shape)
@@ -582,7 +583,7 @@
             if ring * GROUP < STEPS - t:
                 items.append(Item(t, pairs + ring, ring_rows(ring), lift_only=ring * GROUP >= STEPS - 1 - t))
         if t == EARLY:
-            samples[len(items) - 2] = EARLY - 1
+            samples[len(items) - 3] = EARLY - 1
     ready = {(0, g) for g in low_rim + high_rim}
     ready |= {(EARLY, g) for g in range(HALO + GROUP, end - GROUP, GROUP)}
     mended = {(EARLY, g) for g in low_groups + high_groups}, {(EARLY, g) for g in low_rim + high_rim}

time: 61.1 us -> 60.9 us (level)
  no operation moved by 1% of the time
where the time goes in v9:
time: 60.9 us; the launch traced here: 60.7 us
  starting transfers between devices  22.6 us (37%)
  Pallas kernels  20 us (33%)
  blocking collectives  15.9 us (26%)
  waiting for transfers between devices  1.23 us (2%)
  between operations  0.9 us (1%)
    ppermute x1, starting transfers between devices, shards(): near = lax.ppermute(near, MX, [(i, i ^ 1) for i in range(blocks)])  20.5 us
    all_to_all x1, blocking collectives, shards(): got = lax.all_to_all(rows, MX[:2], split_axis=0, concat_axis=0, tiled=True)  15.9 us
    pallas_call x1, Pallas kernels, march(): pl.pallas_call(functools.partial(march_kernel, last_block=last_block), in...  13.6 us
    pallas_call x1, Pallas kernels, early(): pl.pallas_call(early_kernel, in_specs=[vmem] * (1 + len(operators) + len(...  3.77 us
    ppermute x1, starting transfers between devices, shards(): far = lax.ppermute(far, MX, pairs)  1.94 us
    pallas_call x1, Pallas kernels, turn(): pl.pallas_call(turn_kernel, in_specs=[hbm] * (2 + len(staged)), out_shape...  1.46 us
    ppermute x1, waiting for transfers between devices, shards(): given = lax.ppermute(give, MX, [(i, i ^ 1) for i in range(blocks)])  1.23 us
  transfers between devices with their start and end apart: 3, of which 1 were waited for; matrix products, arithmetic and copies ran while one was open for 0% of the time, Pallas kernels for 7%

profile of v9, /device:TPU:513, one launch (start us, length us, event | category | flops | bytes accessed | tf_op | source)
XLA Modules:
  0.0 60.7 jit_solution(2897493426589773081)
XLA Ops:
  0.6 0.0 copy-start.1
  0.6 0.0 copy-start
  0.7 1.5 %turn.1 = (f32[12,128,128]{2,1,0:T(8,128)S(1)}, f32[128,128]{1,0:T(8,128)S(1)}, f32[128,128]{1,0:T(8,128)S(1)}, f32[3,125,125]{2,1,0:T(8,128)S(1)}, f32[125,256]...) custom-call(f32[9,125,128]{2,1,0:T(8,128)} %refs_0_.1, ...), custom_call_target="tpu_custom_call" | custom-call | tf_op jit(solution)/shard_map/turn/pallas_call | solution.py:101
  2.1 20.5 %collective-permute-start = (f32[128,128]{1,0:T(8,128)S(1)}, f32[128,128]{1,0:T(8,128)S(1)}, u32[]{:S(2)}, u32[]{:S(2)}) collective-permute-start(f32[128,128]{1,0:T(8,128)S(1)} %get-tuple-element.31), channel_id=1, source_target_pairs={{0,1},{1,0},{2,3},{3,2},{4,5},{5,4},{6,7},{7,6},{8,9},{9,8},{10,11... | collective-permute-start | bytes 196616 | tf_op jit(solution)/shard_map/ppermute | solution.py:700
  22.7 1.9 %collective-permute-start.1 = (f32[128,128]{1,0:T(8,128)S(1)}, f32[128,128]{1,0:T(8,128)S(1)}, u32[]{:S(2)}, u32[]{:S(2)}) collective-permute-start(f32[128,128]{1,0:T(8,128)S(1)} %get-tuple-element.32), channel_id=1, source_target_pairs={{0,0},{1,2},{2,1},{3,4},{4,3},{5,6},{6,5},{7,8},{8,7},{9,10},{10,9... | collective-permute-start | bytes 196616 | tf_op jit(solution)/shard_map/ppermute | solution.py:699
  24.6 0.0 copy-done.1
  24.6 0.0 copy-done
  24.7 0.3 operators.1
  24.9 3.8 %early.1 = (f32[9,128,128]{2,1,0:T(8,128)S(1)}, f32[9,128,128]{2,1,0:T(8,128)S(1)}, f32[9,128,128]{2,1,0:T(8,128)S(1)}, bf16[256,256]{1,0:T(8,128)(2,1)S(1)}, f3...) custom-call(f32[12,128,128]{2,1,0:T(8,128)S(1)} %get-tuple-element.3, ...), custom_call_target="tpu_custom_call" | custom-call | flops 5000000000 | bytes 4000000 | tf_op jit(solution)/shard_map/early/pallas_call | solution.py:433
  28.7 0.0 collective-permute-done.near_ref
  28.7 0.0 collective-permute-done.1.far_ref
  28.7 13.6 %march.1 = (f32[128,128]{1,0:T(8,128)S(1)}, f32[128,128]{1,0:T(8,128)S(1)}, f32[256,128]{1,0:T(8,128)S(1)}) custom-call(f32[12,128,128]{2,1,0:T(8,128)S(1)} %get-tuple-element.30.own_ref, f32[128,128]{1,0:T(8,128)S(1)} %collective-permute-done.near_ref, f32[128,128]{1,0:T(8,128)S(1)} %collective-permute-done.1.far_ref, ...), custom_call_target="tpu_custom_call" | custom-call | flops 20000000000 | bytes 4000000 | tf_op jit(solution)/shard_map/march/pallas_call | solution.py:603
  42.3 0.1 collective-permute-start.2
  42.5 1.2 %collective-permute-done.2.given_ref = f32[128,128]{1,0:T(8,128)S(1)} collective-permute-done((f32[128,128]{1,0:T(8,128)S(1)}, f32[128,128]{1,0:T(8,128)S(1)}, u32[]{:S(2)}, u32[]{:S(2)}) %collective-permute-start.2) | collective-permute-done | bytes 65568 | tf_op jit(solution)/shard_map/ppermute | solution.py:705
  43.7 15.9 %all_to_all.5 = f32[64,4,128]{2,1,0:T(4,128)S(1)} all-to-all(f32[64,4,128]{2,1,0:T(4,128)S(1)} %bitcast.9), channel_id=1, replica_groups=mesh['shots'=2,'mx_0'=8,'mx_1'=8,'mx_2'=2] {'mx_0','mx_1'}, dimensions={0} | all-to-all | bytes 262144 | tf_op jit(solution)/shard_map/all_to_all | solution.py:707
  59.7 0.9 %finish.1 = (f32[48,256]{1,0:T(8,128)}, f32[1,256]{1,0:T(1,128)}, f32[48,256]{1,0:T(8,128)}) custom-call(f32[256,128]{1,0:T(8,128)S(1)} %bitcast.10, f32[256,128]{1,0:T(8,128)S(1)} %get-tuple-element.50.rev_ref, bf16[256,256]{1,0:T(8,128)(2,1)S(1)} %get-tuple-element.51.to_slot_ref, bf16[256,256]{1,0:T(8,128)(2,1)S(1)} %get-tuple-element.52.to_pos_ref, ...), custom_call_target="tpu_custom_call" | custom-call | tf_op jit(solution)/shard_map/finish/pallas_call | solution.py:670
  (3 shorter events, 0.0 us)
Async XLA Ops:
  0.6 24.0 %copy-start.1 = (f32[3,9,9]{2,0,1:T(4,128)S(1)}, f32[3,9,9]{2,0,1:T(4,128)}, u32[]{:S(2)}) copy-start(f32[3,9,9]{2,0,1:T(4,128)} %param.12) | copy-start | bytes 2920
  0.6 24.0 %copy-start = (f32[2,125,125]{2,0,1:T(2,128)S(1)}, f32[2,125,125]{2,0,1:T(2,128)}, u32[]{:S(2)}) copy-start(f32[2,125,125]{2,0,1:T(2,128)} %param.13) | copy-start | bytes 375004
  2.1 26.6 %collective-permute-start = (f32[128,128]{1,0:T(8,128)S(1)}, f32[128,128]{1,0:T(8,128)S(1)}, u32[]{:S(2)}, u32[]{:S(2)}) collective-permute-start(f32[128,128]{1,0:T(8,128)S(1)} %get-tuple-element.31), channel_id=1, source_target_pairs={{0,1},{1,0},{2,3},{3,2},{4,5},{5,4},{6,7},{7,6},{8,9},{9,8},{10,11... | collective-permute-start | bytes 196616 | tf_op jit(solution)/shard_map/ppermute | solution.py:700
  22.7 6.1 %collective-permute-start.1 = (f32[128,128]{1,0:T(8,128)S(1)}, f32[128,128]{1,0:T(8,128)S(1)}, u32[]{:S(2)}, u32[]{:S(2)}) collective-permute-start(f32[128,128]{1,0:T(8,128)S(1)} %get-tuple-element.32), channel_id=1, source_target_pairs={{0,0},{1,2},{2,1},{3,4},{4,3},{5,6},{6,5},{7,8},{8,7},{9,10},{10,9... | collective-permute-start | bytes 196616 | tf_op jit(solution)/shard_map/ppermute | solution.py:699
  42.3 1.4 %collective-permute-start.2 = (f32[128,128]{1,0:T(8,128)S(1)}, f32[128,128]{1,0:T(8,128)S(1)}, u32[]{:S(2)}, u32[]{:S(2)}) collective-permute-start(f32[128,128]{1,0:T(8,128)S(1)} %get-tuple-element.49), channel_id=1, source_target_pairs={{0,1},{1,0},{2,3},{3,2},{4,5},{5,4},{6,7},{7,6},{8,9},{9,8},{10,11... | collective-permute-start | bytes 196616 | tf_op jit(solution)/shard_map/ppermute | solution.py:705
